TPU v7x, 128 devices: a whole 4x4x4 slice. The times are simulated.
128 devices in a mesh: node: 16 (over z, y), local: 8 (over x, core).
Axes of the slice: x: 4, y: 4, z: 4, core: 2. Of those that a mesh axis runs over, the one named last changes fastest.
Arguments:
- x: bfloat16 [128, 384, 1024], P(('node', 'local'))
- y_cot: bfloat16 [128, 384, 1024], P(('node', 'local'))
- ln1_gain: bfloat16 [2, 1024], P(None, ('node', 'local'))
- ln1_bias: bfloat16 [2, 1024], P(None, ('node', 'local'))
- qkv_weight: bfloat16 [2, 1024, 16, 192], P(None, ('node', 'local'))
- qkv_bias: bfloat16 [2, 3072], P(None, ('node', 'local'))
- out_weight: bfloat16 [2, 1024, 1024], P(None, ('node', 'local'))
- out_bias: bfloat16 [2, 1024], P(None, ('node', 'local'))
- ln2_gain: bfloat16 [2, 1024], P(None, ('node', 'local'))
- ln2_bias: bfloat16 [2, 1024], P(None, ('node', 'local'))
- up_weight: bfloat16 [2, 1024, 4096], P(None, ('node', 'local'))
- up_bias: bfloat16 [2, 4096], P(None, ('node', 'local'))
- down_weight: bfloat16 [2, 4096, 1024], P(None, ('node', 'local'))
- down_bias: bfloat16 [2, 1024], P(None, ('node', 'local'))
Outputs:
- output 1: bfloat16 [128, 384, 1024], P(('node', 'local'))
- output 2: bfloat16 [128, 384, 1024], P(('node', 'local'))
- output 3: bfloat16 [2, 1024], P(None, ('node', 'local'))
- output 4: bfloat16 [2, 1024], P(None, ('node', 'local'))
- output 5: bfloat16 [2, 1024, 16, 192], P(None, ('node', 'local'))
- output 6: bfloat16 [2, 3072], P(None, ('node', 'local'))
- output 7: bfloat16 [2, 1024, 1024], P(None, ('node', 'local'))
- output 8: bfloat16 [2, 1024], P(None, ('node', 'local'))
- output 9: bfloat16 [2, 1024], P(None, ('node', 'local'))
- output 10: bfloat16 [2, 1024], P(None, ('node', 'local'))
- output 11: bfloat16 [2, 1024, 4096], P(None, ('node', 'local'))
- output 12: bfloat16 [2, 4096], P(None, ('node', 'local'))
- output 13: bfloat16 [2, 4096, 1024], P(None, ('node', 'local'))
- output 14: bfloat16 [2, 1024], P(None, ('node', 'local'))
All inputs are finite; a program needn't handle non-finite values.
Results may differ from a plain program's by a relative error of at most 0.018346.
Values are sent between devices in bfloat16 or wider.
A program may use at most 1 GiB of HBM per device.

v0:
```python
import functools
import jax
import jax.numpy as jnp
from jax import lax
from jax.sharding import PartitionSpec as P, NamedSharding

EPSILON = 1e-5


def product(einsum_form, first_op, second_op):
    return jnp.einsum(einsum_form, first_op, second_op, preferred_element_type=jnp.float32)


def rope_tables(seq_len, rot_dim):
    inv_freq = 1.0 / (10000.0 ** (jnp.arange(0, rot_dim, 2, dtype=jnp.float32) / rot_dim))
    angles = jnp.arange(seq_len, dtype=jnp.float32)[:, None] * inv_freq[None, :]
    angles = jnp.concatenate([angles, angles], axis=-1)
    return jnp.cos(angles), jnp.sin(angles)


def norm_pair(hidden32, gain_attn, bias_attn, gain_mlp, bias_mlp):
    center = hidden32 - jnp.mean(hidden32, axis=-1, keepdims=True)
    scaled = center * lax.rsqrt(jnp.mean(center * center, axis=-1, keepdims=True) + EPSILON)
    return ((scaled * gain_attn + bias_attn).astype(jnp.bfloat16),
            (scaled * gain_mlp + bias_mlp).astype(jnp.bfloat16))


def rotary_split(qkv_all, cos_tab, sin_tab):
    head_dim = qkv_all.shape[-1] // 3
    rot_dim = head_dim // 4
    half_dim = rot_dim // 2
    cos_b = cos_tab[:, None, :]
    sin_b = sin_tab[:, None, :]

    def rotate_vec(vectors):
        rot_part = vectors[..., :rot_dim]
        turned = jnp.concatenate([-rot_part[..., half_dim:], rot_part[..., :half_dim]], axis=-1)
        return jnp.concatenate([rot_part * cos_b + turned * sin_b, vectors[..., rot_dim:]], axis=-1)

    query_rot = rotate_vec(qkv_all[..., :head_dim]).astype(jnp.bfloat16)
    key_rot = rotate_vec(qkv_all[..., head_dim:2 * head_dim]).astype(jnp.bfloat16)
    return query_rot, key_rot, qkv_all[..., 2 * head_dim:].astype(jnp.bfloat16)


def gelu_bf16(pre_act):
    return jax.nn.gelu(pre_act, approximate=False).astype(jnp.bfloat16)


def layer_forward(hidden, weights, cos_tab, sin_tab):
    (ln1_gain, ln1_bias, qkv_weight, qkv_bias, out_weight, out_bias,
     ln2_gain, ln2_bias, up_weight, up_bias, down_weight, down_bias) = weights
    num_heads = qkv_weight.shape[1]
    head_dim = qkv_weight.shape[2] // 3
    d_model = hidden.shape[-1]
    seq_len = hidden.shape[1]
    hidden32 = hidden.astype(jnp.float32)
    (normed_attn, normed_mlp), norm_pull = jax.vjp(
        norm_pair, hidden32, ln1_gain.astype(jnp.float32), ln1_bias.astype(jnp.float32),
        ln2_gain.astype(jnp.float32), ln2_bias.astype(jnp.float32))
    qkv_all = product('bsd,dhe->bshe', normed_attn, qkv_weight) + qkv_bias.astype(jnp.float32).reshape(num_heads, 3 * head_dim)
    (query_rot, key_rot, values), rotary_pull = jax.vjp(
        functools.partial(rotary_split, cos_tab=cos_tab, sin_tab=sin_tab), qkv_all)
    scores = product('bqhd,bkhd->bhqk', query_rot, key_rot) * head_dim ** -0.5
    causal = lax.broadcasted_iota(jnp.int32, (seq_len, seq_len), 0) >= lax.broadcasted_iota(jnp.int32, (seq_len, seq_len), 1)
    attn_probs = jax.nn.softmax(jnp.where(causal, scores, -1e30), axis=-1)
    probs_bf = attn_probs.astype(jnp.bfloat16)
    context = product('bhqk,bkhd->bqhd', probs_bf, values).astype(jnp.bfloat16)
    out_heads = out_weight.reshape(num_heads, head_dim, d_model)
    attn_out = product('bqhd,hde->bqe', context, out_heads) + out_bias.astype(jnp.float32)
    pre_act = product('bsd,df->bsf', normed_mlp, up_weight) + up_bias.astype(jnp.float32)
    mlp_act, gelu_pull = jax.vjp(gelu_bf16, pre_act)
    mlp_out = product('bsf,fd->bsd', mlp_act, down_weight) + down_bias.astype(jnp.float32)
    layer_out = (hidden32 + attn_out + mlp_out).astype(jnp.bfloat16)
    saved_state = (norm_pull, normed_attn, normed_mlp, rotary_pull, query_rot, key_rot, values,
                   attn_probs, probs_bf, context, gelu_pull, mlp_act)
    return layer_out, saved_state


def layer_backward(d_out, weights, saved_state):
    (ln1_gain, ln1_bias, qkv_weight, qkv_bias, out_weight, out_bias,
     ln2_gain, ln2_bias, up_weight, up_bias, down_weight, down_bias) = weights
    (norm_pull, normed_attn, normed_mlp, rotary_pull, query_rot, key_rot, values,
     attn_probs, probs_bf, context, gelu_pull, mlp_act) = saved_state
    num_heads = qkv_weight.shape[1]
    head_dim = qkv_weight.shape[2] // 3
    d_model = d_out.shape[-1]
    d_out32 = d_out.astype(jnp.float32)
    out_sum_grad = jnp.sum(d_out32, axis=(0, 1))
    down_grad = product('bsf,bsd->fd', mlp_act, d_out)
    d_act = product('bsd,fd->bsf', d_out, down_weight).astype(jnp.bfloat16)
    (d_pre,) = gelu_pull(d_act)
    up_bias_grad = jnp.sum(d_pre, axis=(0, 1))
    d_pre_bf = d_pre.astype(jnp.bfloat16)
    up_grad = product('bsd,bsf->df', normed_mlp, d_pre_bf)
    d_normed_mlp = product('bsf,df->bsd', d_pre_bf, up_weight).astype(jnp.bfloat16)
    out_heads = out_weight.reshape(num_heads, head_dim, d_model)
    out_grad = product('bqhd,bqe->hde', context, d_out).reshape(d_model, d_model)
    d_context = product('bqe,hde->bqhd', d_out, out_heads).astype(jnp.bfloat16)
    d_probs = product('bqhd,bkhd->bhqk', d_context, values).astype(jnp.bfloat16).astype(jnp.float32)
    d_values = product('bhqk,bqhd->bkhd', probs_bf, d_context).astype(jnp.bfloat16)
    d_scores = (attn_probs * (d_probs - jnp.sum(d_probs * attn_probs, axis=-1, keepdims=True)) * head_dim ** -0.5).astype(jnp.bfloat16)
    d_query = product('bhqk,bkhd->bqhd', d_scores, key_rot).astype(jnp.bfloat16)
    d_key = product('bhqk,bqhd->bkhd', d_scores, query_rot).astype(jnp.bfloat16)
    (d_qkv,) = rotary_pull((d_query, d_key, d_values))
    qkv_bias_grad = jnp.sum(d_qkv, axis=(0, 1)).reshape(-1)
    d_qkv_bf = d_qkv.astype(jnp.bfloat16)
    qkv_grad = product('bsd,bshe->dhe', normed_attn, d_qkv_bf)
    d_normed_attn = product('bshe,dhe->bsd', d_qkv_bf, qkv_weight).astype(jnp.bfloat16)
    d_hidden32, gain1_grad, bias1_grad, gain2_grad, bias2_grad = norm_pull((d_normed_attn, d_normed_mlp))
    d_hidden = (d_out32 + d_hidden32).astype(jnp.bfloat16)
    grad_list = (gain1_grad, bias1_grad, qkv_grad, qkv_bias_grad, out_grad, out_sum_grad,
                 gain2_grad, bias2_grad, up_grad, up_bias_grad, down_grad, out_sum_grad)
    return d_hidden, grad_list


def solution(mesh):
    shard_axes = ('node', 'local')
    act_spec = P(shard_axes)
    param_spec = P(None, shard_axes)

    def gather_layer(shards, layer_idx):
        return [lax.all_gather(tensor[layer_idx], shard_axes, axis=0, tiled=True) for tensor in shards]

    def scatter_grads(grad_list):
        return [lax.psum_scatter(grad_arr, shard_axes, scatter_dimension=0, tiled=True).astype(jnp.bfloat16)
                for grad_arr in grad_list]

    def device_step(x, y_cot, *shards):
        num_layers = shards[0].shape[0]
        cos_tab, sin_tab = rope_tables(x.shape[1], shards[2].shape[3] // 12)
        layer_inputs = []
        hidden = x
        for layer_idx in range(num_layers):
            layer_inputs.append(hidden)
            hidden, _ = layer_forward(hidden, gather_layer(shards, layer_idx), cos_tab, sin_tab)
        y_out = hidden
        d_hidden = y_cot
        layer_grads = [None] * num_layers
        for layer_idx in reversed(range(num_layers)):
            _, saved_state = layer_forward(layer_inputs[layer_idx], gather_layer(shards, layer_idx), cos_tab, sin_tab)
            d_hidden, grad_list = layer_backward(d_hidden, gather_layer(shards, layer_idx), saved_state)
            layer_grads[layer_idx] = scatter_grads(grad_list)
        stacked = tuple(jnp.stack([layer_grads[i][j] for i in range(num_layers)]) for j in range(len(shards)))
        return (y_out, d_hidden) + stacked

    return jax.shard_map(device_step, mesh=mesh,
                         in_specs=(act_spec, act_spec) + (param_spec,) * 12,
                         out_specs=(act_spec, act_spec) + (param_spec,) * 12,
                         check_vma=False)
```

profile of v0, /device:TPU:1, one launch (start us, length us, event | category | flops | bytes accessed | tf_op | source)
XLA Modules:
  0.0 5876.7 jit_solution(11559004105105712946)
XLA Ops:
  29.0 70.9 %all-reduce.53 = (bf16[3072]{0:T(1024)(128)(2,1)S(1)}, bf16[3072]{0:T(1024)(128)(2,1)S(1)}, bf16[4096]{0:T(1024)(128)(2,1)S(1)}, bf16[1024]{0:T(1024)(128)(2,1)S...) all-reduce(bf16[3072]{0:T(1024)(128)(2,1)S(1)} %dynamic-update-slic, ...), channel_id=5, replica_groups=mesh['node'=16,'local'=8] {'node','local'}, use_global_device_ids=true, to_apply=%add.24 | all-reduce | flops 26624 | bytes 106496
  109.5 41.2 all-gather.33.cloned.1.call-done
  150.7 11.8 copy.42
  171.3 50.2 all-gather.41.cloned.1.call-done
  221.5 11.9 copy.45
  251.8 40.3 all-gather.37.cloned.1.call-done
  292.2 21.1 multiply_convert_fusion.1
  313.3 49.5 all-gather.39.cloned.1.call-done
  362.7 8.9 fusion.20
  371.7 57.0 all-gather.35.cloned.1.call-done
  453.4 13.9 convert_bitcast_fusion.6
  467.3 14.2 convert_bitcast_fusion.7
  509.8 20.6 multiply_convert_fusion
  530.3 39.7 all-gather.47.cloned.1.call-done
  570.0 14.0 fusion.304
  592.8 10.6 fusion.190
  611.7 14.5 convert_bitcast_fusion.4
  626.1 14.5 convert_bitcast_fusion.5
  650.9 8.7 fusion.192
  659.7 10.1 fusion.199
  669.9 10.2 fusion.141
  680.2 12.8 fusion.305
  703.1 10.5 fusion.205
  734.6 65.7 %all-reduce.52 = (bf16[1024]{0:T(1024)(128)(2,1)S(1)}, bf16[1024]{0:T(1024)(128)(2,1)S(1)}, bf16[1024]{0:T(1024)(128)(2,1)S(1)}, bf16[1024]{0:T(1024)(128)(2,1)S...) all-reduce(f32[1024]{0:T(1024)S(1)} %get-tuple-element.47, ...), channel_id=27, replica_groups=mesh['node'=16,'local'=8] {'node','local'}, use_global_device_ids=true, to_apply=%region_17.18.clone | all-reduce | flops 24576 | bytes 147456
  815.5 397.1 %reduce-scatter.15.cloned.1.call-done = f32[8,1024]{1,0:T(8,128)} async-done(((f32[1024,1024]{1,0:T(8,128)}), f32[8,1024]{1,0:T(8,128)}) %reduce-scatter.15.cloned.1.call-update) | async-done | bytes 32784 | tf_op jit(solution)/shard_map/reduce_scatter | solution.py:125
  1213.4 645.6 %reduce-scatter.13.cloned.1.call-done = f32[8,1024]{1,0:T(8,128)} async-done(((f32[1024,1024]{1,0:T(8,128)}), f32[8,1024]{1,0:T(8,128)}) %reduce-scatter.13.cloned.1.call-update) | async-done | bytes 32784 | tf_op jit(solution)/shard_map/reduce_scatter | solution.py:125
  1860.4 666.8 %reduce-scatter.11.cloned.1.call-done = f32[8,16,192]{2,0,1:T(8,128)} async-done(((f32[1024,16,192]{2,0,1:T(8,128)}), f32[8,16,192]{2,0,1:T(8,128)}) %reduce-scatter.11.cloned.1.call-update) | async-done | bytes 98320 | tf_op jit(solution)/shard_map/reduce_scatter | solution.py:125
  2528.0 667.2 %reduce-scatter.9.cloned.1.call-done = f32[8,16,192]{2,0,1:T(8,128)} async-done(((f32[1024,16,192]{2,0,1:T(8,128)}), f32[8,16,192]{2,0,1:T(8,128)}) %reduce-scatter.9.cloned.1.call-update) | async-done | bytes 98320 | tf_op jit(solution)/shard_map/reduce_scatter | solution.py:125
  3196.9 666.6 %reduce-scatter.21.cloned.1.call-done = f32[32,1024]{1,0:T(8,128)} async-done(((f32[4096,1024]{1,0:T(8,128)}), f32[32,1024]{1,0:T(8,128)}) %reduce-scatter.21.cloned.1.call-update) | async-done | bytes 131088 | tf_op jit(solution)/shard_map/reduce_scatter | solution.py:125
  3864.4 667.2 %reduce-scatter.19.cloned.1.call-done = f32[8,4096]{1,0:T(8,128)} async-done(((f32[1024,4096]{1,0:T(8,128)}), f32[8,4096]{1,0:T(8,128)}) %reduce-scatter.19.cloned.1.call-update) | async-done | bytes 131088 | tf_op jit(solution)/shard_map/reduce_scatter | solution.py:125
  4532.5 667.2 %reduce-scatter.17.cloned.1.call-done = f32[8,4096]{1,0:T(8,128)} async-done(((f32[1024,4096]{1,0:T(8,128)}), f32[8,4096]{1,0:T(8,128)}) %reduce-scatter.17.cloned.1.call-update) | async-done | bytes 131088 | tf_op jit(solution)/shard_map/reduce_scatter | solution.py:125
  5201.3 666.5 %reduce-scatter.23.cloned.1.call-done = f32[32,1024]{1,0:T(8,128)} async-done(((f32[4096,1024]{1,0:T(8,128)}), f32[32,1024]{1,0:T(8,128)}) %reduce-scatter.23.cloned.1.call-update) | async-done | bytes 131088 | tf_op jit(solution)/shard_map/reduce_scatter | solution.py:125
  (333 shorter events, 194.7 us)
Async XLA Ops:
  7.2 98.3 %all-gather.43.cloned.1.call-start = ((), (), s32[]{:S(2)}) async-start(), calls=%async_computation.21 | async-start | bytes 2113536 | tf_op jit(solution)/shard_map/all_gather | solution.py:122
  8.6 142.2 %all-gather.33.cloned.1.call-start = ((), (), s32[]{:S(2)}) async-start(), calls=%async_computation.16 | async-start | bytes 8454144 | tf_op jit(solution)/shard_map/all_gather | solution.py:122
  10.2 211.3 %all-gather.41.cloned.1.call-start = ((), (), s32[]{:S(2)}) async-start(), calls=%async_computation.20 | async-start | bytes 8454144 | tf_op jit(solution)/shard_map/all_gather | solution.py:122
  10.9 281.2 %all-gather.37.cloned.1.call-start = ((), (), s32[]{:S(2)}) async-start(), calls=%async_computation.18 | async-start | bytes 8454144 | tf_op jit(solution)/shard_map/all_gather | solution.py:122
  12.5 350.2 %all-gather.39.cloned.1.call-start = ((), (), s32[]{:S(2)}) async-start(), calls=%async_computation.19 | async-start | bytes 8454144 | tf_op jit(solution)/shard_map/all_gather | solution.py:122
  14.1 414.6 %all-gather.35.cloned.1.call-start = ((), (), s32[]{:S(2)}) async-start(), calls=%async_computation.17 | async-start | bytes 2113536 | tf_op jit(solution)/shard_map/all_gather | solution.py:122
  14.7 495.0 %all-gather.45.cloned.1.call-start = ((), (), s32[]{:S(2)}) async-start(), calls=%async_computation.22 | async-start | bytes 8454144 | tf_op jit(solution)/shard_map/all_gather | solution.py:122
  15.5 554.6 %all-gather.47.cloned.1.call-start = ((), (), s32[]{:S(2)}) async-start(), calls=%async_computation.23 | async-start | bytes 8454144 | tf_op jit(solution)/shard_map/all_gather | solution.py:122
  16.2 1196.4 %reduce-scatter.15.cloned.1.call-start = ((), (), s32[]{:S(2)}) async-start(), calls=%async_computation.11 | async-start | bytes 4227072 | tf_op jit(solution)/shard_map/reduce_scatter | solution.py:125
  23.5 268.6 %copy-start.37 = (f32[384]{0:T(512)}, f32[384]{0:T(512)S(1)}, u32[]{:S(2)}) copy-start(f32[384]{0:T(512)S(1)} %broadcast_multiply_fusion.1) | copy-start | bytes 4612
  25.6 266.6 %copy-start.39 = (f32[384]{0:T(512)}, f32[384]{0:T(512)S(1)}, u32[]{:S(2)}) copy-start(f32[384]{0:T(512)S(1)} %fusion.232) | copy-start | bytes 4612
  99.8 192.3 %copy-start.29 = (f32[1024]{0:T(1024)}, f32[1024]{0:T(1024)S(1)}, u32[]{:S(2)}) copy-start(f32[1024]{0:T(1024)S(1)} %convert_element_type.549) | copy-start | bytes 12292
  99.8 62.7 %copy-start.47 = (f32[1024]{0:T(1024)}, f32[1024]{0:T(1024)S(1)}, u32[]{:S(2)}) copy-start(f32[1024]{0:T(1024)S(1)} %convert_element_type.546) | copy-start | bytes 12292
  101.0 191.1 %copy-start.32 = (f32[1024]{0:T(1024)}, f32[1024]{0:T(1024)S(1)}, u32[]{:S(2)}) copy-start(f32[1024]{0:T(1024)S(1)} %convert_element_type.550) | copy-start | bytes 12292
  101.0 61.5 %copy-start.52 = (f32[1024]{0:T(1024)}, f32[1024]{0:T(1024)S(1)}, u32[]{:S(2)}) copy-start(f32[1024]{0:T(1024)S(1)} %convert_element_type.547) | copy-start | bytes 12292
  109.5 53.0 copy-start
  171.3 75.1 %copy-start.2 = (bf16[1,384,16,192]{1,3,2,0:T(8,128)(2,1)}, bf16[1,384,16,192]{1,3,2,0:T(8,128)(2,1)S(1)}, u32[]{:S(2)}) copy-start(bf16[1,384,16,192]{1,3,2,0:T(8,128)(2,1)S(1)} %get-tuple-element.88) | copy-start | bytes 7077892
  246.4 45.7 copy-start.45
  362.7 66.0 %copy-start.20 = (bf16[16,64,384]{2,1,0:T(8,128)(2,1)S(1)}, bf16[16,64,384]{2,1,0:T(8,128)(2,1)}, u32[]{:S(2)}) copy-start(bf16[16,64,384]{2,1,0:T(8,128)(2,1)} %fusion.148) | copy-start | bytes 2359300
  362.7 66.0 %copy-start.56 = (f32[1024]{0:T(1024)S(1)}, f32[1024]{0:T(1024)}, u32[]{:S(2)}) copy-start(f32[1024]{0:T(1024)} %convert_element_type.552) | copy-start | bytes 12292
  362.7 66.0 %copy-start.57 = (f32[1024]{0:T(1024)S(1)}, f32[1024]{0:T(1024)}, u32[]{:S(2)}) copy-start(f32[1024]{0:T(1024)} %convert_element_type.548) | copy-start | bytes 12292
  502.0 1356.9 %reduce-scatter.13.cloned.1.call-start = ((), (), s32[]{:S(2)}) async-start(), calls=%async_computation.10 | async-start | bytes 4227072 | tf_op jit(solution)/shard_map/reduce_scatter | solution.py:125
  509.7 60.3 %copy-start.4 = (bf16[1,384,1024]{2,1,0:T(8,128)(2,1)S(1)}, bf16[1,384,1024]{2,1,0:T(8,128)(2,1)}, u32[]{:S(2)}) copy-start(bf16[1,384,1024]{2,1,0:T(8,128)(2,1)} %param.15) | copy-start | bytes 2359300
  592.7 1934.4 %reduce-scatter.11.cloned.1.call-start = ((), (), s32[]{:S(2)}) async-start(), calls=%async_computation.9 | async-start | bytes 16908288 | tf_op jit(solution)/shard_map/reduce_scatter | solution.py:125
  603.4 2591.9 %reduce-scatter.9.cloned.1.call-start = ((), (), s32[]{:S(2)}) async-start(), calls=%async_computation.8 | async-start | bytes 16908288 | tf_op jit(solution)/shard_map/reduce_scatter | solution.py:125
  606.5 19.7 copy-start.24
  659.7 3203.8 %reduce-scatter.21.cloned.1.call-start = ((), (), s32[]{:S(2)}) async-start(), calls=%async_computation.14 | async-start | bytes 16908288 | tf_op jit(solution)/shard_map/reduce_scatter | solution.py:125
  669.9 3861.8 %reduce-scatter.19.cloned.1.call-start = ((), (), s32[]{:S(2)}) async-start(), calls=%async_computation.13 | async-start | bytes 16908288 | tf_op jit(solution)/shard_map/reduce_scatter | solution.py:125
  680.1 4519.6 %reduce-scatter.17.cloned.1.call-start = ((), (), s32[]{:S(2)}) async-start(), calls=%async_computation.12 | async-start | bytes 16908288 | tf_op jit(solution)/shard_map/reduce_scatter | solution.py:125
  703.0 5164.9 %reduce-scatter.23.cloned.1.call-start = ((), (), s32[]{:S(2)}) async-start(), calls=%async_computation.15 | async-start | bytes 16908288 | tf_op jit(solution)/shard_map/reduce_scatter | solution.py:125
  726.8 77.7 %copy-start.43 = (f32[384]{0:T(512)S(1)}, f32[384]{0:T(512)}, u32[]{:S(2)}) copy-start(f32[384]{0:T(512)} %copy-done.42) | copy-start | bytes 4612
  800.5 5069.0 %copy-start.62 = (bf16[2,8]{1,0:T(2,128)(2,1)}, bf16[2,8]{1,0:T(2,128)(2,1)S(1)}, u32[]{:S(2)}) copy-start(bf16[2,8]{1,0:T(2,128)(2,1)S(1)} %pad_maximum_fusion.36) | copy-start | bytes 100
  (53 other events, 311.8 us)
Sparse Core Ops, SparseCore 0:
  11.7 68.9 all-gather.42
  83.7 67.0 all-gather.32
  154.3 67.1 all-gather.40
  224.9 67.1 all-gather.36
  295.5 67.1 all-gather.38
  365.7 62.9 all-gather.34
  432.3 66.9 all-gather.44
  502.8 67.1 all-gather.46
  572.4 640.2 reduce-scatter.14
  1214.8 644.0 reduce-scatter.12
  1861.4 665.6 reduce-scatter.10
  2529.4 665.8 reduce-scatter.8
  3197.6 665.8 reduce-scatter.20
  3865.7 665.8 reduce-scatter.18
  4533.9 665.8 reduce-scatter.16
  5202.0 665.8 reduce-scatter.22
where the time goes:
time: 5890 us; the launch traced here: 5880 us
  waiting for transfers between devices  5320 us (90%)
  matrix products  304 us (5%)
  blocking collectives  137 us (2%)
    reduce_scatter x8, waiting for transfers between devices, scatter_grads(): lax.psum_scatter(grad_arr, shard_axes, scatter_dimension=0, tiled=True)  5040 us
    all_gather x8, waiting for transfers between devices, gather_layer(): lax.all_gather(tensor[layer_idx], shard_axes, axis=0, tiled=True)  278 us
    dot_general x32, matrix products, product(): jnp.einsum(einsum_form, first_op, second_op, preferred_element_type=jnp.f...  275 us
    unnamed x2, blocking collectives  137 us
  transfers between devices with their start and end apart: 16, of which 14 were waited for; matrix products, arithmetic and copies ran while one was open for 7% of the time, Pallas kernels for 0%

commit v1 on v0

v1 whole, which is shorter than its diff:
```python
import functools
import jax
import jax.numpy as jnp
from jax import lax
from jax.experimental import pallas as pl
from jax.experimental.pallas import tpu as pltpu
from jax.sharding import PartitionSpec as P

EPSILON = 1e-5
MESH = pl.DeviceIdType.MESH
ANY = pl.BlockSpec(memory_space=pl.ANY)
IN_VMEM = pl.BlockSpec(memory_space=pltpu.VMEM)
ORDERS = ((2, 1, 0), (1, 0, 2), (0, 2, 1))
VMEM_LIMIT = 60 * 2**20


def flip(index, mask):
    if mask == 1:
        return index + 1 - 2 * lax.rem(index, 2)
    if mask == 3:
        return 3 - index
    return lax.rem(index + 2, 4)


def place():
    node = lax.axis_index('node')
    local = lax.axis_index('local')
    return (node // 4, lax.rem(node, 4), local // 2), lax.rem(local, 2)


def device_at(chip, core):
    return (chip[0] * 4 + chip[1], chip[2] * 2 + core)


def moved(chip, axis, mask):
    return tuple(flip(v, mask) if k == axis else v for k, v in enumerate(chip))


def colour_plan(colour):
    return ORDERS[colour // 2], ((1, 3) if colour % 2 == 0 else (3, 1))


def entry_barrier(chip, core):
    barrier = pltpu.get_barrier_semaphore()
    for axis in range(3):
        for mask in (1, 3):
            pl.semaphore_signal(barrier, inc=1, device_id=device_at(moved(chip, axis, mask), core), device_id_type=MESH)
    pl.semaphore_signal(barrier, inc=1, device_id=device_at(chip, 1 - core), device_id_type=MESH)
    pl.semaphore_wait(barrier, 7)


GATHER_PARTS = ((0, 0, 2048, 0), (0, 2048, 2048, 1), (1, 0, 512, 2), (1, 512, 512, 3),
                (2, 0, 2048, 4), (2, 2048, 1024, 5), (3, 0, 1024, 5))


def gather_kernel(n_layers, *refs):
    shards, refs = refs[:5], refs[5:]
    fulls, refs = refs[:4 * n_layers + 1], refs[4 * n_layers + 1:]
    send_sem, recv_sem, pass_send, pass_recv, own_sem = refs
    chip, core = place()
    entry_barrier(chip, core)
    every = pl.ds(0, 4)
    copies = []

    parts = []
    for layer in range(n_layers):
        for arr, col, width, colour in GATHER_PARTS:
            parts.append((fulls[4 * layer + arr], shards[arr].at[layer, :, pl.ds(col, width)], col, width, colour))
    parts.append((fulls[-1], shards[4], 0, 128, 4))

    def box(part, where):
        full, _, col, width, _ = part
        return full.at[where[0], where[1], where[2], core, :, pl.ds(col, width)]

    def reach(n, slot, where, target, own):
        part = parts[n]
        copy = pltpu.make_async_remote_copy(
            src_ref=part[1] if own else box(part, where), dst_ref=box(part, where),
            send_sem=send_sem.at[n, slot], recv_sem=recv_sem.at[n, slot],
            device_id=device_at(target, core), device_id_type=MESH)
        copy.start()
        copies.append(copy)
        return copy

    def pass_on(n, slot, where, own):
        part = parts[n]
        copy = pltpu.make_async_remote_copy(
            src_ref=part[1] if own else box(part, where), dst_ref=box(part, where),
            send_sem=pass_send.at[n, slot], recv_sem=pass_recv.at[n, slot],
            device_id=device_at(chip, 1 - core), device_id_type=MESH)
        copy.start()
        copies.append(copy)
        return copy

    def span(order, stage, value):
        where = list(chip)
        for axis in order[:stage]:
            where[axis] = every
        where[order[stage]] = value
        return where

    own = []
    for layer in range(n_layers):
        for arr in range(4):
            own.append(pltpu.make_async_copy(
                shards[arr].at[layer], fulls[4 * layer + arr].at[chip[0], chip[1], chip[2], core], own_sem.at[4 * layer + arr]))
    own.append(pltpu.make_async_copy(shards[4], fulls[-1].at[chip[0], chip[1], chip[2], core], own_sem.at[4 * n_layers]))
    for copy in own:
        copy.start()

    passed = []
    first = {}
    for stage in range(3):
        for turn in range(2):
            for n, part in enumerate(parts):
                order, masks = colour_plan(part[4])
                axis = order[stage]
                target = moved(chip, axis, masks[turn])
                first[n, turn] = reach(n, 3 * stage + turn, span(order, stage, chip[axis]), target, stage == 0)
        if stage == 0:
            for n, part in enumerate(parts):
                passed.append(pass_on(n, 9, list(chip), True))
            for copy in own:
                copy.wait()
        second = {}
        for n, part in enumerate(parts):
            order, masks = colour_plan(part[4])
            axis = order[stage]
            first[n, 0].wait_recv()
            where = span(order, stage, flip(chip[axis], masks[0]))
            second[n] = reach(n, 3 * stage + 2, where, moved(chip, axis, masks[1]), False)
            passed.append(pass_on(n, 3 * stage, where, False))
        for n, part in enumerate(parts):
            order, masks = colour_plan(part[4])
            axis = order[stage]
            first[n, 1].wait_recv()
            passed.append(pass_on(n, 3 * stage + 1, span(order, stage, flip(chip[axis], masks[1])), False))
            second[n].wait_recv()
            passed.append(pass_on(n, 3 * stage + 2, span(order, stage, flip(chip[axis], 2)), False))
    for copy in passed:
        copy.wait_recv()
    for copy in copies:
        copy.wait_send()


def gather_all(up, down, qkv, out, small):
    n_layers = up.shape[0]
    shards = (up, down, qkv, out, small)
    n_parts = len(GATHER_PARTS) * n_layers + 1
    shapes = [jax.ShapeDtypeStruct((4, 4, 4, 2) + tensor.shape[1:], tensor.dtype) for _ in range(n_layers) for tensor in shards[:4]]
    shapes.append(jax.ShapeDtypeStruct((4, 4, 4, 2) + small.shape, small.dtype))
    fulls = pl.pallas_call(
        functools.partial(gather_kernel, n_layers),
        out_shape=shapes,
        in_specs=[IN_VMEM] * 5,
        out_specs=[ANY] * len(shapes),
        scratch_shapes=[pltpu.SemaphoreType.DMA((n_parts, 9)), pltpu.SemaphoreType.DMA((n_parts, 9)),
                        pltpu.SemaphoreType.DMA((n_parts, 10)), pltpu.SemaphoreType.DMA((n_parts, 10)),
                        pltpu.SemaphoreType.DMA((4 * n_layers + 1,))],
        compiler_params=pltpu.CompilerParams(collective_id=0, has_side_effects=True),
        name='gather_weights',
    )(*shards)
    layers = []
    for layer in range(n_layers):
        layers.append([full.reshape((-1, full.shape[-1])) for full in fulls[4 * layer:4 * layer + 4]])
    return layers, fulls[-1].reshape((128,) + small.shape)


REDUCE_PARTS = ((0, 0, 1024, 0), (0, 1024, 1024, 1), (1, 0, 256, 2), (1, 256, 256, 3),
                (2, 0, 1024, 4), (2, 1024, 512, 5), (3, 0, 512, 5), (4, 0, 128, 4))


def reduce_kernel(*refs):
    grads, sums, refs = refs[:5], refs[5:10], refs[10:]
    n_parts = len(REDUCE_PARTS)
    kept, refs = refs[:n_parts], refs[n_parts:]
    came, refs = [refs[6 * n:6 * n + 6] for n in range(n_parts)], refs[6 * n_parts:]
    send_sem, recv_sem, load_sem, tile = refs
    chip, core = place()
    entry_barrier(chip, core)
    copies = []
    started = {}

    def reach(n, slot, src, dst, target, to_core=core):
        copy = pltpu.make_async_remote_copy(
            src_ref=src, dst_ref=dst, send_sem=send_sem.at[n, slot], recv_sem=recv_sem.at[n, slot],
            device_id=device_at(target, to_core), device_id_type=MESH)
        copy.start()
        copies.append(copy)
        started[n, slot] = copy

    def at_axis(ref, axis, value, n_axes, lead=()):
        every = [pl.ds(0, 4)] * n_axes
        every[axis] = value
        return ref.at[tuple(lead) + tuple(every)]

    def add_into(dst, src, n_axes):
        if n_axes == 0:
            dst[...] += src[...]
            return
        rows, cols = dst.shape[-2:]

        @pl.loop(0, 4 ** n_axes)
        def _(k):
            index = (k,) if n_axes == 1 else (k // 4, lax.rem(k, 4))
            dst[index] += src[index]

    plans = [colour_plan(part[3]) for part in REDUCE_PARTS]

    loads = {}
    for slot in (1, 0):
        for n, (arr, col, width, colour) in enumerate(REDUCE_PARTS):
            order, (one, two) = plans[n]
            axis = order[0]
            mine = chip[axis]
            target = moved(chip, axis, one)
            theirs = flip(mine, one) if slot == 0 else flip(mine, 2)
            cols = grads[arr].at[:, :, :, :, pl.ds(col, width)]
            reach(n, slot, at_axis(cols, axis, theirs, 3), came[n][0].at[slot], target)
    for slot in (1, 0):
        for n, (arr, col, width, colour) in enumerate(REDUCE_PARTS):
            order, (one, two) = plans[n]
            axis = order[0]
            keep = chip[axis] if slot == 0 else flip(chip[axis], two)
            cols = grads[arr].at[:, :, :, :, pl.ds(col, width)]
            loads[n, slot] = pltpu.make_async_copy(at_axis(cols, axis, keep, 3), kept[n].at[slot], load_sem.at[n, slot])
            loads[n, slot].start()

    def remaining(order, stage):
        return [axis for axis in range(3) if axis not in order[:stage]]

    for n in range(n_parts):
        order, (one, two) = plans[n]
        loads[n, 1].wait()
        started[n, 1].wait_recv()
        add_into(kept[n].at[1], came[n][0].at[1], 2)
        reach(n, 2, kept[n].at[1], came[n][1], moved(chip, order[0], two))
    for n in range(n_parts):
        loads[n, 0].wait()
        started[n, 0].wait_recv()
        add_into(kept[n].at[0], came[n][0].at[0], 2)

    def held(n, stage):
        order, _ = plans[n]
        axes = remaining(order, 1)
        ref = kept[n].at[0]
        if stage == 1:
            return ref, axes.index(order[1]), 2
        fixed = axes.index(order[1])
        return at_axis(ref, fixed, chip[order[1]], 2), 0, 1

    for stage in (1, 2):
        base = 3 * stage
        for n in range(n_parts):
            order, (one, two) = plans[n]
            ref, spot, n_axes = held(n, stage)
            mine = chip[order[stage]]
            started[n, base - 1].wait_recv()
            arrived = came[n][2 * stage - 1]
            for slot in (1, 0):
                theirs = flip(mine, one) if slot == 0 else flip(mine, 2)
                view = at_axis(ref, spot, theirs, n_axes)
                add_into(view, at_axis(arrived, spot, theirs, n_axes), n_axes - 1)
                reach(n, base + slot, view, came[n][2 * stage].at[slot], moved(chip, order[stage], one))
            for keep in (flip(mine, two), mine):
                add_into(at_axis(ref, spot, keep, n_axes), at_axis(arrived, spot, keep, n_axes), n_axes - 1)
        for n in range(n_parts):
            order, (one, two) = plans[n]
            ref, spot, n_axes = held(n, stage)
            mine = chip[order[stage]]
            started[n, base + 1].wait_recv()
            view = at_axis(ref, spot, flip(mine, two), n_axes)
            add_into(view, came[n][2 * stage].at[1], n_axes - 1)
            reach(n, base + 2, view, came[n][2 * stage + 1], moved(chip, order[stage], two))
        for n in range(n_parts):
            order, _ = plans[n]
            ref, spot, n_axes = held(n, stage)
            started[n, base].wait_recv()
            add_into(at_axis(ref, spot, chip[order[stage]], n_axes), came[n][2 * stage].at[0], n_axes - 1)

    for n, (arr, col, width, colour) in enumerate(REDUCE_PARTS):
        order, _ = plans[n]
        ref, _, _ = held(n, 2)
        box = ref.at[chip[order[2]]]
        started[n, 8].wait_recv()
        add_into(box, came[n][5], 0)
        if arr == 4:
            reach(n, 9, box, tile, chip, 1 - core)
            continue
        rows = box.shape[0] // 2
        theirs = box.at[pl.ds(pl.multiple_of((1 - core) * rows, rows), rows)]
        reach(n, 9, theirs, sums[arr].at[core, :, pl.ds(col, width)], chip, 1 - core)
    for n, (arr, col, width, colour) in enumerate(REDUCE_PARTS):
        order, _ = plans[n]
        ref, _, _ = held(n, 2)
        box = ref.at[chip[order[2]]]
        started[n, 9].wait_recv()
        if arr == 4:
            sums[4][...] = box[...] + tile[...]
            continue
        rows = box.shape[0] // 2
        sums[arr][core, :, pl.ds(col, width)] = box[pl.ds(pl.multiple_of(core * rows, rows), rows), :]
    for copy in copies:
        copy.wait_send()


def reduce_all(up, down, qkv, out, small):
    grads = [tensor.reshape((4, 4, 4, -1, tensor.shape[-1])) for tensor in (up, down, qkv, out, small)]
    shapes = [jax.ShapeDtypeStruct((2, g.shape[3] // 2, g.shape[4]), jnp.float32) for g in grads[:4]]
    shapes.append(jax.ShapeDtypeStruct((8, 128), jnp.float32))
    kept, came = [], []
    for arr, col, width, colour in REDUCE_PARTS:
        block = (grads[arr].shape[3], width)
        kept.append(pltpu.VMEM((2, 4, 4) + block, jnp.float32))
        for lead in ((2, 4, 4), (4, 4), (2, 4), (4,), (2,), ()):
            came.append(pltpu.VMEM(lead + block, jnp.float32))
    n_parts = len(REDUCE_PARTS)
    return pl.pallas_call(
        reduce_kernel,
        out_shape=shapes,
        in_specs=[ANY] * 5,
        out_specs=[IN_VMEM] * 5,
        scratch_shapes=kept + came + [pltpu.SemaphoreType.DMA((n_parts, 10)), pltpu.SemaphoreType.DMA((n_parts, 10)),
                                      pltpu.SemaphoreType.DMA((n_parts, 2)), pltpu.VMEM((8, 128), jnp.float32)],
        compiler_params=pltpu.CompilerParams(collective_id=1, has_side_effects=True, vmem_limit_bytes=VMEM_LIMIT),
        name='reduce_gradients',
    )(*grads)


def product(einsum_form, first_op, second_op):
    return jnp.einsum(einsum_form, first_op, second_op, preferred_element_type=jnp.float32)


def rope_tables(seq_len, rot_dim):
    inv_freq = 1.0 / (10000.0 ** (jnp.arange(0, rot_dim, 2, dtype=jnp.float32) / rot_dim))
    angles = jnp.arange(seq_len, dtype=jnp.float32)[:, None] * inv_freq[None, :]
    angles = jnp.concatenate([angles, angles], axis=-1)
    return jnp.cos(angles), jnp.sin(angles)


def norm_pair(hidden32, gain_attn, bias_attn, gain_mlp, bias_mlp):
    center = hidden32 - jnp.mean(hidden32, axis=-1, keepdims=True)
    scaled = center * lax.rsqrt(jnp.mean(center * center, axis=-1, keepdims=True) + EPSILON)
    return ((scaled * gain_attn + bias_attn).astype(jnp.bfloat16),
            (scaled * gain_mlp + bias_mlp).astype(jnp.bfloat16))


def rotary_split(qkv_all, cos_tab, sin_tab):
    head_dim = qkv_all.shape[-1] // 3
    rot_dim = head_dim // 4
    half_dim = rot_dim // 2
    cos_b = cos_tab[:, None, :]
    sin_b = sin_tab[:, None, :]

    def rotate_vec(vectors):
        rot_part = vectors[..., :rot_dim]
        turned = jnp.concatenate([-rot_part[..., half_dim:], rot_part[..., :half_dim]], axis=-1)
        return jnp.concatenate([rot_part * cos_b + turned * sin_b, vectors[..., rot_dim:]], axis=-1)

    query_rot = rotate_vec(qkv_all[..., :head_dim]).astype(jnp.bfloat16)
    key_rot = rotate_vec(qkv_all[..., head_dim:2 * head_dim]).astype(jnp.bfloat16)
    return query_rot, key_rot, qkv_all[..., 2 * head_dim:].astype(jnp.bfloat16)


def gelu_bf16(pre_act):
    return jax.nn.gelu(pre_act, approximate=False).astype(jnp.bfloat16)


def layer_forward(hidden, weights, vectors, cos_tab, sin_tab):
    up_weight, down_weight, qkv_weight, out_weight = weights
    ln1_gain, ln1_bias, ln2_gain, ln2_bias, qkv_bias, out_bias, up_bias, down_bias = vectors
    seq_len, d_model = hidden.shape
    num_heads = 16
    head_dim = d_model // num_heads
    hidden32 = hidden.astype(jnp.float32)
    (normed_attn, normed_mlp), norm_pull = jax.vjp(norm_pair, hidden32, ln1_gain, ln1_bias, ln2_gain, ln2_bias)
    qkv_all = (product('sd,de->se', normed_attn, qkv_weight) + qkv_bias).reshape(seq_len, num_heads, 3 * head_dim)
    (query_rot, key_rot, values), rotary_pull = jax.vjp(
        functools.partial(rotary_split, cos_tab=cos_tab, sin_tab=sin_tab), qkv_all)
    scores = product('qhd,khd->hqk', query_rot, key_rot) * head_dim ** -0.5
    causal = lax.broadcasted_iota(jnp.int32, (seq_len, seq_len), 0) >= lax.broadcasted_iota(jnp.int32, (seq_len, seq_len), 1)
    attn_probs = jax.nn.softmax(jnp.where(causal, scores, -1e30), axis=-1)
    probs_bf = attn_probs.astype(jnp.bfloat16)
    context = product('hqk,khd->qhd', probs_bf, values).astype(jnp.bfloat16).reshape(seq_len, d_model)
    attn_out = product('qe,ed->qd', context, out_weight) + out_bias
    pre_act = product('sd,df->sf', normed_mlp, up_weight) + up_bias
    mlp_act, gelu_pull = jax.vjp(gelu_bf16, pre_act)
    mlp_out = product('sf,fd->sd', mlp_act, down_weight) + down_bias
    layer_out = (hidden32 + attn_out + mlp_out).astype(jnp.bfloat16)
    saved_state = (norm_pull, normed_attn, normed_mlp, rotary_pull, query_rot, key_rot, values,
                   attn_probs, probs_bf, context, gelu_pull, mlp_act)
    return layer_out, saved_state


def layer_backward(d_out, weights, saved_state, with_partner, half_of):
    up_weight, down_weight, qkv_weight, out_weight = weights
    (norm_pull, normed_attn, normed_mlp, rotary_pull, query_rot, key_rot, values,
     attn_probs, probs_bf, context, gelu_pull, mlp_act) = saved_state
    seq_len, d_model = d_out.shape
    num_heads = 16
    head_dim = d_model // num_heads
    d_out32 = d_out.astype(jnp.float32)
    out_sum_grad = jnp.sum(d_out32, axis=0)

    def both(left, right):
        mine, other = half_of(right)
        return left, mine, with_partner(other)

    d_act = product('sd,fd->sf', d_out, down_weight).astype(jnp.bfloat16)
    (d_pre,) = gelu_pull(d_act)
    up_bias_grad = jnp.sum(d_pre, axis=0)
    d_pre_bf = d_pre.astype(jnp.bfloat16)
    d_normed_mlp = product('sf,df->sd', d_pre_bf, up_weight).astype(jnp.bfloat16)
    d_context = product('qd,ed->qe', d_out, out_weight).astype(jnp.bfloat16).reshape(seq_len, num_heads, head_dim)
    d_probs = product('qhd,khd->hqk', d_context, values).astype(jnp.bfloat16).astype(jnp.float32)
    d_values = product('hqk,qhd->khd', probs_bf, d_context).astype(jnp.bfloat16)
    d_scores = (attn_probs * (d_probs - jnp.sum(d_probs * attn_probs, axis=-1, keepdims=True)) * head_dim ** -0.5).astype(jnp.bfloat16)
    d_query = product('hqk,khd->qhd', d_scores, key_rot).astype(jnp.bfloat16)
    d_key = product('hqk,qhd->khd', d_scores, query_rot).astype(jnp.bfloat16)
    (d_qkv,) = rotary_pull((d_query, d_key, d_values))
    d_qkv = d_qkv.reshape(seq_len, 3 * d_model)
    qkv_bias_grad = jnp.sum(d_qkv, axis=0)
    d_qkv_bf = d_qkv.astype(jnp.bfloat16)
    d_normed_attn = product('se,de->sd', d_qkv_bf, qkv_weight).astype(jnp.bfloat16)
    d_hidden32, gain1_grad, bias1_grad, gain2_grad, bias2_grad = norm_pull((d_normed_attn, d_normed_mlp))
    d_hidden = (d_out32 + d_hidden32).astype(jnp.bfloat16)

    def weight_grad(left, left_other, right):
        mine, other = half_of(right)
        rows = jnp.concatenate([left, left_other], axis=0)
        cols = jnp.concatenate([mine, with_partner(other)], axis=0)
        return product('sd,se->de', rows, cols)

    out_half = half_of(d_out)
    d_out_cols = jnp.concatenate([out_half[0], with_partner(out_half[1])], axis=0)

    def on_d_out(left):
        return product('sd,se->de', jnp.concatenate([left, with_partner(left)], axis=0), d_out_cols)

    down_grad = on_d_out(mlp_act)
    out_grad = on_d_out(context)
    up_grad = weight_grad(normed_mlp, with_partner(normed_mlp), d_pre_bf)
    qkv_grad = weight_grad(normed_attn, with_partner(normed_attn), d_qkv_bf)
    vectors = (gain1_grad, bias1_grad, gain2_grad, bias2_grad, qkv_bias_grad, out_sum_grad, up_bias_grad, out_sum_grad)
    return d_hidden, (up_grad, down_grad, qkv_grad, out_grad), vectors


def pack_vectors(vectors):
    packed = jnp.concatenate(vectors, axis=-1)
    return jnp.pad(packed, ((0, 0), (0, 128 - packed.shape[-1])))


def solution(mesh):
    shard_axes = ('node', 'local')
    act_spec = P(shard_axes)
    param_spec = P(None, shard_axes)
    n_local = mesh.shape['local']
    pairs = [(i, i + 1 - 2 * (i % 2)) for i in range(n_local)]

    def with_partner(tensor):
        return lax.ppermute(tensor, 'local', pairs)

    def device_step(x, y_cot, ln1_gain, ln1_bias, qkv_weight, qkv_bias, out_weight, out_bias,
                    ln2_gain, ln2_bias, up_weight, up_bias, down_weight, down_bias):
        num_layers = ln1_gain.shape[0]
        core = lax.rem(lax.axis_index('local'), 2)
        cos_tab, sin_tab = rope_tables(x.shape[1], qkv_weight.shape[3] // 12)

        def half_of(tensor):
            width = tensor.shape[1] // 2
            return (lax.dynamic_slice_in_dim(tensor, core * width, width, 1),
                    lax.dynamic_slice_in_dim(tensor, (1 - core) * width, width, 1))

        small = (ln1_gain, ln1_bias, ln2_gain, ln2_bias, qkv_bias, out_bias, up_bias, down_bias)
        widths = [tensor.shape[1] for tensor in small]
        small_tile = jnp.pad(pack_vectors(small), ((0, 8 - num_layers), (0, 0)))
        layers, small_full = gather_all(up_weight, down_weight, qkv_weight.reshape(num_layers, -1, 3 * x.shape[2]),
                                        out_weight, small_tile)

        def vectors_of(layer):
            found, start = [], 0
            for width in widths:
                found.append(small_full[:, layer, start:start + width].reshape(-1).astype(jnp.float32))
                start += width
            return found

        hidden = x[0]
        states = []
        for layer in range(num_layers):
            hidden, state = layer_forward(hidden, layers[layer], vectors_of(layer), cos_tab, sin_tab)
            states.append(state)
        y_out = hidden
        d_hidden = y_cot[0]
        sums = [None] * num_layers
        for layer in reversed(range(num_layers)):
            d_hidden, weight_grads, vector_grads = layer_backward(d_hidden, layers[layer], states[layer], with_partner, half_of)
            rows = pack_vectors([grad.reshape(128, -1) for grad in vector_grads])
            tiles = jnp.pad(rows.reshape(64, 2, 128), ((0, 0), (0, 6), (0, 0)))
            sums[layer] = reduce_all(*weight_grads, tiles)

        def joined(arr, shape):
            return jnp.stack([s[arr].swapaxes(0, 1).reshape(shape[1:]).astype(jnp.bfloat16) for s in sums])

        small_sums = jnp.stack([lax.dynamic_index_in_dim(s[4], core, 0, False) for s in sums]).astype(jnp.bfloat16)
        small_grads, start = [], 0
        for width in widths:
            small_grads.append(small_sums[:, start:start + width])
            start += width
        g1, b1, g2, b2, qb, ob, ub, db = small_grads
        return (y_out[None], d_hidden[None], g1, b1, joined(2, qkv_weight.shape), qb, joined(3, out_weight.shape), ob,
                g2, b2, joined(0, up_weight.shape), ub, joined(1, down_weight.shape), db)

    return jax.shard_map(device_step, mesh=mesh,
                         in_specs=(act_spec, act_spec) + (param_spec,) * 12,
                         out_specs=(act_spec, act_spec) + (param_spec,) * 12,
                         check_vma=False)
```

time: 5890 us -> 712 us (0.12)
  waiting for transfers between devices: 5320 us -> 0.04 us
  Pallas kernels: 0 us -> 322 us
  blocking collectives: 137 us -> 0 us
    reduce_scatter x8 -> x0, waiting for transfers between devices: 5040 us -> none  [scatter_grads(): lax.psum_scatter(grad_arr, shard_axes, scatter_dimension=0, tiled=True)]
    pallas_call x0 -> x3, Pallas kernels: none -> 322 us  [the longest x2 205 us: reduce_all(): pl.pallas_call(reduce_kernel, out_shape=shapes, in_specs=[ANY] * 5, out_s...]
    all_gather x8 -> x0, waiting for transfers between devices: 278 us -> none  [gather_layer(): lax.all_gather(tensor[layer_idx], shard_axes, axis=0, tiled=True)]
    unnamed x2 -> x0, blocking collectives: 137 us -> none
    dot_general x32 -> x34, matrix products: 275 us -> 267 us  [product(): jnp.einsum(einsum_form, first_op, second_op, preferred_element_type=jnp.f...]
  transfers between devices with their start and end apart: 16 -> 14, of which waited for: 14 -> 0; matrix products, arithmetic and copies ran while one was open for 7% -> 49% of each run, Pallas kernels for 0% -> 31%
where the time goes in v1:
time: 712 us; the launch traced here: 703 us
  Pallas kernels  322 us (45%)
  matrix products  281 us (39%)
  local copies, waits for them, and re-layouts  53.4 us (8%)
  other arithmetic  38.2 us (5%)
    dot_general x34, matrix products, product(): jnp.einsum(einsum_form, first_op, second_op, preferred_element_type=jnp.f...  267 us
    pallas_call x2, Pallas kernels, reduce_all(): pl.pallas_call(reduce_kernel, out_shape=shapes, in_specs=[ANY] * 5, out_s...  205 us
    pallas_call x1, Pallas kernels, gather_all(): pl.pallas_call(functools.partial(gather_kernel, n_layers), out_shape=shap...  117 us
    sub x2, matrix products, layer_forward(): attn_probs = jax.nn.softmax(jnp.where(causal, scores, -1e+30), axis=-1)  14.3 us
  transfers between devices with their start and end apart: 14, of which 0 were waited for; matrix products, arithmetic and copies ran while one was open for 49% of the time, Pallas kernels for 31%

profile of v1, /device:TPU:1, one launch (start us, length us, event | category | flops | bytes accessed | tf_op | source)
XLA Modules:
  0.0 702.6 jit_solution(13593553540031320162)
XLA Ops:
  8.0 117.0 %gather_weights.1 = (bf16[4,4,4,2,8,4096]{5,4,3,2,1,0:T(8,128)(2,1)}, bf16[4,4,4,2,32,1024]{5,4,3,2,1,0:T(8,128)(2,1)}, bf16[4,4,4,2,8,3072]{5,4,3,2,1,0:T(8,128...) custom-call(bf16[2,8,4096]{2,1,0:T(8,128)(2,1)} %refs_0_.1, ...), custom_call_target="tpu_custom_call" | custom-call | tf_op jit(solution)/shard_map/gather_weights/pallas_call | solution.py:152
  132.8 7.3 %convolution_add_fusion.3 = f32[384,3072]{1,0:T(8,128)} fusion(bf16[1024,3072]{1,0:T(8,128)(2,1)} %bitcast.268, f32[3072]{0:T(1024)S(1)} %reshape.604, bf16[1,384,1024]{2,1,0:T(8,128)(2,1)S(1)} %copy-done.4, f32[1024]{0:T(1024)S(1)} %reshape.603, f32[1024]{0:T(1024)S(1)} %reshape.602, f32[384]{0:T(512)S(1)} %fusion.207, f32[384]{0:T(512)S(1)} %broadcast_multiply_fusion.1), kind=kOutput, calls=%fused_computation.93 | convolution fusion | flops 2419458048 | bytes 11820032 | tf_op jit(solution)/shard_map/sd,de->se/dot_general | solution.py:331
  140.1 6.0 copy.49
  153.7 8.8 %fusion.260 = (f32[16,384]{1,0:T(8,128)}, f32[16,384,384]{1,2,0:T(8,128)}) fusion(pred[384,384]{0,1:T(8,128)(4,1)} %iota_compare_fusion, bf16[384,16,48]{0,2,1:T(8,128)(2,1)} %get-tuple-element.103, bf16[384,16,16]{0,2,1:T(8,128)(2,1)} %get-tuple-element.79, bf16[384,16,48]{0,2,1:T(8,128)(2,1)} %get-tuple-element.102, ...), kind=kOutput, calls=%fused_computation.400 | convolution fusion | flops 314573184 | bytes 11182080 | tf_op jit(solution)/shard_map/sub | solution.py:382
  162.5 5.5 fusion.149
  173.8 20.6 %multiply_convert_fusion.1 = (bf16[384,4096]{1,0:T(8,128)(2,1)}, f32[384,4096]{1,0:T(8,128)}, f32[384,4096]{1,0:T(8,128)}) fusion(f32[4096]{0:T(1024)S(1)} %reshape.608, bf16[1024,4096]{1,0:T(8,128)(2,1)} %bitcast.254, bf16[1,384,1024]{2,1,0:T(8,128)(2,1)S(1)} %copy-done.4, f32[1024]{0:T(1024)S(1)} %reshape.607, f32[1024]{0:T(1024)S(1)} %reshape.606, ...), kind=kOutput, calls=%fused_computation.63 | convolution fusion | flops 3327393792 | bytes 24931328 | tf_op jit(solution)/shard_map/sd,df->sf/dot_general | solution.py:331
  194.4 6.9 fusion.262
  207.3 7.8 %convolution_add_fusion.2 = f32[384,3072]{1,0:T(8,128)} fusion(bf16[384,1024]{1,0:T(8,128)(2,1)} %get-tuple-element.106, bf16[1024,3072]{1,0:T(8,128)(2,1)} %bitcast.272, f32[3072]{0:T(1024)S(1)} %reshape.612), kind=kOutput, calls=%fused_computation.92 | convolution fusion | flops 2417098752 | bytes 11808768 | tf_op jit(solution)/shard_map/sd,de->se/dot_general | solution.py:331
  215.1 6.2 copy.59
  231.7 5.5 fusion.261
  237.8 6.4 fusion.166
  244.3 12.7 %convert_bitcast_fusion.4 = f32[384,16,64]{0,2,1:T(8,128)S(1)} fusion(bf16[16,384,384]{1,2,0:T(8,128)(2,1)} %convolution_convert_fusion.3, bf16[384,16,48]{0,2,1:T(8,128)(2,1)S(1)} %copy-done.34, bf16[384,16,16]{0,2,1:T(8,128)(2,1)S(1)} %copy-done.42, f32[16,384,384]{1,2,0:T(8,128)} %get-tuple-element.160, f32[16,384]{1,0:T(8,128)} %copy-done.71), kind=kOutput, calls=%fused_computation.220 | convolution fusion | flops 325589376 | bytes 16539648 | tf_op jit(solution)/shard_map/hqk,qhd->khd/dot_general | solution.py:331
  257.1 13.5 %convert_bitcast_fusion.3 = f32[384,16,64]{0,2,1:T(8,128)} fusion(bf16[16,384,384]{1,2,0:T(8,128)(2,1)} %convolution_convert_fusion.3, bf16[384,16,48]{0,2,1:T(8,128)(2,1)S(1)} %copy-done.32, bf16[384,16,16]{0,2,1:T(8,128)(2,1)S(1)} %get-tuple-element.77, f32[16,384,384]{1,2,0:T(8,128)} %get-tuple-element.160, f32[16,384]{1,0:T(8,128)S(1)} %copy-done.72), kind=kOutput, calls=%fused_computation.219 | convolution fusion | flops 325589376 | bytes 16539648 | tf_op jit(solution)/shard_map/hqk,khd->qhd/dot_general | solution.py:331
  282.3 20.2 %multiply_convert_fusion = (bf16[384,4096]{1,0:T(8,128)(2,1)}, f32[384,4096]{1,0:T(8,128)}, f32[384,4096]{1,0:T(8,128)}) fusion(f32[4096]{0:T(1024)S(1)} %copy-done.55, bf16[384,1024]{1,0:T(8,128)(2,1)} %get-tuple-element.107, bf16[1024,4096]{1,0:T(8,128)(2,1)S(1)} %bitcast.267), kind=kOutput, calls=%fused_computation.50 | convolution fusion | flops 3325034496 | bytes 24920064 | tf_op jit(solution)/shard_map/sd,df->sf/dot_general | solution.py:331
  302.5 8.4 %fusion.249 = (f32[4096]{0:T(1024)S(1)}, bf16[384,4096]{1,0:T(8,128)(2,1)S(1)}) fusion(f32[384,4096]{1,0:T(8,128)} %get-tuple-element.69, f32[384,4096]{1,0:T(8,128)} %get-tuple-element.158, bf16[4096,1024]{1,0:T(8,128)(2,1)S(1)} %bitcast.263, bf16[1,384,1024]{2,1,0:T(8,128)(2,1)S(1)} %copy-done.19), kind=kOutput, calls=%fused_computation.389 | convolution fusion | flops 3247960064 | bytes 24920064 | tf_op jit(solution)/shard_map/sd,fd->sf/dot_general | solution.py:331
  310.9 8.6 %fusion.124 = (f32[1024]{0:T(1024)S(1)}, f32[384]{0:T(512)S(1)}, f32[1024]{0:T(1024)S(1)}, f32[1024]{0:T(1024)S(1)}, f32[1024]{0:T(1024)S(1)}, /*index=5*/bf16[384,1024]{1,0:T(8,128)(2,1)S(1)}) fusion(bf16[384,1024]{1,0:T(8,128)(2,1)S(1)} %copy-done.7, f32[384]{0:T(512)S(1)} %fusion.208, f32[384]{0:T(512)S(1)} %broadcast_multiply_fusion, ...), kind=kOutput, calls=%fused_computation.192 | convolution fusion | flops 3227905536 | bytes 13922816 | tf_op jit(solution)/shard_map/sf,df->sd/dot_general | solution.py:331
  322.6 5.8 fusion.155
  332.7 6.7 fusion.169
  339.4 4.8 convolution_convert_fusion.2
  344.2 14.5 %convert_bitcast_fusion.2 = f32[384,16,64]{0,2,1:T(8,128)} fusion(bf16[16,384,384]{1,2,0:T(8,128)(2,1)} %convolution_convert_fusion.2, bf16[384,16,48]{0,2,1:T(8,128)(2,1)} %get-tuple-element.102, bf16[384,16,16]{0,2,1:T(8,128)(2,1)} %get-tuple-element.78, f32[16,384,384]{1,2,0:T(8,128)} %get-tuple-element.155, f32[16,384]{1,0:T(8,128)S(1)} %copy-done.70), kind=kOutput, calls=%fused_computation.218 | convolution fusion | flops 325589376 | bytes 16539648 | tf_op jit(solution)/shard_map/hqk,qhd->khd/dot_general | solution.py:331
  358.6 14.2 %convert_bitcast_fusion.1 = f32[384,16,64]{0,2,1:T(8,128)} fusion(bf16[16,384,384]{1,2,0:T(8,128)(2,1)} %convolution_convert_fusion.2, bf16[384,16,48]{0,2,1:T(8,128)(2,1)} %get-tuple-element.103, bf16[384,16,16]{0,2,1:T(8,128)(2,1)S(1)} %copy-done.40, f32[16,384,384]{1,2,0:T(8,128)} %get-tuple-element.155, f32[16,384]{1,0:T(8,128)S(1)} %copy-done.70), kind=kOutput, calls=%fused_computation.217 | convolution fusion | flops 325589376 | bytes 16539648 | tf_op jit(solution)/shard_map/hqk,khd->qhd/dot_general | solution.py:331
  386.1 9.0 %fusion.263 = f32[384,1024]{1,0:T(8,128)} fusion(bf16[384,4096]{1,0:T(8,128)(2,1)} %get-tuple-element.68, bf16[4096,1024]{1,0:T(8,128)(2,1)} %bitcast.260), kind=kOutput, calls=%fused_computation.403 | convolution fusion | flops 3221225472 | bytes 13107200 | tf_op jit(solution)/shard_map/sf,fd->sd/dot_general | solution.py:331
  395.2 13.0 %fusion.248 = (f32[4096]{0:T(1024)S(1)}, bf16[384,4096]{1,0:T(8,128)(2,1)S(1)}) fusion(f32[384,4096]{1,0:T(8,128)} %get-tuple-element.71, f32[384,4096]{1,0:T(8,128)} %get-tuple-element.153, bf16[384,1024]{1,0:T(8,128)(2,1)S(1)} %get-tuple-element.63, bf16[4096,1024]{1,0:T(8,128)(2,1)} %bitcast.259), kind=kOutput, calls=%fused_computation.388 | convolution fusion | flops 3247960064 | bytes 24920064 | tf_op jit(solution)/shard_map/sd,fd->sf/dot_general | solution.py:331
  408.3 5.4 fusion.127
  439.5 7.2 %fusion.76 = f32[1024,1536]{1,0:T(8,128)} fusion(bf16[384,1536]{0,1:T(8,128)(2,1)} %collective-permute-done.12, bf16[384,1536]{0,1:T(8,128)(2,1)S(1)} %copy-done.22, bf16[384,1024]{1,0:T(8,128)(2,1)} %collective-permute-done.11, bf16[384,1024]{1,0:T(8,128)(2,1)} %get-tuple-element.106), kind=kOutput, calls=%fused_computation.140 | convolution fusion | flops 2423783424 | bytes 10223616 | tf_op jit(solution)/shard_map/sd,se->de/dot_general | solution.py:331
  446.7 7.0 fusion.72
  453.7 8.7 %fusion.64 = f32[1024,2048]{1,0:T(8,128)} fusion(bf16[384,2048]{1,0:T(8,128)(2,1)} %collective-permute-done.8, bf16[384,2048]{1,0:T(8,128)(2,1)S(1)} %copy-done.9, bf16[384,1024]{1,0:T(8,128)(2,1)} %collective-permute-done.7, bf16[384,1024]{1,0:T(8,128)(2,1)} %get-tuple-element.107), kind=kOutput, calls=%fused_computation.106 | convolution fusion | flops 3230662656 | bytes 13107200 | tf_op jit(solution)/shard_map/sd,se->de/dot_general | solution.py:331
  462.4 6.0 fusion.60
  468.4 9.6 %fusion.26 = f32[4096,512]{1,0:T(8,128)} fusion(bf16[384,4096]{1,0:T(8,128)(2,1)} %collective-permute-done.9, bf16[384,4096]{1,0:T(8,128)(2,1)} %get-tuple-element.68, bf16[384,512]{1,0:T(8,128)(2,1)} %collective-permute-done.10, bf16[384,512]{1,0:T(8,128)(2,1)S(1)} %copy-done.35), kind=kOutput, calls=%fused_computation.38 | convolution fusion | flops 3235381248 | bytes 15466496 | tf_op jit(solution)/shard_map/sd,se->de/dot_general | solution.py:331
  478.0 103.3 %reduce_gradients.3 = (f32[2,8,2048]{2,1,0:T(8,128)}, f32[2,32,512]{2,1,0:T(8,128)}, f32[2,8,1536]{2,1,0:T(8,128)}, f32[2,8,512]{2,1,0:T(8,128)}, f32[8,128]{1,0:T(8,128)}) custom-call(f32[4,4,4,16,2048]{4,3,2,1,0:T(8,128)} %bitcast.222, f32[4,4,4,64,512]{4,3,2,1,0:T(8,128)} %bitcast.233, f32[4,4,4,16,1536]{4,3,2,1,0:T(8,128)} %bitcast.236, ...), custom_call_target="tpu_custom_call" | custom-call | tf_op jit(solution)/shard_map/reduce_gradients/pallas_call | solution.py:318
  582.0 9.6 %fusion.22 = f32[4096,512]{1,0:T(8,128)} fusion(bf16[384,4096]{1,0:T(8,128)(2,1)} %collective-permute-done.2, bf16[384,4096]{1,0:T(8,128)(2,1)} %get-tuple-element.70, bf16[384,512]{1,0:T(8,128)(2,1)} %collective-permute-done.3, bf16[384,512]{1,0:T(8,128)(2,1)S(1)} %copy-done.36), kind=kOutput, calls=%fused_computation.34 | convolution fusion | flops 3235381248 | bytes 15466496 | tf_op jit(solution)/shard_map/sd,se->de/dot_general | solution.py:331
  591.5 101.6 %reduce_gradients.2 = (f32[2,8,2048]{2,1,0:T(8,128)}, f32[2,32,512]{2,1,0:T(8,128)}, f32[2,8,1536]{2,1,0:T(8,128)}, f32[2,8,512]{2,1,0:T(8,128)}, f32[8,128]{1,0:T(8,128)}) custom-call(f32[4,4,4,16,2048]{4,3,2,1,0:T(8,128)} %bitcast.221, f32[4,4,4,64,512]{4,3,2,1,0:T(8,128)} %bitcast.234, f32[4,4,4,16,1536]{4,3,2,1,0:T(8,128)} %bitcast.235, ...), custom_call_target="tpu_custom_call" | custom-call | tf_op jit(solution)/shard_map/reduce_gradients/pallas_call | solution.py:318
  (341 shorter events, 112.8 us)
Async XLA Ops:
  0.6 130.1 %copy-start.4 = (bf16[1,384,1024]{2,1,0:T(8,128)(2,1)S(1)}, bf16[1,384,1024]{2,1,0:T(8,128)(2,1)}, u32[]{:S(2)}) copy-start(bf16[1,384,1024]{2,1,0:T(8,128)(2,1)} %param.14) | copy-start | bytes 2359300
  2.8 412.9 %collective-permute-start.10 = (bf16[384,512]{1,0:T(8,128)(2,1)}, bf16[384,512]{1,0:T(8,128)(2,1)}, u32[]{:S(2)}, u32[]{:S(2)}) collective-permute-start(bf16[384,512]{1,0:T(8,128)(2,1)} %get-tuple-element.112), channel_id=1, source_target_pairs={{0,1},{1,0},{2,3},{3,2},{4,5},{5,4},{6,7},{7,6},{8,9},{9,8},{10,11... | collective-permute-start | bytes 1179656 | tf_op jit(solution)/shard_map/ppermute | solution.py:461
  131.0 42.8 %copy-start.49 = (f32[384]{0:T(512)}, f32[384]{0:T(512)S(1)}, u32[]{:S(2)}) copy-start(f32[384]{0:T(512)S(1)} %broadcast_multiply_fusion.1) | copy-start | bytes 4612
  131.3 42.5 %copy-start.60 = (f32[384]{0:T(512)}, f32[384]{0:T(512)S(1)}, u32[]{:S(2)}) copy-start(f32[384]{0:T(512)S(1)} %fusion.207) | copy-start | bytes 4612
  150.3 80.1 %copy-start.27 = (f32[384,16]{0,1:T(8,128)}, f32[384,16]{0,1:T(8,128)S(1)}, u32[]{:S(2)}) copy-start(f32[384,16]{0,1:T(8,128)S(1)} %get-tuple-element.145) | copy-start | bytes 73732
  150.3 80.1 %copy-start.29 = (f32[384,16]{0,1:T(8,128)}, f32[384,16]{0,1:T(8,128)S(1)}, u32[]{:S(2)}) copy-start(f32[384,16]{0,1:T(8,128)S(1)} %get-tuple-element.146) | copy-start | bytes 73732
  168.0 249.7 %collective-permute-start.6 = (bf16[384,1024]{0,1:T(8,128)(2,1)}, bf16[384,1024]{0,1:T(8,128)(2,1)}, u32[]{:S(2)}, u32[]{:S(2)}) collective-permute-start(bf16[384,1024]{0,1:T(8,128)(2,1)} %bitcast.6), channel_id=1, source_target_pairs={{0,1},{1,0},{2,3},{3,2},{4,5},{5,4},{6,7},{7,6},{8,9},{9,8},{10,11... | collective-permute-start | bytes 2359304 | tf_op jit(solution)/shard_map/ppermute | solution.py:461
  173.6 20.9 %copy-start.64 = (f32[1024]{0:T(1024)}, f32[1024]{0:T(1024)S(1)}, u32[]{:S(2)}) copy-start(f32[1024]{0:T(1024)S(1)} %reshape.607) | copy-start | bytes 12292
  173.7 20.7 %copy-start.58 = (f32[1024]{0:T(1024)}, f32[1024]{0:T(1024)S(1)}, u32[]{:S(2)}) copy-start(f32[1024]{0:T(1024)S(1)} %reshape.606) | copy-start | bytes 12292
  206.3 211.5 %collective-permute-start.11 = (bf16[384,1024]{1,0:T(8,128)(2,1)}, bf16[384,1024]{1,0:T(8,128)(2,1)}, u32[]{:S(2)}, u32[]{:S(2)}) collective-permute-start(bf16[384,1024]{1,0:T(8,128)(2,1)} %get-tuple-element.106), channel_id=1, source_target_pairs={{0,1},{1,0},{2,3},{3,2},{4,5},{5,4},{6,7},{7,6},{8,9},{9,8},{10,11... | collective-permute-start | bytes 2359304 | tf_op jit(solution)/shard_map/ppermute | solution.py:461
  206.8 217.9 %collective-permute-start.7 = (bf16[384,1024]{1,0:T(8,128)(2,1)}, bf16[384,1024]{1,0:T(8,128)(2,1)}, u32[]{:S(2)}, u32[]{:S(2)}) collective-permute-start(bf16[384,1024]{1,0:T(8,128)(2,1)} %get-tuple-element.107), channel_id=1, source_target_pairs={{0,1},{1,0},{2,3},{3,2},{4,5},{5,4},{6,7},{7,6},{8,9},{9,8},{10,11... | collective-permute-start | bytes 2359304 | tf_op jit(solution)/shard_map/ppermute | solution.py:461
  257.0 14.9 %copy-start.20 = (f32[384,16,64]{0,2,1:T(8,128)}, f32[384,16,64]{0,2,1:T(8,128)S(1)}, u32[]{:S(2)}) copy-start(f32[384,16,64]{0,2,1:T(8,128)S(1)} %convert_bitcast_fusion.4) | copy-start | bytes 4718596
  279.5 23.0 %slice-start.4 = ((s8[8388608]{0:T(1024)(128)(4,1)}), s8[4194304]{0:T(1024)(128)(4,1)S(1)}, s32[]{:S(2)}) async-start(s8[8388608]{0:T(1024)(128)(4,1)} %bitcast.261), calls=%async_computation.4 | async-start | bytes 8388608
  282.3 20.2 %copy-start.19 = (bf16[1,384,1024]{2,1,0:T(8,128)(2,1)S(1)}, bf16[1,384,1024]{2,1,0:T(8,128)(2,1)}, u32[]{:S(2)}) copy-start(bf16[1,384,1024]{2,1,0:T(8,128)(2,1)} %param.15) | copy-start | bytes 2359300
  282.3 20.2 %slice-start.5 = ((s8[8388608]{0:T(1024)(128)(4,1)}), s8[4194304]{0:T(1024)(128)(4,1)S(1)}, s32[]{:S(2)}) async-start(s8[8388608]{0:T(1024)(128)(4,1)} %bitcast.261), calls=%async_computation.5 | async-start | bytes 8388608
  321.7 93.9 %collective-permute-start.3 = (bf16[384,512]{1,0:T(8,128)(2,1)}, bf16[384,512]{1,0:T(8,128)(2,1)}, u32[]{:S(2)}, u32[]{:S(2)}) collective-permute-start(bf16[384,512]{1,0:T(8,128)(2,1)} %get-tuple-element.109), channel_id=1, source_target_pairs={{0,1},{1,0},{2,3},{3,2},{4,5},{5,4},{6,7},{7,6},{8,9},{9,8},{10,11... | collective-permute-start | bytes 1179656 | tf_op jit(solution)/shard_map/ppermute | solution.py:461
  344.2 14.5 %copy-start.40 = (bf16[384,16,16]{0,2,1:T(8,128)(2,1)S(1)}, bf16[384,16,16]{0,2,1:T(8,128)(2,1)}, u32[]{:S(2)}) copy-start(bf16[384,16,16]{0,2,1:T(8,128)(2,1)} %get-tuple-element.79) | copy-start | bytes 589828
  358.6 14.3 %copy-start.30 = (f32[384,16]{0,1:T(8,128)S(1)}, f32[384,16]{0,1:T(8,128)}, u32[]{:S(2)}) copy-start(f32[384,16]{0,1:T(8,128)} %copy-done.29) | copy-start | bytes 73732
  386.1 22.1 %slice-start.2 = ((s8[8388608]{0:T(1024)(128)(4,1)}), s8[4194304]{0:T(1024)(128)(4,1)S(1)}, s32[]{:S(2)}) async-start(s8[8388608]{0:T(1024)(128)(4,1)} %bitcast.255), calls=%async_computation.2 | async-start | bytes 8388608
  415.6 9.2 %collective-permute-start.13 = (bf16[384,1024]{0,1:T(8,128)(2,1)}, bf16[384,1024]{0,1:T(8,128)(2,1)}, u32[]{:S(2)}, u32[]{:S(2)}) collective-permute-start(bf16[384,1024]{0,1:T(8,128)(2,1)} %bitcast.280), channel_id=1, source_target_pairs={{0,1},{1,0},{2,3},{3,2},{4,5},{5,4},{6,7},{7,6},{8,9},{9,8},{10,11... | collective-permute-start | bytes 2359304 | tf_op jit(solution)/shard_map/ppermute | solution.py:461
  415.7 9.5 %collective-permute-start.4 = (bf16[384,1024]{1,0:T(8,128)(2,1)}, bf16[384,1024]{1,0:T(8,128)(2,1)}, u32[]{:S(2)}, u32[]{:S(2)}) collective-permute-start(bf16[384,1024]{1,0:T(8,128)(2,1)} %get-tuple-element.104), channel_id=1, source_target_pairs={{0,1},{1,0},{2,3},{3,2},{4,5},{5,4},{6,7},{7,6},{8,9},{9,8},{10,11... | collective-permute-start | bytes 2359304 | tf_op jit(solution)/shard_map/ppermute | solution.py:461
  417.7 50.7 %collective-permute-start.9 = (bf16[384,4096]{1,0:T(8,128)(2,1)}, bf16[384,4096]{1,0:T(8,128)(2,1)}, u32[]{:S(2)}, u32[]{:S(2)}) collective-permute-start(bf16[384,4096]{1,0:T(8,128)(2,1)} %get-tuple-element.68), channel_id=1, source_target_pairs={{0,1},{1,0},{2,3},{3,2},{4,5},{5,4},{6,7},{7,6},{8,9},{9,8},{10,11... | collective-permute-start | bytes 9437192 | tf_op jit(solution)/shard_map/ppermute | solution.py:461
  417.8 13.5 %collective-permute-start.12 = (bf16[384,1536]{0,1:T(8,128)(2,1)}, bf16[384,1536]{0,1:T(8,128)(2,1)}, u32[]{:S(2)}, u32[]{:S(2)}) collective-permute-start(bf16[384,1536]{0,1:T(8,128)(2,1)} %get-tuple-element.99), channel_id=1, source_target_pairs={{0,1},{1,0},{2,3},{3,2},{4,5},{5,4},{6,7},{7,6},{8,9},{9,8},{10,11... | collective-permute-start | bytes 3538952 | tf_op jit(solution)/shard_map/ppermute | solution.py:461
  424.7 157.3 %collective-permute-start.2 = (bf16[384,4096]{1,0:T(8,128)(2,1)}, bf16[384,4096]{1,0:T(8,128)(2,1)}, u32[]{:S(2)}, u32[]{:S(2)}) collective-permute-start(bf16[384,4096]{1,0:T(8,128)(2,1)} %get-tuple-element.70), channel_id=1, source_target_pairs={{0,1},{1,0},{2,3},{3,2},{4,5},{5,4},{6,7},{7,6},{8,9},{9,8},{10,11... | collective-permute-start | bytes 9437192 | tf_op jit(solution)/shard_map/ppermute | solution.py:461
  424.8 21.8 %collective-permute-start.5 = (bf16[384,1536]{0,1:T(8,128)(2,1)}, bf16[384,1536]{0,1:T(8,128)(2,1)}, u32[]{:S(2)}, u32[]{:S(2)}) collective-permute-start(bf16[384,1536]{0,1:T(8,128)(2,1)} %get-tuple-element.97), channel_id=1, source_target_pairs={{0,1},{1,0},{2,3},{3,2},{4,5},{5,4},{6,7},{7,6},{8,9},{9,8},{10,11... | collective-permute-start | bytes 3538952 | tf_op jit(solution)/shard_map/ppermute | solution.py:461
  425.2 28.5 %collective-permute-start.8 = (bf16[384,2048]{1,0:T(8,128)(2,1)}, bf16[384,2048]{1,0:T(8,128)(2,1)}, u32[]{:S(2)}, u32[]{:S(2)}) collective-permute-start(bf16[384,2048]{1,0:T(8,128)(2,1)} %get-tuple-element.95), channel_id=1, source_target_pairs={{0,1},{1,0},{2,3},{3,2},{4,5},{5,4},{6,7},{7,6},{8,9},{9,8},{10,11... | collective-permute-start | bytes 4718600 | tf_op jit(solution)/shard_map/ppermute | solution.py:461
  431.3 31.1 %collective-permute-start.1 = (bf16[384,2048]{1,0:T(8,128)(2,1)}, bf16[384,2048]{1,0:T(8,128)(2,1)S(1)}, u32[]{:S(2)}, u32[]{:S(2)}) collective-permute-start(bf16[384,2048]{1,0:T(8,128)(2,1)} %get-tuple-element.93), channel_id=1, source_target_pairs={{0,1},{1,0},{2,3},{3,2},{4,5},{5,4},{6,7},{7,6},{8,9},{9,8},{10,11... | collective-permute-start | bytes 4718600 | tf_op jit(solution)/shard_map/ppermute | solution.py:461
  446.6 15.8 %collective-permute-start = (bf16[384,1024]{1,0:T(8,128)(2,1)S(1)}, bf16[384,1024]{1,0:T(8,128)(2,1)S(1)}, u32[]{:S(2)}, u32[]{:S(2)}) collective-permute-start(bf16[384,1024]{1,0:T(8,128)(2,1)S(1)} %copy-done.23), channel_id=1, source_target_pairs={{0,1},{1,0},{2,3},{3,2},{4,5},{5,4},{6,7},{7,6},{8,9},{9,8},{10,11... | collective-permute-start | bytes 2359304 | tf_op jit(solution)/shard_map/ppermute | solution.py:461
  591.5 104.1 %copy-start.48 = (f32[2,8,512]{2,1,0:T(8,128)S(1)}, f32[2,8,512]{2,1,0:T(8,128)}, u32[]{:S(2)}) copy-start(f32[2,8,512]{2,1,0:T(8,128)} %get-tuple-element.47) | copy-start | bytes 98308
  591.5 104.1 %copy-start.46 = (f32[2,8,1536]{2,1,0:T(8,128)S(1)}, f32[2,8,1536]{2,1,0:T(8,128)}, u32[]{:S(2)}) copy-start(f32[2,8,1536]{2,1,0:T(8,128)} %get-tuple-element.45) | copy-start | bytes 294916
  591.5 104.3 %copy-start.45 = (f32[2,8,2048]{2,1,0:T(8,128)S(1)}, f32[2,8,2048]{2,1,0:T(8,128)}, u32[]{:S(2)}) copy-start(f32[2,8,2048]{2,1,0:T(8,128)} %get-tuple-element.49) | copy-start | bytes 393220
  591.5 104.3 %copy-start.44 = (f32[2,32,512]{2,1,0:T(8,128)S(1)}, f32[2,32,512]{2,1,0:T(8,128)}, u32[]{:S(2)}) copy-start(f32[2,32,512]{2,1,0:T(8,128)} %get-tuple-element.51) | copy-start | bytes 393220
  (68 other events, 414.4 us)

commit v2 on v1

--- a/solution.py
+++ b/solution.py
@@ -327,127 +327,330 @@
     )(*grads)
 
 
+SEQ, WIDTH, HIDDEN, TILE = 384, 1024, 4096, 512
+N_TILES = HIDDEN // TILE
+PAIR = 128
+INV_SQRT2 = 0.7071067811865476
+INV_SQRT2PI = 0.3989422804014327
+SCALE = 0.125
+
+
+def dot(a, b):
+    return lax.dot_general(a, b, (((1,), (0,)), ((), ())), preferred_element_type=jnp.float32)
+
+
+def dot_t(a, b):
+    return lax.dot_general(a, b, (((1,), (1,)), ((), ())), preferred_element_type=jnp.float32)
+
+
+def lanes(start, width=PAIR):
+    return pl.ds(pl.multiple_of(start, PAIR), width)
+
+
+def turn(x, cos, sin_a, sin_b):
+    return x * cos + pltpu.roll(x, PAIR - 8, 1) * sin_a + pltpu.roll(x, 8, 1) * sin_b
+
+
+def turn_back(d, cos, sin_a, sin_b):
+    return d * cos + pltpu.roll(d * sin_a, 8, 1) + pltpu.roll(d * sin_b, PAIR - 8, 1)
+
+
+def split_heads(x):
+    first = lax.broadcasted_iota(jnp.int32, (PAIR, PAIR), 1) < PAIR // 2
+    rows = []
+    for j in range(SEQ // PAIR):
+        block = x[j * PAIR:(j + 1) * PAIR]
+        rows += [jnp.where(first, block, jnp.zeros_like(block)), jnp.where(first, jnp.zeros_like(block), block)]
+    return jnp.concatenate(rows, axis=0)
+
+
+def probabilities(q_block, keys, i):
+    scores = dot_t(q_block, keys)
+    causal = (lax.broadcasted_iota(jnp.int32, (PAIR, PAIR), 0) >= lax.broadcasted_iota(jnp.int32, (PAIR, PAIR), 1))
+    probs = [None] * (2 * i + 2)
+    for head in range(2):
+        chunks = [scores[:, (2 * j + head) * PAIR:(2 * j + head + 1) * PAIR] * SCALE for j in range(i + 1)]
+        chunks[i] = jnp.where(causal, chunks[i], -1e30)
+        top = chunks[0]
+        for chunk in chunks[1:]:
+            top = jnp.maximum(top, chunk)
+        top = jnp.max(top, axis=1, keepdims=True)
+        chunks = [jnp.exp(chunk - top) for chunk in chunks]
+        total = chunks[0]
+        for chunk in chunks[1:]:
+            total = total + chunk
+        inverse = 1.0 / jnp.sum(total, axis=1, keepdims=True)
+        for j in range(i + 1):
+            probs[2 * j + head] = chunks[j] * inverse
+    return probs
+
+
+def normalised(h):
+    center = h - jnp.mean(h, axis=1, keepdims=True)
+    inverse = lax.rsqrt(jnp.mean(center * center, axis=1, keepdims=True) + EPSILON)
+    return center * inverse, inverse
+
+
+LN_ROWS = 64
+
+
+def forward_kernel(h_ref, g1_ref, b1_ref, g2_ref, b2_ref, qkvb_ref, outb_ref, upb_ref, cos_ref, sina_ref, sinb_ref,
+                   wqkv, wout, wup, wdown, y_ref, n1_ref, n2_ref, qkv_ref, ctx_ref, act_ref, pre_hbm,
+                   wqkv_v, wout_v, wup_v, wdown_v, acc, pre_v, sems, pre_sems):
+    loads = []
+    for k in range(6):
+        loads.append(pltpu.make_async_copy(wqkv.at[:, pl.ds(k * 512, 512)], wqkv_v.at[:, pl.ds(k * 512, 512)], sems.at[k]))
+    loads.append(pltpu.make_async_copy(wout, wout_v, sems.at[6]))
+    for t in range(N_TILES):
+        loads.append(pltpu.make_async_copy(wup.at[:, pl.ds(t * TILE, TILE)], wup_v.at[:, pl.ds(t * TILE, TILE)], sems.at[7 + 2 * t]))
+        loads.append(pltpu.make_async_copy(wdown.at[pl.ds(t * TILE, TILE)], wdown_v.at[pl.ds(t * TILE, TILE)], sems.at[8 + 2 * t]))
+    for load in loads:
+        load.start()
+
+    @pl.loop(0, SEQ // LN_ROWS)
+    def _(r):
+        rows = pl.ds(pl.multiple_of(r * LN_ROWS, LN_ROWS), LN_ROWS)
+        scaled, _ = normalised(h_ref[rows, :].astype(jnp.float32))
+        n1_ref[rows, :] = (scaled * g1_ref[...] + b1_ref[...]).astype(jnp.bfloat16)
+        n2_ref[rows, :] = (scaled * g2_ref[...] + b2_ref[...]).astype(jnp.bfloat16)
+
+    for k in range(6):
+        loads[k].wait()
+        x = dot(n1_ref[...], wqkv_v[:, k * 512:(k + 1) * 512]) + qkvb_ref[:, k * 512:(k + 1) * 512]
+        for c in range(4):
+            block = x[:, c * PAIR:(c + 1) * PAIR]
+            if k < 4:
+                block = turn(block, cos_ref[...], sina_ref[...], sinb_ref[...])
+            qkv_ref[:, k * 512 + c * PAIR:k * 512 + (c + 1) * PAIR] = block.astype(jnp.bfloat16)
+
+    @pl.loop(0, WIDTH // PAIR)
+    def _(pair):
+        keys = split_heads(qkv_ref[:, lanes(WIDTH + pair * PAIR)])
+        values = split_heads(qkv_ref[:, lanes(2 * WIDTH + pair * PAIR)])
+        for i in range(SEQ // PAIR):
+            n = (i + 1) * 2 * PAIR
+            probs = probabilities(qkv_ref[i * PAIR:(i + 1) * PAIR, lanes(pair * PAIR)], keys[:n], i)
+            probs = jnp.concatenate([p.astype(jnp.bfloat16) for p in probs], axis=1)
+            ctx_ref[i * PAIR:(i + 1) * PAIR, lanes(pair * PAIR)] = dot(probs, values[:n]).astype(jnp.bfloat16)
+
+    loads[6].wait()
+    for k in range(2):
+        cols = slice(k * 512, (k + 1) * 512)
+        acc[:, cols] = h_ref[:, cols].astype(jnp.float32) + dot(ctx_ref[...], wout_v[:, cols]) + outb_ref[:, cols]
+    stores = []
+    for t in range(N_TILES):
+        cols = slice(t * TILE, (t + 1) * TILE)
+        loads[7 + 2 * t].wait()
+        pre = dot(n2_ref[...], wup_v[:, cols]) + upb_ref[:, cols]
+        pre_v[t] = pre
+        stores.append(pltpu.make_async_copy(pre_v.at[t], pre_hbm.at[t], pre_sems.at[t]))
+        stores[-1].start()
+        act_ref[:, cols] = (0.5 * pre * (1.0 + lax.erf(pre * INV_SQRT2))).astype(jnp.bfloat16)
+        loads[8 + 2 * t].wait()
+        acc[...] += dot(act_ref[:, cols], wdown_v[cols, :])
+    y_ref[...] = acc[...].astype(jnp.bfloat16)
+    for store in stores:
+        store.wait()
+
+
+def forward_layer(hidden, weights, vectors, tables):
+    up_weight, down_weight, qkv_weight, out_weight = weights
+    g1, b1, g2, b2, qkv_bias, out_bias, up_bias, down_bias = [v.reshape(1, -1) for v in vectors]
+    bf16 = jnp.bfloat16
+    shapes = [((SEQ, WIDTH), bf16)] * 3 + [((SEQ, 3 * WIDTH), bf16), ((SEQ, WIDTH), bf16), ((SEQ, HIDDEN), bf16),
+                                           ((N_TILES, SEQ, TILE), jnp.float32)]
+    return pl.pallas_call(
+        forward_kernel,
+        out_shape=[jax.ShapeDtypeStruct(s, d) for s, d in shapes],
+        in_specs=[IN_VMEM] * 11 + [ANY] * 4,
+        out_specs=[IN_VMEM] * 6 + [ANY],
+        scratch_shapes=[pltpu.VMEM((WIDTH, 3 * WIDTH), bf16), pltpu.VMEM((WIDTH, WIDTH), bf16), pltpu.VMEM((WIDTH, HIDDEN), bf16),
+                        pltpu.VMEM((HIDDEN, WIDTH), bf16), pltpu.VMEM((SEQ, WIDTH), jnp.float32),
+                        pltpu.VMEM((N_TILES, SEQ, TILE), jnp.float32), pltpu.SemaphoreType.DMA((23,)), pltpu.SemaphoreType.DMA((N_TILES,))],
+        compiler_params=pltpu.CompilerParams(vmem_limit_bytes=VMEM_LIMIT),
+        cost_estimate=pl.CostEstimate(flops=10 * 10**9, bytes_accessed=45 * 10**6, transcendentals=4 * 10**6),
+        name='forward_layer',
+    )(hidden, g1, b1, g2, b2, qkv_bias, out_bias + down_bias, up_bias, *tables, qkv_weight, out_weight, up_weight, down_weight)
+
+
+def backward_kernel(dout_ref, h_ref, g1_ref, g2_ref, cos_ref, sina_ref, sinb_ref, qkv_ref, pre_hbm, wqkv, wout, wup, wdown,
+                    dh_ref, dpre_ref, dqkv_ref, dg1_ref, db1_ref, dg2_ref, db2_ref, dqkvb_ref, dupb_ref, dsum_ref,
+                    wqkv_v, wout_v, wup_v, wdown_v, pre_v, dn2, dn1, dctx, dk_acc, dv_acc, tile_sems, wout_sem, qkv_sems):
+    def tile_loads(t, slot):
+        start = pl.multiple_of(t * TILE, TILE)
+        return (pltpu.make_async_copy(wdown.at[pl.ds(start, TILE)], wdown_v.at[slot], tile_sems.at[slot, 0]),
+                pltpu.make_async_copy(pre_hbm.at[t], pre_v.at[slot], tile_sems.at[slot, 1]),
+                pltpu.make_async_copy(wup.at[:, pl.ds(start, TILE)], wup_v.at[slot], tile_sems.at[slot, 2]))
+
+    def qkv_load(k):
+        return pltpu.make_async_copy(wqkv.at[:, pl.ds(k * WIDTH, WIDTH)], wqkv_v.at[k % 2], qkv_sems.at[k % 2])
+
+    for t in range(2):
+        for load in tile_loads(t, t):
+            load.start()
+    load_out = pltpu.make_async_copy(wout, wout_v, wout_sem)
+    load_out.start()
+    for k in range(2):
+        qkv_load(k).start()
+    dsum_ref[...] = jnp.sum(dout_ref[...].astype(jnp.float32), axis=0, keepdims=True)
+    dn2[...] = jnp.zeros_like(dn2)
+
+    @pl.loop(0, N_TILES)
+    def _(t):
+        slot = lax.rem(t, 2)
+        cols = pl.ds(pl.multiple_of(t * TILE, TILE), TILE)
+        for load in tile_loads(t, slot):
+            load.wait()
+        d_act = dot_t(dout_ref[...], wdown_v[slot]).astype(jnp.bfloat16).astype(jnp.float32)
+        pre = pre_v[slot]
+        slope = 0.5 * (1.0 + lax.erf(pre * INV_SQRT2)) + pre * (INV_SQRT2PI * jnp.exp(-0.5 * pre * pre))
+        d_pre = d_act * slope
+        dupb_ref[:, cols] = jnp.sum(d_pre, axis=0, keepdims=True)
+        d_pre = d_pre.astype(jnp.bfloat16)
+        dpre_ref[:, cols] = d_pre
+        dn2[...] += dot_t(d_pre, wup_v[slot])
+
+        @pl.when(t + 2 < N_TILES)
+        def _():
+            for load in tile_loads(t + 2, slot):
+                load.start()
+
+    load_out.wait()
+    for k in range(2):
+        rows = slice(k * 512, (k + 1) * 512)
+        dctx[:, rows] = dot_t(dout_ref[...], wout_v[rows, :]).astype(jnp.bfloat16)
+
+    @pl.loop(0, WIDTH // PAIR)
+    def _(pair):
+        at = lanes(pair * PAIR)
+        keys = split_heads(qkv_ref[:, lanes(WIDTH + pair * PAIR)])
+        values = split_heads(qkv_ref[:, lanes(2 * WIDTH + pair * PAIR)])
+        q_t = qkv_ref[:, at].T
+        dc_t = dctx[:, at].T
+        dbq = jnp.zeros((1, PAIR), jnp.float32)
+        for i in range(SEQ // PAIR):
+            n = (i + 1) * 2 * PAIR
+            rows = slice(i * PAIR, (i + 1) * PAIR)
+            probs = probabilities(qkv_ref[rows, at], keys[:n], i)
+            d_all = dot_t(dctx[rows, at], values[:n]).astype(jnp.bfloat16).astype(jnp.float32)
+            d_probs = [d_all[:, j * PAIR:(j + 1) * PAIR] for j in range(2 * i + 2)]
+            d_scores = [None] * (2 * i + 2)
+            for head in range(2):
+                mean = probs[head] * d_probs[head]
+                for j in range(1, i + 1):
+                    mean = mean + probs[2 * j + head] * d_probs[2 * j + head]
+                mean = jnp.sum(mean, axis=1, keepdims=True)
+                for j in range(head, 2 * i + 2, 2):
+                    d_scores[j] = (probs[j] * (d_probs[j] - mean) * SCALE).astype(jnp.bfloat16)
+            d_scores = jnp.concatenate(d_scores, axis=1)
+            probs = jnp.concatenate([p.astype(jnp.bfloat16) for p in probs], axis=1)
+            d_query = dot(d_scores, keys[:n]).astype(jnp.bfloat16).astype(jnp.float32)
+            d_query = turn_back(d_query, cos_ref[rows, :], sina_ref[rows, :], sinb_ref[rows, :])
+            dbq = dbq + jnp.sum(d_query, axis=0, keepdims=True)
+            dqkv_ref[rows, at] = d_query.astype(jnp.bfloat16)
+            d_keys = dot(q_t[:, rows], d_scores)
+            d_values = dot(dc_t[:, rows], probs)
+            old = 2 * i * PAIR
+            if i:
+                dk_acc[:, :old] += d_keys[:, :old]
+                dv_acc[:, :old] += d_values[:, :old]
+            dk_acc[:, old:n] = d_keys[:, old:]
+            dv_acc[:, old:n] = d_values[:, old:]
+        dqkvb_ref[:, at] = dbq
+        first = lax.broadcasted_iota(jnp.int32, (PAIR, PAIR), 0) < PAIR // 2
+        dbk = jnp.zeros((1, PAIR), jnp.float32)
+        dbv = jnp.zeros((1, PAIR), jnp.float32)
+        for j in range(SEQ // PAIR):
+            rows = slice(j * PAIR, (j + 1) * PAIR)
+            left, right = slice(2 * j * PAIR, (2 * j + 1) * PAIR), slice((2 * j + 1) * PAIR, (2 * j + 2) * PAIR)
+            d_key = jnp.where(first, dk_acc[:, left], dk_acc[:, right]).T.astype(jnp.bfloat16).astype(jnp.float32)
+            d_key = turn_back(d_key, cos_ref[rows, :], sina_ref[rows, :], sinb_ref[rows, :])
+            dbk = dbk + jnp.sum(d_key, axis=0, keepdims=True)
+            dqkv_ref[rows, lanes(WIDTH + pair * PAIR)] = d_key.astype(jnp.bfloat16)
+            d_value = jnp.where(first, dv_acc[:, left], dv_acc[:, right]).T.astype(jnp.bfloat16)
+            dbv = dbv + jnp.sum(d_value.astype(jnp.float32), axis=0, keepdims=True)
+            dqkv_ref[rows, lanes(2 * WIDTH + pair * PAIR)] = d_value
+        dqkvb_ref[:, lanes(WIDTH + pair * PAIR)] = dbk
+        dqkvb_ref[:, lanes(2 * WIDTH + pair * PAIR)] = dbv
+
+    for k in range(3):
+        qkv_load(k).wait()
+        part = dot_t(dqkv_ref[:, k * WIDTH:(k + 1) * WIDTH], wqkv_v[k % 2])
+        if k == 0:
+            dn1[...] = part
+            qkv_load(2).start()
+        else:
+            dn1[...] += part
+
+    for ref in (dg1_ref, db1_ref, dg2_ref, db2_ref):
+        ref[...] = jnp.zeros_like(ref)
+
+    @pl.loop(0, SEQ // LN_ROWS)
+    def _(r):
+        rows = pl.ds(pl.multiple_of(r * LN_ROWS, LN_ROWS), LN_ROWS)
+        scaled, inverse = normalised(h_ref[rows, :].astype(jnp.float32))
+        d1 = dn1[rows, :].astype(jnp.bfloat16).astype(jnp.float32)
+        d2 = dn2[rows, :].astype(jnp.bfloat16).astype(jnp.float32)
+        dg1_ref[...] += jnp.sum(d1 * scaled, axis=0, keepdims=True)
+        db1_ref[...] += jnp.sum(d1, axis=0, keepdims=True)
+        dg2_ref[...] += jnp.sum(d2 * scaled, axis=0, keepdims=True)
+        db2_ref[...] += jnp.sum(d2, axis=0, keepdims=True)
+        d_scaled = d1 * g1_ref[...] + d2 * g2_ref[...]
+        d_h = inverse * (d_scaled - jnp.mean(d_scaled, axis=1, keepdims=True)
+                         - scaled * jnp.mean(d_scaled * scaled, axis=1, keepdims=True))
+        dh_ref[rows, :] = (dout_ref[rows, :].astype(jnp.float32) + d_h).astype(jnp.bfloat16)
+
+
+def backward_layer(d_out, hidden, weights, vectors, tables, qkv, pre):
+    up_weight, down_weight, qkv_weight, out_weight = weights
+    g1, g2 = vectors[0].reshape(1, -1), vectors[2].reshape(1, -1)
+    bf16, f32 = jnp.bfloat16, jnp.float32
+    shapes = [((SEQ, WIDTH), bf16), ((SEQ, HIDDEN), bf16), ((SEQ, 3 * WIDTH), bf16)] + [((1, WIDTH), f32)] * 4
+    shapes += [((1, 3 * WIDTH), f32), ((1, HIDDEN), f32), ((1, WIDTH), f32)]
+    return pl.pallas_call(
+        backward_kernel,
+        out_shape=[jax.ShapeDtypeStruct(s, d) for s, d in shapes],
+        in_specs=[IN_VMEM] * 8 + [ANY] * 5,
+        out_specs=[IN_VMEM] * 10,
+        scratch_shapes=[pltpu.VMEM((2, WIDTH, WIDTH), bf16), pltpu.VMEM((WIDTH, WIDTH), bf16), pltpu.VMEM((2, WIDTH, TILE), bf16),
+                        pltpu.VMEM((2, TILE, WIDTH), bf16), pltpu.VMEM((2, SEQ, TILE), f32), pltpu.VMEM((SEQ, WIDTH), f32),
+                        pltpu.VMEM((SEQ, WIDTH), f32), pltpu.VMEM((SEQ, WIDTH), bf16), pltpu.VMEM((PAIR, 2 * SEQ), f32),
+                        pltpu.VMEM((PAIR, 2 * SEQ), f32), pltpu.SemaphoreType.DMA((2, 3)), pltpu.SemaphoreType.DMA,
+                        pltpu.SemaphoreType.DMA((2,))],
+        compiler_params=pltpu.CompilerParams(vmem_limit_bytes=VMEM_LIMIT),
+        cost_estimate=pl.CostEstimate(flops=13 * 10**9, bytes_accessed=45 * 10**6, transcendentals=6 * 10**6),
+        name='backward_layer',
+    )(d_out, hidden, g1, g2, *tables, qkv, pre, qkv_weight, out_weight, up_weight, down_weight)
+
+
 def product(einsum_form, first_op, second_op):
     return jnp.einsum(einsum_form, first_op, second_op, preferred_element_type=jnp.float32)
 
 
-def rope_tables(seq_len, rot_dim):
+def rope_tables(seq_len, head_dim):
+    rot_dim = head_dim // 4
     inv_freq = 1.0 / (10000.0 ** (jnp.arange(0, rot_dim, 2, dtype=jnp.float32) / rot_dim))
     angles = jnp.arange(seq_len, dtype=jnp.float32)[:, None] * inv_freq[None, :]
-    angles = jnp.concatenate([angles, angles], axis=-1)
-    return jnp.cos(angles), jnp.sin(angles)
-
-
-def norm_pair(hidden32, gain_attn, bias_attn, gain_mlp, bias_mlp):
-    center = hidden32 - jnp.mean(hidden32, axis=-1, keepdims=True)
-    scaled = center * lax.rsqrt(jnp.mean(center * center, axis=-1, keepdims=True) + EPSILON)
-    return ((scaled * gain_attn + bias_attn).astype(jnp.bfloat16),
-            (scaled * gain_mlp + bias_mlp).astype(jnp.bfloat16))
-
-
-def rotary_split(qkv_all, cos_tab, sin_tab):
-    head_dim = qkv_all.shape[-1] // 3
-    rot_dim = head_dim // 4
-    half_dim = rot_dim // 2
-    cos_b = cos_tab[:, None, :]
-    sin_b = sin_tab[:, None, :]
-
-    def rotate_vec(vectors):
-        rot_part = vectors[..., :rot_dim]
-        turned = jnp.concatenate([-rot_part[..., half_dim:], rot_part[..., :half_dim]], axis=-1)
-        return jnp.concatenate([rot_part * cos_b + turned * sin_b, vectors[..., rot_dim:]], axis=-1)
-
-    query_rot = rotate_vec(qkv_all[..., :head_dim]).astype(jnp.bfloat16)
-    key_rot = rotate_vec(qkv_all[..., head_dim:2 * head_dim]).astype(jnp.bfloat16)
-    return query_rot, key_rot, qkv_all[..., 2 * head_dim:].astype(jnp.bfloat16)
-
-
-def gelu_bf16(pre_act):
-    return jax.nn.gelu(pre_act, approximate=False).astype(jnp.bfloat16)
-
-
-def layer_forward(hidden, weights, vectors, cos_tab, sin_tab):
-    up_weight, down_weight, qkv_weight, out_weight = weights
-    ln1_gain, ln1_bias, ln2_gain, ln2_bias, qkv_bias, out_bias, up_bias, down_bias = vectors
-    seq_len, d_model = hidden.shape
-    num_heads = 16
-    head_dim = d_model // num_heads
-    hidden32 = hidden.astype(jnp.float32)
-    (normed_attn, normed_mlp), norm_pull = jax.vjp(norm_pair, hidden32, ln1_gain, ln1_bias, ln2_gain, ln2_bias)
-    qkv_all = (product('sd,de->se', normed_attn, qkv_weight) + qkv_bias).reshape(seq_len, num_heads, 3 * head_dim)
-    (query_rot, key_rot, values), rotary_pull = jax.vjp(
-        functools.partial(rotary_split, cos_tab=cos_tab, sin_tab=sin_tab), qkv_all)
-    scores = product('qhd,khd->hqk', query_rot, key_rot) * head_dim ** -0.5
-    causal = lax.broadcasted_iota(jnp.int32, (seq_len, seq_len), 0) >= lax.broadcasted_iota(jnp.int32, (seq_len, seq_len), 1)
-    attn_probs = jax.nn.softmax(jnp.where(causal, scores, -1e30), axis=-1)
-    probs_bf = attn_probs.astype(jnp.bfloat16)
-    context = product('hqk,khd->qhd', probs_bf, values).astype(jnp.bfloat16).reshape(seq_len, d_model)
-    attn_out = product('qe,ed->qd', context, out_weight) + out_bias
-    pre_act = product('sd,df->sf', normed_mlp, up_weight) + up_bias
-    mlp_act, gelu_pull = jax.vjp(gelu_bf16, pre_act)
-    mlp_out = product('sf,fd->sd', mlp_act, down_weight) + down_bias
-    layer_out = (hidden32 + attn_out + mlp_out).astype(jnp.bfloat16)
-    saved_state = (norm_pull, normed_attn, normed_mlp, rotary_pull, query_rot, key_rot, values,
-                   attn_probs, probs_bf, context, gelu_pull, mlp_act)
-    return layer_out, saved_state
-
-
-def layer_backward(d_out, weights, saved_state, with_partner, half_of):
-    up_weight, down_weight, qkv_weight, out_weight = weights
-    (norm_pull, normed_attn, normed_mlp, rotary_pull, query_rot, key_rot, values,
-     attn_probs, probs_bf, context, gelu_pull, mlp_act) = saved_state
-    seq_len, d_model = d_out.shape
-    num_heads = 16
-    head_dim = d_model // num_heads
-    d_out32 = d_out.astype(jnp.float32)
-    out_sum_grad = jnp.sum(d_out32, axis=0)
-
-    def both(left, right):
-        mine, other = half_of(right)
-        return left, mine, with_partner(other)
-
-    d_act = product('sd,fd->sf', d_out, down_weight).astype(jnp.bfloat16)
-    (d_pre,) = gelu_pull(d_act)
-    up_bias_grad = jnp.sum(d_pre, axis=0)
-    d_pre_bf = d_pre.astype(jnp.bfloat16)
-    d_normed_mlp = product('sf,df->sd', d_pre_bf, up_weight).astype(jnp.bfloat16)
-    d_context = product('qd,ed->qe', d_out, out_weight).astype(jnp.bfloat16).reshape(seq_len, num_heads, head_dim)
-    d_probs = product('qhd,khd->hqk', d_context, values).astype(jnp.bfloat16).astype(jnp.float32)
-    d_values = product('hqk,qhd->khd', probs_bf, d_context).astype(jnp.bfloat16)
-    d_scores = (attn_probs * (d_probs - jnp.sum(d_probs * attn_probs, axis=-1, keepdims=True)) * head_dim ** -0.5).astype(jnp.bfloat16)
-    d_query = product('hqk,khd->qhd', d_scores, key_rot).astype(jnp.bfloat16)
-    d_key = product('hqk,qhd->khd', d_scores, query_rot).astype(jnp.bfloat16)
-    (d_qkv,) = rotary_pull((d_query, d_key, d_values))
-    d_qkv = d_qkv.reshape(seq_len, 3 * d_model)
-    qkv_bias_grad = jnp.sum(d_qkv, axis=0)
-    d_qkv_bf = d_qkv.astype(jnp.bfloat16)
-    d_normed_attn = product('se,de->sd', d_qkv_bf, qkv_weight).astype(jnp.bfloat16)
-    d_hidden32, gain1_grad, bias1_grad, gain2_grad, bias2_grad = norm_pull((d_normed_attn, d_normed_mlp))
-    d_hidden = (d_out32 + d_hidden32).astype(jnp.bfloat16)
-
-    def weight_grad(left, left_other, right):
-        mine, other = half_of(right)
-        rows = jnp.concatenate([left, left_other], axis=0)
-        cols = jnp.concatenate([mine, with_partner(other)], axis=0)
-        return product('sd,se->de', rows, cols)
-
-    out_half = half_of(d_out)
-    d_out_cols = jnp.concatenate([out_half[0], with_partner(out_half[1])], axis=0)
-
-    def on_d_out(left):
-        return product('sd,se->de', jnp.concatenate([left, with_partner(left)], axis=0), d_out_cols)
-
-    down_grad = on_d_out(mlp_act)
-    out_grad = on_d_out(context)
-    up_grad = weight_grad(normed_mlp, with_partner(normed_mlp), d_pre_bf)
-    qkv_grad = weight_grad(normed_attn, with_partner(normed_attn), d_qkv_bf)
-    vectors = (gain1_grad, bias1_grad, gain2_grad, bias2_grad, qkv_bias_grad, out_sum_grad, up_bias_grad, out_sum_grad)
-    return d_hidden, (up_grad, down_grad, qkv_grad, out_grad), vectors
+    cos, sin = jnp.cos(angles), jnp.sin(angles)
+    zero = jnp.zeros_like(sin)
+    rest = jnp.zeros((seq_len, head_dim - rot_dim), jnp.float32)
+    tables = ([cos, cos, rest + 1.0], [-sin, zero, rest], [zero, sin, rest])
+    return [jnp.tile(jnp.concatenate(table, axis=1), (1, 2)) for table in tables]
 
 
 def pack_vectors(vectors):
     packed = jnp.concatenate(vectors, axis=-1)
     return jnp.pad(packed, ((0, 0), (0, 128 - packed.shape[-1])))
+
+
+def heads_last(tensor):
+    lead = tensor.shape[:-2]
+    return jnp.swapaxes(tensor.reshape(lead + (16, 3, 64)), -3, -2).reshape(lead + (3072,))
+
+
+def heads_first(tensor):
+    lead = tensor.shape[:-1]
+    return jnp.swapaxes(tensor.reshape(lead + (3, 16, 64)), -3, -2).reshape(lead + (16, 192))
 
 
 def solution(mesh):
@@ -464,42 +667,60 @@
                     ln2_gain, ln2_bias, up_weight, up_bias, down_weight, down_bias):
         num_layers = ln1_gain.shape[0]
         core = lax.rem(lax.axis_index('local'), 2)
-        cos_tab, sin_tab = rope_tables(x.shape[1], qkv_weight.shape[3] // 12)
+        tables = rope_tables(x.shape[1], qkv_weight.shape[3] // 3)
 
         def half_of(tensor):
             width = tensor.shape[1] // 2
             return (lax.dynamic_slice_in_dim(tensor, core * width, width, 1),
                     lax.dynamic_slice_in_dim(tensor, (1 - core) * width, width, 1))
 
+        def columns(tensor):
+            mine, other = half_of(tensor)
+            return jnp.concatenate([mine, with_partner(other)], axis=0)
+
+        def rows(tensor):
+            return jnp.concatenate([tensor, with_partner(tensor)], axis=0)
+
         small = (ln1_gain, ln1_bias, ln2_gain, ln2_bias, qkv_bias, out_bias, up_bias, down_bias)
         widths = [tensor.shape[1] for tensor in small]
         small_tile = jnp.pad(pack_vectors(small), ((0, 8 - num_layers), (0, 0)))
-        layers, small_full = gather_all(up_weight, down_weight, qkv_weight.reshape(num_layers, -1, 3 * x.shape[2]),
-                                        out_weight, small_tile)
+        layers, small_full = gather_all(up_weight, down_weight, heads_last(qkv_weight), out_weight, small_tile)
 
         def vectors_of(layer):
             found, start = [], 0
             for width in widths:
                 found.append(small_full[:, layer, start:start + width].reshape(-1).astype(jnp.float32))
                 start += width
+            found[4] = heads_last(found[4].reshape(16, 192))
             return found
 
         hidden = x[0]
-        states = []
+        inputs, states, vectors = [], [], []
         for layer in range(num_layers):
-            hidden, state = layer_forward(hidden, layers[layer], vectors_of(layer), cos_tab, sin_tab)
+            inputs.append(hidden)
+            vectors.append(vectors_of(layer))
+            hidden, *state = forward_layer(hidden, layers[layer], vectors[layer], tables)
             states.append(state)
         y_out = hidden
         d_hidden = y_cot[0]
         sums = [None] * num_layers
         for layer in reversed(range(num_layers)):
-            d_hidden, weight_grads, vector_grads = layer_backward(d_hidden, layers[layer], states[layer], with_partner, half_of)
-            rows = pack_vectors([grad.reshape(128, -1) for grad in vector_grads])
-            tiles = jnp.pad(rows.reshape(64, 2, 128), ((0, 0), (0, 6), (0, 0)))
-            sums[layer] = reduce_all(*weight_grads, tiles)
-
-        def joined(arr, shape):
-            return jnp.stack([s[arr].swapaxes(0, 1).reshape(shape[1:]).astype(jnp.bfloat16) for s in sums])
+            normed_attn, normed_mlp, qkv, context, act, pre = states[layer]
+            d_out = d_hidden
+            d_hidden, d_pre, d_qkv, dg1, db1, dg2, db2, dqkvb, dupb, dsum = backward_layer(
+                d_out, inputs[layer], layers[layer], vectors[layer], tables, qkv, pre)
+            d_out_cols = columns(d_out)
+            down_grad = product('sd,se->de', rows(act), d_out_cols)
+            out_grad = product('sd,se->de', rows(context), d_out_cols)
+            up_grad = product('sd,se->de', rows(normed_mlp), columns(d_pre))
+            qkv_grad = product('sd,se->de', rows(normed_attn), columns(d_qkv))
+            vector_grads = (dg1, db1, dg2, db2, heads_first(dqkvb), dsum, dupb, dsum)
+            packed = pack_vectors([grad.reshape(128, -1) for grad in vector_grads])
+            tiles = jnp.pad(packed.reshape(64, 2, 128), ((0, 0), (0, 6), (0, 0)))
+            sums[layer] = reduce_all(up_grad, down_grad, qkv_grad, out_grad, tiles)
+
+        def joined(arr):
+            return jnp.stack([jnp.concatenate([s[arr][0], s[arr][1]], axis=1) for s in sums]).astype(jnp.bfloat16)
 
         small_sums = jnp.stack([lax.dynamic_index_in_dim(s[4], core, 0, False) for s in sums]).astype(jnp.bfloat16)
         small_grads, start = [], 0
@@ -507,8 +728,8 @@
             small_grads.append(small_sums[:, start:start + width])
             start += width
         g1, b1, g2, b2, qb, ob, ub, db = small_grads
-        return (y_out[None], d_hidden[None], g1, b1, joined(2, qkv_weight.shape), qb, joined(3, out_weight.shape), ob,
-                g2, b2, joined(0, up_weight.shape), ub, joined(1, down_weight.shape), db)
+        return (y_out[None], d_hidden[None], g1, b1, heads_first(joined(2)), qb, joined(3), ob,
+                g2, b2, joined(0), ub, joined(1), db)
 
     return jax.shard_map(device_step, mesh=mesh,
                          in_specs=(act_spec, act_spec) + (param_spec,) * 12,

time: 712 us -> 606 us (0.85)
  matrix products: 281 us -> 51.2 us
  Pallas kernels: 322 us -> 473 us
  other arithmetic: 38.2 us -> 19.5 us
    dot_general x34 -> x8, matrix products: 267 us -> 51.2 us  [product(): jnp.einsum(einsum_form, first_op, second_op, preferred_element_type=jnp.f...]
    pallas_call x0 -> x4, Pallas kernels: none -> 149 us  [the longest x2 83.5 us: backward_layer(): pl.pallas_call(backward_kernel, out_shape=[jax.ShapeDtypeStruct(s, d) for...]
    sub x2 -> x0, matrix products: 14.3 us -> none  [layer_forward(): attn_probs = jax.nn.softmax(jnp.where(causal, scores, -1e+30), axis=-1)]
    pallas_call x0 -> x14, other arithmetic: none -> 13.4 us  [backward_layer(): pl.pallas_call(backward_kernel, out_shape=[jax.ShapeDtypeStruct(s, d) for...]
    add x2 -> x3, local copies, waits for them, and re-layouts: 12.2 us -> 1.38 us  [the longest x2 1.38 us: forward_layer(): out_bias + down_bias]
  transfers between devices with their start and end apart: 14 -> 14, of which waited for: 0 -> 0; matrix products, arithmetic and copies ran while one was open for 49% -> 13% of each run, Pallas kernels for 31% -> 24%
where the time goes in v2:
time: 606 us; the launch traced here: 600 us
  Pallas kernels  473 us (78%)
  matrix products  51.2 us (8%)
  local copies, waits for them, and re-layouts  50.8 us (8%)
  other arithmetic  19.5 us (3%)
    pallas_call x2, Pallas kernels, reduce_all(): pl.pallas_call(reduce_kernel, out_shape=shapes, in_specs=[ANY] * 5, out_s...  206 us
    pallas_call x1, Pallas kernels, gather_all(): pl.pallas_call(functools.partial(gather_kernel, n_layers), out_shape=shap...  118 us
    pallas_call x2, Pallas kernels, backward_layer(): pl.pallas_call(backward_kernel, out_shape=[jax.ShapeDtypeStruct(s, d) for...  83.5 us
    pallas_call x2, Pallas kernels, forward_layer(): pl.pallas_call(forward_kernel, out_shape=[jax.ShapeDtypeStruct(s, d) for...  65.9 us
    dot_general x8, matrix products, product(): jnp.einsum(einsum_form, first_op, second_op, preferred_element_type=jnp.f...  51.2 us
    pallas_call x14, other arithmetic, backward_layer(): pl.pallas_call(backward_kernel, out_shape=[jax.ShapeDtypeStruct(s, d) for...  13.4 us
    dynamic_slice x6, local copies, waits for them, and re-layouts, half_of(): lax.dynamic_slice_in_dim(tensor, core * width, width, 1)  13.2 us
  transfers between devices with their start and end apart: 14, of which 0 were waited for; matrix products, arithmetic and copies ran while one was open for 13% of the time, Pallas kernels for 24%

profile of v2, /device:TPU:1, one launch (start us, length us, event | category | flops | bytes accessed | tf_op | source)
XLA Modules:
  0.0 600.2 jit_solution(13382294299726876162)
XLA Ops:
  0.6 1.0 reshape.369
  4.0 117.7 %gather_weights.1 = (bf16[4,4,4,2,8,4096]{5,4,3,2,1,0:T(8,128)(2,1)}, bf16[4,4,4,2,32,1024]{5,4,3,2,1,0:T(8,128)(2,1)}, bf16[4,4,4,2,8,3072]{5,4,3,2,1,0:T(8,128...) custom-call(bf16[2,8,4096]{2,1,0:T(8,128)(2,1)} %refs_0_.1, ...), custom_call_target="tpu_custom_call" | custom-call | tf_op jit(solution)/shard_map/gather_weights/pallas_call | solution.py:152
  121.7 4.3 fusion.58
  126.0 1.2 fusion.57
  127.2 1.2 fusion.59
  141.4 32.8 %forward_layer.2 = (bf16[384,1024]{1,0:T(8,128)(2,1)}, bf16[384,1024]{1,0:T(8,128)(2,1)}, bf16[384,1024]{1,0:T(8,128)(2,1)}, bf16[384,3072]{1,0:T(8,128)(2,1)}, ...) custom-call(bf16[384,1024]{1,0:T(8,128)(2,1)} %bitcast.159, ...), custom_call_target="tpu_custom_call" | custom-call | flops 10000000000 | bytes 45000000 | tf_op jit(solution)/shard_map/forward_layer/pallas_call | solution.py:462
  174.2 33.1 %forward_layer.3 = (bf16[384,1024]{1,0:T(8,128)(2,1)}, bf16[384,1024]{1,0:T(8,128)(2,1)}, bf16[384,1024]{1,0:T(8,128)(2,1)}, bf16[384,3072]{1,0:T(8,128)(2,1)}, ...) custom-call(bf16[384,1024]{1,0:T(8,128)(2,1)} %get-tuple-element.72.h_ref, ...), custom_call_target="tpu_custom_call" | custom-call | flops 10000000000 | bytes 45000000 | tf_op jit(solution)/shard_map/forward_layer/pallas_call | solution.py:462
  207.3 41.9 %backward_layer.2 = (bf16[384,1024]{1,0:T(8,128)(2,1)}, bf16[384,4096]{1,0:T(8,128)(2,1)}, bf16[384,3072]{1,0:T(8,128)(2,1)}, f32[1,1024]{1,0:T(1,128)}, f32[1,1...) custom-call(bf16[384,1024]{1,0:T(8,128)(2,1)} %bitcast.136, ...), custom_call_target="tpu_custom_call" | custom-call | flops 12999999488 | bytes 45000000 | tf_op jit(solution)/shard_map/backward_layer/pallas_call | solution.py:610
  249.3 1.9 constant_dynamic-slice_fusion.9
  253.1 41.6 %backward_layer.3 = (bf16[384,1024]{1,0:T(8,128)(2,1)}, bf16[384,4096]{1,0:T(8,128)(2,1)}, bf16[384,3072]{1,0:T(8,128)(2,1)}, f32[1,1024]{1,0:T(1,128)}, f32[1,1...) custom-call(bf16[384,1024]{1,0:T(8,128)(2,1)} %get-tuple-element.80., ...), custom_call_target="tpu_custom_call" | custom-call | flops 12999999488 | bytes 45000000 | tf_op jit(solution)/shard_map/backward_layer/pallas_call | solution.py:610
  295.3 3.1 constant_dynamic-slice_fusion.7
  299.2 3.5 constant_dynamic-slice_fusion.11
  304.0 1.6 constant_dynamic-slice_fusion.2
  312.4 1.7 concatenate.105
  316.5 1.4 reduce.48
  318.0 1.3 reduce.42
  319.4 1.3 reduce.43
  320.8 1.3 reduce.44
  322.3 1.3 reduce.45
  324.3 1.3 reduce.47
  325.8 1.7 concatenate.113
  329.4 2.2 constant_dynamic-slice_fusion.4
  332.0 3.8 fusion.30
  335.8 3.8 fusion.40
  339.7 7.2 %fusion.16 = f32[1024,1536]{1,0:T(8,128)} fusion(bf16[384,1536]{1,0:T(8,128)(2,1)} %collective-permute-done.5, bf16[384,1536]{1,0:T(8,128)(2,1)S(1)} %copy-done.1, bf16[384,1024]{1,0:T(8,128)(2,1)} %collective-permute-done.4, bf16[384,1024]{1,0:T(8,128)(2,1)} %get-tuple-element.87), kind=kOutput, calls=%fused_computation.16 | convolution fusion | flops 2423783424 | bytes 10223616 | tf_op jit(solution)/shard_map/sd,se->de/dot_general | solution.py:627
  347.3 7.2 %fusion.20 = f32[1024,1536]{1,0:T(8,128)} fusion(bf16[384,1536]{1,0:T(8,128)(2,1)} %collective-permute-done.12, bf16[384,1536]{1,0:T(8,128)(2,1)S(1)} %copy-done.2, bf16[384,1024]{1,0:T(8,128)(2,1)} %collective-permute-done.11, bf16[384,1024]{1,0:T(8,128)(2,1)} %get-tuple-element.101), kind=kOutput, calls=%fused_computation.20 | convolution fusion | flops 2423783424 | bytes 10223616 | tf_op jit(solution)/shard_map/sd,se->de/dot_general | solution.py:627
  354.5 6.2 %fusion.8 = f32[1024,2048]{1,0:T(8,128)} fusion(bf16[384,2048]{1,0:T(8,128)(2,1)S(1)} %collective-permute-done.1, bf16[384,2048]{1,0:T(8,128)(2,1)S(1)} %get-tuple-element.120, bf16[384,1024]{1,0:T(8,128)(2,1)S(1)} %copy-done.7, bf16[384,1024]{1,0:T(8,128)(2,1)S(1)} %copy-done.5), kind=kOutput, calls=%fused_computation.8 | convolution fusion | flops 3230662656 | bytes 13107200 | tf_op jit(solution)/shard_map/sd,se->de/dot_general | solution.py:627
  360.7 5.7 fusion.12
  366.4 8.7 %fusion = f32[4096,512]{1,0:T(8,128)} fusion(bf16[384,4096]{1,0:T(8,128)(2,1)} %collective-permute-done.2, bf16[384,4096]{1,0:T(8,128)(2,1)S(1)} %copy-done.24, bf16[384,512]{1,0:T(8,128)(2,1)S(1)} %copy-done.26, bf16[384,512]{1,0:T(8,128)(2,1)S(1)} %copy-done.10), kind=kOutput, calls=%fused_computation | convolution fusion | flops 3235381248 | bytes 15466496 | tf_op jit(solution)/shard_map/sd,se->de/dot_general | solution.py:627
  375.1 102.4 %reduce_gradients.2 = (f32[2,8,2048]{2,1,0:T(8,128)}, f32[2,32,512]{2,1,0:T(8,128)}, f32[2,8,1536]{2,1,0:T(8,128)}, f32[2,8,512]{2,1,0:T(8,128)}, f32[8,128]{1,0:T(8,128)}) custom-call(f32[4,4,4,16,2048]{4,3,2,1,0:T(8,128)} %bitcast.120, f32[4,4,4,64,512]{4,3,2,1,0:T(8,128)} %bitcast.121, f32[4,4,4,16,1536]{4,3,2,1,0:T(8,128)} %bitcast.124, ...), custom_call_target="tpu_custom_call" | custom-call | tf_op jit(solution)/shard_map/reduce_gradients/pallas_call | solution.py:318
  478.2 8.6 %fusion.4 = f32[4096,512]{1,0:T(8,128)} fusion(bf16[384,4096]{1,0:T(8,128)(2,1)} %collective-permute-done.9, bf16[384,4096]{1,0:T(8,128)(2,1)S(1)} %copy-done.23, bf16[384,512]{1,0:T(8,128)(2,1)S(1)} %copy-done.28, bf16[384,512]{1,0:T(8,128)(2,1)S(1)} %copy-done.9), kind=kOutput, calls=%fused_computation.4 | convolution fusion | flops 3235381248 | bytes 15466496 | tf_op jit(solution)/shard_map/sd,se->de/dot_general | solution.py:627
  486.8 103.5 %reduce_gradients.3 = (f32[2,8,2048]{2,1,0:T(8,128)}, f32[2,32,512]{2,1,0:T(8,128)}, f32[2,8,1536]{2,1,0:T(8,128)}, f32[2,8,512]{2,1,0:T(8,128)}, f32[8,128]{1,0:T(8,128)}) custom-call(f32[4,4,4,16,2048]{4,3,2,1,0:T(8,128)} %bitcast.119, f32[4,4,4,64,512]{4,3,2,1,0:T(8,128)} %bitcast.122, f32[4,4,4,16,1536]{4,3,2,1,0:T(8,128)} %bitcast.123, ...), custom_call_target="tpu_custom_call" | custom-call | tf_op jit(solution)/shard_map/reduce_gradients/pallas_call | solution.py:318
  (200 shorter events, 42.7 us)
Async XLA Ops:
  207.3 44.4 %copy-start.4 = (bf16[384,1024]{1,0:T(8,128)(2,1)S(1)}, bf16[384,1024]{1,0:T(8,128)(2,1)}, u32[]{:S(2)}) copy-start(bf16[384,1024]{1,0:T(8,128)(2,1)} %get-tuple-element.84) | copy-start | bytes 2359300
  207.3 44.9 %copy-start.8 = (bf16[1,384,1024]{2,1,0:T(8,128)(2,1)S(1)}, bf16[1,384,1024]{2,1,0:T(8,128)(2,1)}, u32[]{:S(2)}) copy-start(bf16[1,384,1024]{2,1,0:T(8,128)(2,1)} %param.15) | copy-start | bytes 2359300
  251.2 43.5 %collective-permute-start.3 = (bf16[384,512]{1,0:T(8,128)(2,1)S(1)}, bf16[384,512]{1,0:T(8,128)(2,1)S(1)}, u32[]{:S(2)}, u32[]{:S(2)}) collective-permute-start(bf16[384,512]{1,0:T(8,128)(2,1)S(1)} %get-tuple-element.129), channel_id=1, source_target_pairs={{0,1},{1,0},{2,3},{3,2},{4,5},{5,4},{6,7},{7,6},{8,9},{9,8},{10,11... | collective-permute-start | bytes 1179656 | tf_op jit(solution)/shard_map/ppermute | solution.py:664
  251.2 47.4 %collective-permute-start.6 = (bf16[384,1024]{1,0:T(8,128)(2,1)}, bf16[384,1024]{1,0:T(8,128)(2,1)}, u32[]{:S(2)}, u32[]{:S(2)}) collective-permute-start(bf16[384,1024]{1,0:T(8,128)(2,1)} %get-tuple-element.89), channel_id=1, source_target_pairs={{0,1},{1,0},{2,3},{3,2},{4,5},{5,4},{6,7},{7,6},{8,9},{9,8},{10,11... | collective-permute-start | bytes 2359304 | tf_op jit(solution)/shard_map/ppermute | solution.py:664
  251.7 47.3 %collective-permute-start.4 = (bf16[384,1024]{1,0:T(8,128)(2,1)}, bf16[384,1024]{1,0:T(8,128)(2,1)}, u32[]{:S(2)}, u32[]{:S(2)}) collective-permute-start(bf16[384,1024]{1,0:T(8,128)(2,1)} %get-tuple-element.87), channel_id=1, source_target_pairs={{0,1},{1,0},{2,3},{3,2},{4,5},{5,4},{6,7},{7,6},{8,9},{9,8},{10,11... | collective-permute-start | bytes 2359304 | tf_op jit(solution)/shard_map/ppermute | solution.py:664
  251.7 51.0 %collective-permute-start = (bf16[384,1024]{1,0:T(8,128)(2,1)S(1)}, bf16[384,1024]{1,0:T(8,128)(2,1)S(1)}, u32[]{:S(2)}, u32[]{:S(2)}) collective-permute-start(bf16[384,1024]{1,0:T(8,128)(2,1)S(1)} %copy-done.4), channel_id=1, source_target_pairs={{0,1},{1,0},{2,3},{3,2},{4,5},{5,4},{6,7},{7,6},{8,9},{9,8},{10,11... | collective-permute-start | bytes 2359304 | tf_op jit(solution)/shard_map/ppermute | solution.py:664
  253.0 45.4 %collective-permute-start.10 = (bf16[384,512]{1,0:T(8,128)(2,1)S(1)}, bf16[384,512]{1,0:T(8,128)(2,1)S(1)}, u32[]{:S(2)}, u32[]{:S(2)}) collective-permute-start(bf16[384,512]{1,0:T(8,128)(2,1)S(1)} %get-tuple-element.131), channel_id=1, source_target_pairs={{0,1},{1,0},{2,3},{3,2},{4,5},{5,4},{6,7},{7,6},{8,9},{9,8},{10,11... | collective-permute-start | bytes 1179656 | tf_op jit(solution)/shard_map/ppermute | solution.py:664
  294.7 10.9 %collective-permute-start.13 = (bf16[384,1024]{1,0:T(8,128)(2,1)}, bf16[384,1024]{1,0:T(8,128)(2,1)}, u32[]{:S(2)}, u32[]{:S(2)}) collective-permute-start(bf16[384,1024]{1,0:T(8,128)(2,1)} %get-tuple-element.103), channel_id=1, source_target_pairs={{0,1},{1,0},{2,3},{3,2},{4,5},{5,4},{6,7},{7,6},{8,9},{9,8},{10,11... | collective-permute-start | bytes 2359304 | tf_op jit(solution)/shard_map/ppermute | solution.py:664
  298.4 33.1 %collective-permute-start.5 = (bf16[384,1536]{1,0:T(8,128)(2,1)}, bf16[384,1536]{1,0:T(8,128)(2,1)}, u32[]{:S(2)}, u32[]{:S(2)}) collective-permute-start(bf16[384,1536]{1,0:T(8,128)(2,1)} %get-tuple-element.125), channel_id=1, source_target_pairs={{0,1},{1,0},{2,3},{3,2},{4,5},{5,4},{6,7},{7,6},{8,9},{9,8},{10,11... | collective-permute-start | bytes 3538952 | tf_op jit(solution)/shard_map/ppermute | solution.py:664
  298.6 30.4 %collective-permute-start.11 = (bf16[384,1024]{1,0:T(8,128)(2,1)}, bf16[384,1024]{1,0:T(8,128)(2,1)}, u32[]{:S(2)}, u32[]{:S(2)}) collective-permute-start(bf16[384,1024]{1,0:T(8,128)(2,1)} %get-tuple-element.101), channel_id=1, source_target_pairs={{0,1},{1,0},{2,3},{3,2},{4,5},{5,4},{6,7},{7,6},{8,9},{9,8},{10,11... | collective-permute-start | bytes 2359304 | tf_op jit(solution)/shard_map/ppermute | solution.py:664
  299.0 67.4 %collective-permute-start.2 = (bf16[384,4096]{1,0:T(8,128)(2,1)}, bf16[384,4096]{1,0:T(8,128)(2,1)}, u32[]{:S(2)}, u32[]{:S(2)}) collective-permute-start(bf16[384,4096]{1,0:T(8,128)(2,1)} %get-tuple-element.86), channel_id=1, source_target_pairs={{0,1},{1,0},{2,3},{3,2},{4,5},{5,4},{6,7},{7,6},{8,9},{9,8},{10,11... | collective-permute-start | bytes 9437192 | tf_op jit(solution)/shard_map/ppermute | solution.py:664
  299.2 4.8 copy-start
  303.6 50.9 %collective-permute-start.1 = (bf16[384,2048]{1,0:T(8,128)(2,1)}, bf16[384,2048]{1,0:T(8,128)(2,1)S(1)}, u32[]{:S(2)}, u32[]{:S(2)}) collective-permute-start(bf16[384,2048]{1,0:T(8,128)(2,1)} %get-tuple-element.121), channel_id=1, source_target_pairs={{0,1},{1,0},{2,3},{3,2},{4,5},{5,4},{6,7},{7,6},{8,9},{9,8},{10,11... | collective-permute-start | bytes 4718600 | tf_op jit(solution)/shard_map/ppermute | solution.py:664
  304.0 4.7 copy-start.21
  304.0 5.5 copy-start.20
  304.0 6.3 %copy-start.19 = (f32[1,1024]{1,0:T(1,128)S(1)}, f32[1,1024]{1,0:T(1,128)}, u32[]{:S(2)}) copy-start(f32[1,1024]{1,0:T(1,128)} %get-tuple-element.93) | copy-start | bytes 12292
  304.0 7.6 %copy-start.18 = (f32[1,1024]{1,0:T(1,128)S(1)}, f32[1,1024]{1,0:T(1,128)}, u32[]{:S(2)}) copy-start(f32[1,1024]{1,0:T(1,128)} %get-tuple-element.95) | copy-start | bytes 12292
  304.0 11.6 %copy-start.16 = (f32[1,3072]{1,0:T(1,128)S(1)}, f32[1,3072]{1,0:T(1,128)}, u32[]{:S(2)}) copy-start(f32[1,3072]{1,0:T(1,128)} %get-tuple-element.108) | copy-start | bytes 36868
  305.6 41.3 %collective-permute-start.12 = (bf16[384,1536]{1,0:T(8,128)(2,1)}, bf16[384,1536]{1,0:T(8,128)(2,1)}, u32[]{:S(2)}, u32[]{:S(2)}) collective-permute-start(bf16[384,1536]{1,0:T(8,128)(2,1)} %get-tuple-element.127), channel_id=1, source_target_pairs={{0,1},{1,0},{2,3},{3,2},{4,5},{5,4},{6,7},{7,6},{8,9},{9,8},{10,11... | collective-permute-start | bytes 3538952 | tf_op jit(solution)/shard_map/ppermute | solution.py:664
  329.0 149.2 %collective-permute-start.9 = (bf16[384,4096]{1,0:T(8,128)(2,1)}, bf16[384,4096]{1,0:T(8,128)(2,1)}, u32[]{:S(2)}, u32[]{:S(2)}) collective-permute-start(bf16[384,4096]{1,0:T(8,128)(2,1)} %get-tuple-element.100), channel_id=1, source_target_pairs={{0,1},{1,0},{2,3},{3,2},{4,5},{5,4},{6,7},{7,6},{8,9},{9,8},{10,11... | collective-permute-start | bytes 9437192 | tf_op jit(solution)/shard_map/ppermute | solution.py:664
  331.6 29.1 %collective-permute-start.8 = (bf16[384,2048]{1,0:T(8,128)(2,1)S(1)}, bf16[384,2048]{1,0:T(8,128)(2,1)S(1)}, u32[]{:S(2)}, u32[]{:S(2)}) collective-permute-start(bf16[384,2048]{1,0:T(8,128)(2,1)S(1)} %get-tuple-element.123), channel_id=1, source_target_pairs={{0,1},{1,0},{2,3},{3,2},{4,5},{5,4},{6,7},{7,6},{8,9},{9,8},{10,11... | collective-permute-start | bytes 4718600 | tf_op jit(solution)/shard_map/ppermute | solution.py:664
  339.7 7.3 %copy-start.3 = (bf16[384,1024]{1,0:T(8,128)(2,1)S(1)}, bf16[384,1024]{1,0:T(8,128)(2,1)}, u32[]{:S(2)}) copy-start(bf16[384,1024]{1,0:T(8,128)(2,1)} %get-tuple-element.98) | copy-start | bytes 2359300
  339.7 7.6 %copy-start.2 = (bf16[384,1536]{1,0:T(8,128)(2,1)S(1)}, bf16[384,1536]{1,0:T(8,128)(2,1)}, u32[]{:S(2)}) copy-start(bf16[384,1536]{1,0:T(8,128)(2,1)} %get-tuple-element.126) | copy-start | bytes 3538948
  346.9 13.8 %collective-permute-start.7 = (bf16[384,1024]{1,0:T(8,128)(2,1)S(1)}, bf16[384,1024]{1,0:T(8,128)(2,1)S(1)}, u32[]{:S(2)}, u32[]{:S(2)}) collective-permute-start(bf16[384,1024]{1,0:T(8,128)(2,1)S(1)} %copy-done.3), channel_id=1, source_target_pairs={{0,1},{1,0},{2,3},{3,2},{4,5},{5,4},{6,7},{7,6},{8,9},{9,8},{10,11... | collective-permute-start | bytes 2359304 | tf_op jit(solution)/shard_map/ppermute | solution.py:664
  347.3 7.2 %copy-start.5 = (bf16[384,1024]{1,0:T(8,128)(2,1)S(1)}, bf16[384,1024]{1,0:T(8,128)(2,1)}, u32[]{:S(2)}) copy-start(bf16[384,1024]{1,0:T(8,128)(2,1)} %get-tuple-element.84) | copy-start | bytes 2359300
  347.3 7.2 %copy-start.7 = (bf16[384,1024]{1,0:T(8,128)(2,1)S(1)}, bf16[384,1024]{1,0:T(8,128)(2,1)}, u32[]{:S(2)}) copy-start(bf16[384,1024]{1,0:T(8,128)(2,1)} %copy-done.6) | copy-start | bytes 2359300
  360.7 5.7 copy-start.24
  375.1 103.1 %copy-start.23 = (bf16[384,4096]{1,0:T(8,128)(2,1)S(1)}, bf16[384,4096]{1,0:T(8,128)(2,1)}, u32[]{:S(2)}) copy-start(bf16[384,4096]{1,0:T(8,128)(2,1)} %get-tuple-element.100) | copy-start | bytes 9437188
  486.8 106.0 %copy-start.12 = (f32[2,32,512]{2,1,0:T(8,128)S(1)}, f32[2,32,512]{2,1,0:T(8,128)}, u32[]{:S(2)}) copy-start(f32[2,32,512]{2,1,0:T(8,128)} %get-tuple-element.118) | copy-start | bytes 393220
  486.8 107.0 %copy-start.11 = (f32[2,8,2048]{2,1,0:T(8,128)S(1)}, f32[2,8,2048]{2,1,0:T(8,128)}, u32[]{:S(2)}) copy-start(f32[2,8,2048]{2,1,0:T(8,128)} %get-tuple-element.116) | copy-start | bytes 393220
  486.8 107.9 %copy-start.14 = (f32[2,8,512]{2,1,0:T(8,128)S(1)}, f32[2,8,512]{2,1,0:T(8,128)}, u32[]{:S(2)}) copy-start(f32[2,8,512]{2,1,0:T(8,128)} %get-tuple-element.114) | copy-start | bytes 98308
  486.8 108.7 %copy-start.13 = (f32[2,8,1536]{2,1,0:T(8,128)S(1)}, f32[2,8,1536]{2,1,0:T(8,128)}, u32[]{:S(2)}) copy-start(f32[2,8,1536]{2,1,0:T(8,128)} %get-tuple-element.112) | copy-start | bytes 294916
  (11 other events, 31.6 us)

commit v3 on v2

--- a/solution.py
+++ b/solution.py
@@ -1,6 +1,7 @@
 import functools
 import jax
 import jax.numpy as jnp
+import numpy as np
 from jax import lax
 from jax.experimental import pallas as pl
 from jax.experimental.pallas import tpu as pltpu
@@ -49,121 +50,360 @@
     pl.semaphore_wait(barrier, 7)
 
 
+SHARES = (8, 8, 8, 8, 24, 8, 32, 8)
+SIZES = tuple(128 * share for share in SHARES)
+OFFSETS = tuple(sum(SIZES[:k]) for k in range(len(SIZES)))
+N_VEC = sum(SIZES)
+
+
+SEQ, WIDTH, HIDDEN, TILE = 384, 1024, 4096, 512
+N_TILES = HIDDEN // TILE
+PAIR = 128
+INV_SQRT2 = 0.7071067811865476
+INV_SQRT2PI = 0.3989422804014327
+SCALE = 0.125
+
+
+def dot(a, b):
+    return lax.dot_general(a, b, (((1,), (0,)), ((), ())), preferred_element_type=jnp.float32)
+
+
+def dot_t(a, b):
+    return lax.dot_general(a, b, (((1,), (1,)), ((), ())), preferred_element_type=jnp.float32)
+
+
+def lanes(start, width=PAIR):
+    return pl.ds(pl.multiple_of(start, PAIR), width)
+
+
+def turn(x, cos, sin_a, sin_b):
+    return x * cos + pltpu.roll(x, PAIR - 8, 1) * sin_a + pltpu.roll(x, 8, 1) * sin_b
+
+
+def turn_back(d, cos, sin_a, sin_b):
+    return d * cos + pltpu.roll(d * sin_a, 8, 1) + pltpu.roll(d * sin_b, PAIR - 8, 1)
+
+
+def split_heads(x):
+    first = lax.broadcasted_iota(jnp.int32, (PAIR, PAIR), 1) < PAIR // 2
+    rows = []
+    for j in range(SEQ // PAIR):
+        block = x[j * PAIR:(j + 1) * PAIR]
+        rows += [jnp.where(first, block, jnp.zeros_like(block)), jnp.where(first, jnp.zeros_like(block), block)]
+    return jnp.concatenate(rows, axis=0)
+
+
+def probabilities(q_block, keys, i):
+    scores = dot_t(q_block, keys)
+    causal = (lax.broadcasted_iota(jnp.int32, (PAIR, PAIR), 0) >= lax.broadcasted_iota(jnp.int32, (PAIR, PAIR), 1))
+    probs = [None] * (2 * i + 2)
+    for head in range(2):
+        chunks = [scores[:, (2 * j + head) * PAIR:(2 * j + head + 1) * PAIR] * SCALE for j in range(i + 1)]
+        chunks[i] = jnp.where(causal, chunks[i], -1e30)
+        top = chunks[0]
+        for chunk in chunks[1:]:
+            top = jnp.maximum(top, chunk)
+        top = jnp.max(top, axis=1, keepdims=True)
+        chunks = [jnp.exp(chunk - top) for chunk in chunks]
+        total = chunks[0]
+        for chunk in chunks[1:]:
+            total = total + chunk
+        inverse = 1.0 / jnp.sum(total, axis=1, keepdims=True)
+        for j in range(i + 1):
+            probs[2 * j + head] = chunks[j] * inverse
+    return probs
+
+
+def normalised(h):
+    center = h - jnp.mean(h, axis=1, keepdims=True)
+    inverse = lax.rsqrt(jnp.mean(center * center, axis=1, keepdims=True) + EPSILON)
+    return center * inverse, inverse
+
+
+LN_ROWS = 64
+
+
 GATHER_PARTS = ((0, 0, 2048, 0), (0, 2048, 2048, 1), (1, 0, 512, 2), (1, 512, 512, 3),
                 (2, 0, 2048, 4), (2, 2048, 1024, 5), (3, 0, 1024, 5))
 
 
-def gather_kernel(n_layers, *refs):
-    shards, refs = refs[:5], refs[5:]
+class Gather:
+    def __init__(self, chip, core, parts, sems):
+        self.chip, self.core, self.parts = chip, core, parts
+        self.send_sem, self.recv_sem, self.pass_send, self.pass_recv = sems
+        self.copies, self.passed, self.first, self.second = [], {}, {}, {}
+
+    def copy(self, sems, n, slot, where, own, device):
+        full, shard, cols, _ = self.parts[n]
+        box = full.at[where[0], where[1], where[2], self.core, :, cols]
+        copy = pltpu.make_async_remote_copy(
+            src_ref=shard if own else box, dst_ref=box, send_sem=sems[0].at[n, slot], recv_sem=sems[1].at[n, slot],
+            device_id=device, device_id_type=MESH)
+        copy.start()
+        self.copies.append(copy)
+        return copy
+
+    def reach(self, n, slot, where, own, axis, mask):
+        return self.copy((self.send_sem, self.recv_sem), n, slot, where, own, device_at(moved(self.chip, axis, mask), self.core))
+
+    def pass_on(self, n, slot, where, own=False):
+        copy = self.copy((self.pass_send, self.pass_recv), n, slot, where, own, device_at(self.chip, 1 - self.core))
+        self.passed.setdefault(n, []).append(copy)
+
+    def span(self, n, stage, mask):
+        order, masks = colour_plan(self.parts[n][3])
+        where = list(self.chip)
+        for axis in order[:stage]:
+            where[axis] = pl.ds(0, 4)
+        where[order[stage]] = flip(self.chip[order[stage]], mask) if mask else self.chip[order[stage]]
+        return where, order[stage], masks
+
+    def start(self, ns, stage):
+        for turn in range(2):
+            for n in ns:
+                where, axis, masks = self.span(n, stage, 0)
+                self.first[n, turn] = self.reach(n, 3 * stage + turn, where, stage == 0, axis, masks[turn])
+
+    def pass_own(self, ns):
+        for n in ns:
+            self.pass_on(n, 9, list(self.chip), True)
+
+    def middle(self, ns, stage):
+        for n in ns:
+            order, masks = colour_plan(self.parts[n][3])
+            self.first[n, 0].wait_recv()
+            where, axis, masks = self.span(n, stage, masks[0])
+            self.second[n] = self.reach(n, 3 * stage + 2, where, False, axis, masks[1])
+            self.pass_on(n, 3 * stage, where)
+
+    def late(self, ns, stage):
+        for n in ns:
+            _, masks = colour_plan(self.parts[n][3])
+            self.first[n, 1].wait_recv()
+            self.pass_on(n, 3 * stage + 1, self.span(n, stage, masks[1])[0])
+
+    def end(self, ns, stage):
+        for n in ns:
+            self.second[n].wait_recv()
+            self.pass_on(n, 3 * stage + 2, self.span(n, stage, 2)[0])
+
+    def arrived(self, ns):
+        for n in ns:
+            for copy in self.passed.pop(n):
+                copy.wait_recv()
+
+
+def unpack_vectors(small_v, layer, sel_shard, sel_lane, vec_ref):
+    tiles = small_v[...].astype(jnp.float32).reshape((PAIR,) + small_v.shape[-2:])
+    held = jnp.where(lax.broadcasted_iota(jnp.int32, tiles.shape, 1) == layer, tiles, 0.0)
+    held = jnp.sum(held, axis=1).astype(jnp.bfloat16)
+    for k in range(N_VEC // WIDTH):
+        cols = slice(k * WIDTH, (k + 1) * WIDTH)
+        number = lax.broadcasted_iota(jnp.int32, (PAIR, WIDTH), 0)
+        pick = (number == sel_lane[:, cols]).astype(jnp.float32).astype(jnp.bfloat16)
+        spread = jnp.where(number == sel_shard[:, cols], dot(held, pick), 0.0)
+        vec_ref[layer:layer + 1, cols] = jnp.sum(spread, axis=0, keepdims=True)
+
+
+def forward_kernel(n_layers, *refs):
+    x_ref, cos_ref, sina_ref, sinb_ref, sel_shard, sel_lane = refs[:6]
+    shards, refs = refs[6:11], refs[11:]
     fulls, refs = refs[:4 * n_layers + 1], refs[4 * n_layers + 1:]
-    send_sem, recv_sem, pass_send, pass_recv, own_sem = refs
+    vec_ref, refs = refs[0], refs[1:]
+    saved, refs = refs[:7 * n_layers], refs[7 * n_layers:]
+    (wup_v, wdown_v, wqkv_v, wout_v, small_v, acc, pre_v, n1_v, n2_v, qkv_v, ctx_v, act_v, y_v,
+     send_sem, recv_sem, pass_send, pass_recv, own_sem, load_sem, save_sem, share_send, share_recv) = refs
     chip, core = place()
     entry_barrier(chip, core)
-    every = pl.ds(0, 4)
-    copies = []
 
     parts = []
     for layer in range(n_layers):
         for arr, col, width, colour in GATHER_PARTS:
-            parts.append((fulls[4 * layer + arr], shards[arr].at[layer, :, pl.ds(col, width)], col, width, colour))
-    parts.append((fulls[-1], shards[4], 0, 128, 4))
-
-    def box(part, where):
-        full, _, col, width, _ = part
-        return full.at[where[0], where[1], where[2], core, :, pl.ds(col, width)]
-
-    def reach(n, slot, where, target, own):
-        part = parts[n]
-        copy = pltpu.make_async_remote_copy(
-            src_ref=part[1] if own else box(part, where), dst_ref=box(part, where),
-            send_sem=send_sem.at[n, slot], recv_sem=recv_sem.at[n, slot],
-            device_id=device_at(target, core), device_id_type=MESH)
-        copy.start()
-        copies.append(copy)
-        return copy
-
-    def pass_on(n, slot, where, own):
-        part = parts[n]
-        copy = pltpu.make_async_remote_copy(
-            src_ref=part[1] if own else box(part, where), dst_ref=box(part, where),
-            send_sem=pass_send.at[n, slot], recv_sem=pass_recv.at[n, slot],
-            device_id=device_at(chip, 1 - core), device_id_type=MESH)
-        copy.start()
-        copies.append(copy)
-        return copy
-
-    def span(order, stage, value):
-        where = list(chip)
-        for axis in order[:stage]:
-            where[axis] = every
-        where[order[stage]] = value
-        return where
+            cols = pl.ds(col, width)
+            parts.append((fulls[4 * layer + arr], shards[arr].at[layer, :, cols], cols, colour))
+    parts.append((fulls[-1], shards[4], pl.ds(0, PAIR), 4))
+    gather = Gather(chip, core, parts, (send_sem, recv_sem, pass_send, pass_recv))
+    per = len(GATHER_PARTS)
+    now = list(range(per)) + [len(parts) - 1]
+    nxt = list(range(per, 2 * per))
 
     own = []
     for layer in range(n_layers):
         for arr in range(4):
-            own.append(pltpu.make_async_copy(
-                shards[arr].at[layer], fulls[4 * layer + arr].at[chip[0], chip[1], chip[2], core], own_sem.at[4 * layer + arr]))
-    own.append(pltpu.make_async_copy(shards[4], fulls[-1].at[chip[0], chip[1], chip[2], core], own_sem.at[4 * n_layers]))
+            own.append((shards[arr].at[layer], fulls[4 * layer + arr]))
+    own.append((shards[4], fulls[-1]))
+    own = [pltpu.make_async_copy(src, dst.at[chip[0], chip[1], chip[2], core], own_sem.at[k]) for k, (src, dst) in enumerate(own)]
+    gather.start(now, 0)
     for copy in own:
         copy.start()
-
-    passed = []
-    first = {}
+    gather.start(nxt, 0)
+    gather.pass_own(now + nxt)
+    for copy in own:
+        copy.wait()
     for stage in range(3):
-        for turn in range(2):
-            for n, part in enumerate(parts):
-                order, masks = colour_plan(part[4])
-                axis = order[stage]
-                target = moved(chip, axis, masks[turn])
-                first[n, turn] = reach(n, 3 * stage + turn, span(order, stage, chip[axis]), target, stage == 0)
-        if stage == 0:
-            for n, part in enumerate(parts):
-                passed.append(pass_on(n, 9, list(chip), True))
-            for copy in own:
+        gather.middle(now, stage)
+        if stage:
+            gather.start(nxt, stage)
+        gather.late(now, stage)
+        gather.end(now, stage)
+        if stage < 2:
+            gather.start(now, stage + 1)
+            gather.middle(nxt, stage)
+            gather.late(nxt, stage)
+            gather.end(nxt, stage)
+
+    saves, shares = [], []
+
+    def save(src, dst):
+        copy = pltpu.make_async_copy(src, dst, save_sem.at[len(saves)])
+        copy.start()
+        saves.append(copy)
+
+    def share(src, dst):
+        save(src, dst.at[core])
+        copy = pltpu.make_async_remote_copy(
+            src_ref=src, dst_ref=dst.at[core], send_sem=share_send.at[len(shares)], recv_sem=share_recv.at[len(shares)],
+            device_id=device_at(chip, 1 - core), device_id_type=MESH)
+        copy.start()
+        shares.append(copy)
+
+    def load(layer, arr, k, width=None):
+        full, held = fulls[4 * layer + arr].at[:, :, :, :, :, :], (wup_v, wdown_v, wqkv_v, wout_v)[arr]
+        if width:
+            cols = pl.ds(k * width, width)
+            full, held = full.at[:, :, :, :, :, cols], held.at[:, :, :, :, :, cols]
+        copy = pltpu.make_async_copy(full, held, load_sem.at[arr, k])
+        copy.start()
+        return copy
+
+    def matrix(held, cols=slice(None)):
+        return held[:, :, :, :, :, cols].reshape((-1, held.shape[-1] if cols == slice(None) else cols.stop - cols.start))
+
+    def have(layer, arrs):
+        gather.arrived([n for n in (now if layer == 0 else nxt) if n in gather.passed
+                        and (parts[n][0] is fulls[-1] or any(parts[n][0] is fulls[4 * layer + arr] for arr in arrs))])
+
+    for layer in range(n_layers):
+        h_ref = y_v if layer else x_ref
+        y_hbm, n1_hbm, n2_hbm, ctx_hbm, act_hbm, qkv_hbm, pre_hbm = saved[7 * layer:7 * layer + 7]
+        have(layer, [2])
+        loads = [load(layer, 2, k, TILE) for k in range(6)]
+        if layer == 0:
+            fetch = pltpu.make_async_copy(fulls[-1], small_v, load_sem.at[3, 1])
+            fetch.start()
+            fetch.wait()
+            for k in range(n_layers):
+                unpack_vectors(small_v, k, sel_shard, sel_lane, vec_ref)
+        else:
+            for copy in saves:
                 copy.wait()
-        second = {}
-        for n, part in enumerate(parts):
-            order, masks = colour_plan(part[4])
-            axis = order[stage]
-            first[n, 0].wait_recv()
-            where = span(order, stage, flip(chip[axis], masks[0]))
-            second[n] = reach(n, 3 * stage + 2, where, moved(chip, axis, masks[1]), False)
-            passed.append(pass_on(n, 3 * stage, where, False))
-        for n, part in enumerate(parts):
-            order, masks = colour_plan(part[4])
-            axis = order[stage]
-            first[n, 1].wait_recv()
-            passed.append(pass_on(n, 3 * stage + 1, span(order, stage, flip(chip[axis], masks[1])), False))
-            second[n].wait_recv()
-            passed.append(pass_on(n, 3 * stage + 2, span(order, stage, flip(chip[axis], 2)), False))
-    for copy in passed:
+            for copy in shares:
+                copy.wait_send()
+            saves.clear()
+
+        def vector(k, cols=slice(None)):
+            at = OFFSETS[k]
+            return vec_ref[layer:layer + 1, at:at + SIZES[k]] if cols == slice(None) else vec_ref[layer:layer + 1, at + cols.start:at + cols.stop]
+
+        for r in range(SEQ // LN_ROWS):
+            rows = slice(r * LN_ROWS, (r + 1) * LN_ROWS)
+            scaled, _ = normalised(h_ref[rows, :].astype(jnp.float32))
+            n1_v[rows, :] = (scaled * vector(0) + vector(1)).astype(jnp.bfloat16)
+            n2_v[rows, :] = (scaled * vector(2) + vector(3)).astype(jnp.bfloat16)
+        share(n1_v, n1_hbm)
+        share(n2_v, n2_hbm)
+        for k in range(6):
+            cols = slice(k * TILE, (k + 1) * TILE)
+            loads[k].wait()
+            x = dot(n1_v[...], matrix(wqkv_v, cols)) + vector(4, cols)
+            for c in range(TILE // PAIR):
+                block = x[:, c * PAIR:(c + 1) * PAIR]
+                if k < 4:
+                    block = turn(block, cos_ref[...], sina_ref[...], sinb_ref[...])
+                at = k * TILE + c * PAIR
+                qkv_v[:, at:at + PAIR] = block.astype(jnp.bfloat16)
+        save(qkv_v, qkv_hbm)
+        have(layer, [0, 1, 3])
+        out_load = load(layer, 3, 0)
+        up_loads = [load(layer, 0, t, TILE) for t in range(N_TILES)]
+        down_load = load(layer, 1, 0)
+
+        @pl.loop(0, WIDTH // PAIR)
+        def _(pair):
+            keys = split_heads(qkv_v[:, lanes(WIDTH + pair * PAIR)])
+            values = split_heads(qkv_v[:, lanes(2 * WIDTH + pair * PAIR)])
+            for i in range(SEQ // PAIR):
+                n = (i + 1) * 2 * PAIR
+                rows = slice(i * PAIR, (i + 1) * PAIR)
+                probs = probabilities(qkv_v[rows, lanes(pair * PAIR)], keys[:n], i)
+                probs = jnp.concatenate([p.astype(jnp.bfloat16) for p in probs], axis=1)
+                ctx_v[rows, lanes(pair * PAIR)] = dot(probs, values[:n]).astype(jnp.bfloat16)
+
+        share(ctx_v, ctx_hbm)
+        if layer == 0:
+            gather.middle(nxt, 2)
+        out_load.wait()
+        for cols in (slice(0, TILE), slice(TILE, WIDTH)):
+            acc[:, cols] = (h_ref[:, cols].astype(jnp.float32) + dot(ctx_v[...], matrix(wout_v, cols))
+                            + (vector(5, cols) + vector(7, cols)))
+        down_load.wait()
+        for t in range(N_TILES):
+            cols = slice(t * TILE, (t + 1) * TILE)
+            up_loads[t].wait()
+            pre = dot(n2_v[...], matrix(wup_v, cols)) + vector(6, cols)
+            pre_v[t] = pre
+            act_v[:, cols] = (0.5 * pre * (1.0 + lax.erf(pre * INV_SQRT2))).astype(jnp.bfloat16)
+            acc[...] += dot(act_v[:, cols], wdown_v[t // 2, t % 2 * 2:t % 2 * 2 + 2].reshape((TILE, WIDTH)))
+            if layer == 0 and t == N_TILES // 2:
+                gather.late(nxt, 2)
+        save(pre_v, pre_hbm)
+        share(act_v, act_hbm)
+        y_v[...] = acc[...].astype(jnp.bfloat16)
+        save(y_v, y_hbm)
+        if layer == 0:
+            gather.end(nxt, 2)
+    for copy in saves:
+        copy.wait()
+    per = len(shares) // n_layers
+    for copy in shares:
         copy.wait_recv()
-    for copy in copies:
+    for copy in shares[-per:]:
         copy.wait_send()
-
-
-def gather_all(up, down, qkv, out, small):
-    n_layers = up.shape[0]
-    shards = (up, down, qkv, out, small)
+    for copy in gather.copies:
+        copy.wait_send()
+
+
+def forward(x, shards, small_tile, tables, sel_shard, sel_lane):
+    n_layers = shards[0].shape[0]
+    bf16, f32 = jnp.bfloat16, jnp.float32
+    chips = (4, 4, 4, 2)
+    full = [(chips + tensor.shape[1:], bf16) for tensor in shards]
+    shapes = full * n_layers + [(chips + small_tile.shape, bf16), ((n_layers, N_VEC), f32)]
+    kept = [((SEQ, WIDTH), bf16)] + [((2, SEQ, width), bf16) for width in (WIDTH, WIDTH, WIDTH, HIDDEN)]
+    kept += [((SEQ, 3 * WIDTH), bf16), ((N_TILES, SEQ, TILE), f32)]
+    shapes += kept * n_layers
     n_parts = len(GATHER_PARTS) * n_layers + 1
-    shapes = [jax.ShapeDtypeStruct((4, 4, 4, 2) + tensor.shape[1:], tensor.dtype) for _ in range(n_layers) for tensor in shards[:4]]
-    shapes.append(jax.ShapeDtypeStruct((4, 4, 4, 2) + small.shape, small.dtype))
-    fulls = pl.pallas_call(
-        functools.partial(gather_kernel, n_layers),
-        out_shape=shapes,
-        in_specs=[IN_VMEM] * 5,
-        out_specs=[ANY] * len(shapes),
-        scratch_shapes=[pltpu.SemaphoreType.DMA((n_parts, 9)), pltpu.SemaphoreType.DMA((n_parts, 9)),
-                        pltpu.SemaphoreType.DMA((n_parts, 10)), pltpu.SemaphoreType.DMA((n_parts, 10)),
-                        pltpu.SemaphoreType.DMA((4 * n_layers + 1,))],
-        compiler_params=pltpu.CompilerParams(collective_id=0, has_side_effects=True),
-        name='gather_weights',
-    )(*shards)
-    layers = []
-    for layer in range(n_layers):
-        layers.append([full.reshape((-1, full.shape[-1])) for full in fulls[4 * layer:4 * layer + 4]])
-    return layers, fulls[-1].reshape((128,) + small.shape)
+    dma = pltpu.SemaphoreType.DMA
+    scratch = [pltpu.VMEM(*s) for s in full]
+    scratch += [pltpu.VMEM(chips + small_tile.shape, bf16), pltpu.VMEM((SEQ, WIDTH), f32), pltpu.VMEM((N_TILES, SEQ, TILE), f32)]
+    scratch += [pltpu.VMEM((SEQ, width), bf16) for width in (WIDTH, WIDTH, 3 * WIDTH, WIDTH, HIDDEN, WIDTH)]
+    scratch += [dma((n_parts, 9)), dma((n_parts, 9)), dma((n_parts, 10)), dma((n_parts, 10)), dma((4 * n_layers + 1,)),
+                dma((4, N_TILES)), dma((7,)), dma((4 * n_layers,)), dma((4 * n_layers,))]
+    out_specs = [ANY] * len(shapes)
+    out_specs[4 * n_layers + 1] = IN_VMEM
+    outs = pl.pallas_call(
+        functools.partial(forward_kernel, n_layers),
+        out_shape=[jax.ShapeDtypeStruct(s, d) for s, d in shapes],
+        in_specs=[IN_VMEM] * 11,
+        out_specs=out_specs,
+        scratch_shapes=scratch,
+        compiler_params=pltpu.CompilerParams(collective_id=0, has_side_effects=True, vmem_limit_bytes=VMEM_LIMIT),
+        cost_estimate=pl.CostEstimate(flops=20 * 10**9, bytes_accessed=10**8, transcendentals=10**7),
+        name='forward_layers',
+    )(x, *tables, sel_shard, sel_lane, *shards, small_tile)
+    weights = [[t.reshape((-1, t.shape[-1])) for t in outs[4 * k:4 * k + 4]] for k in range(n_layers)]
+    outs = outs[4 * n_layers + 1:]
+    return weights, outs[0], [outs[1 + 7 * k:8 + 7 * k] for k in range(n_layers)]
 
 
 REDUCE_PARTS = ((0, 0, 1024, 0), (0, 1024, 1024, 1), (1, 0, 256, 2), (1, 256, 256, 3),
@@ -325,152 +565,6 @@
         compiler_params=pltpu.CompilerParams(collective_id=1, has_side_effects=True, vmem_limit_bytes=VMEM_LIMIT),
         name='reduce_gradients',
     )(*grads)
-
-
-SEQ, WIDTH, HIDDEN, TILE = 384, 1024, 4096, 512
-N_TILES = HIDDEN // TILE
-PAIR = 128
-INV_SQRT2 = 0.7071067811865476
-INV_SQRT2PI = 0.3989422804014327
-SCALE = 0.125
-
-
-def dot(a, b):
-    return lax.dot_general(a, b, (((1,), (0,)), ((), ())), preferred_element_type=jnp.float32)
-
-
-def dot_t(a, b):
-    return lax.dot_general(a, b, (((1,), (1,)), ((), ())), preferred_element_type=jnp.float32)
-
-
-def lanes(start, width=PAIR):
-    return pl.ds(pl.multiple_of(start, PAIR), width)
-
-
-def turn(x, cos, sin_a, sin_b):
-    return x * cos + pltpu.roll(x, PAIR - 8, 1) * sin_a + pltpu.roll(x, 8, 1) * sin_b
-
-
-def turn_back(d, cos, sin_a, sin_b):
-    return d * cos + pltpu.roll(d * sin_a, 8, 1) + pltpu.roll(d * sin_b, PAIR - 8, 1)
-
-
-def split_heads(x):
-    first = lax.broadcasted_iota(jnp.int32, (PAIR, PAIR), 1) < PAIR // 2
-    rows = []
-    for j in range(SEQ // PAIR):
-        block = x[j * PAIR:(j + 1) * PAIR]
-        rows += [jnp.where(first, block, jnp.zeros_like(block)), jnp.where(first, jnp.zeros_like(block), block)]
-    return jnp.concatenate(rows, axis=0)
-
-
-def probabilities(q_block, keys, i):
-    scores = dot_t(q_block, keys)
-    causal = (lax.broadcasted_iota(jnp.int32, (PAIR, PAIR), 0) >= lax.broadcasted_iota(jnp.int32, (PAIR, PAIR), 1))
-    probs = [None] * (2 * i + 2)
-    for head in range(2):
-        chunks = [scores[:, (2 * j + head) * PAIR:(2 * j + head + 1) * PAIR] * SCALE for j in range(i + 1)]
-        chunks[i] = jnp.where(causal, chunks[i], -1e30)
-        top = chunks[0]
-        for chunk in chunks[1:]:
-            top = jnp.maximum(top, chunk)
-        top = jnp.max(top, axis=1, keepdims=True)
-        chunks = [jnp.exp(chunk - top) for chunk in chunks]
-        total = chunks[0]
-        for chunk in chunks[1:]:
-            total = total + chunk
-        inverse = 1.0 / jnp.sum(total, axis=1, keepdims=True)
-        for j in range(i + 1):
-            probs[2 * j + head] = chunks[j] * inverse
-    return probs
-
-
-def normalised(h):
-    center = h - jnp.mean(h, axis=1, keepdims=True)
-    inverse = lax.rsqrt(jnp.mean(center * center, axis=1, keepdims=True) + EPSILON)
-    return center * inverse, inverse
-
-
-LN_ROWS = 64
-
-
-def forward_kernel(h_ref, g1_ref, b1_ref, g2_ref, b2_ref, qkvb_ref, outb_ref, upb_ref, cos_ref, sina_ref, sinb_ref,
-                   wqkv, wout, wup, wdown, y_ref, n1_ref, n2_ref, qkv_ref, ctx_ref, act_ref, pre_hbm,
-                   wqkv_v, wout_v, wup_v, wdown_v, acc, pre_v, sems, pre_sems):
-    loads = []
-    for k in range(6):
-        loads.append(pltpu.make_async_copy(wqkv.at[:, pl.ds(k * 512, 512)], wqkv_v.at[:, pl.ds(k * 512, 512)], sems.at[k]))
-    loads.append(pltpu.make_async_copy(wout, wout_v, sems.at[6]))
-    for t in range(N_TILES):
-        loads.append(pltpu.make_async_copy(wup.at[:, pl.ds(t * TILE, TILE)], wup_v.at[:, pl.ds(t * TILE, TILE)], sems.at[7 + 2 * t]))
-        loads.append(pltpu.make_async_copy(wdown.at[pl.ds(t * TILE, TILE)], wdown_v.at[pl.ds(t * TILE, TILE)], sems.at[8 + 2 * t]))
-    for load in loads:
-        load.start()
-
-    @pl.loop(0, SEQ // LN_ROWS)
-    def _(r):
-        rows = pl.ds(pl.multiple_of(r * LN_ROWS, LN_ROWS), LN_ROWS)
-        scaled, _ = normalised(h_ref[rows, :].astype(jnp.float32))
-        n1_ref[rows, :] = (scaled * g1_ref[...] + b1_ref[...]).astype(jnp.bfloat16)
-        n2_ref[rows, :] = (scaled * g2_ref[...] + b2_ref[...]).astype(jnp.bfloat16)
-
-    for k in range(6):
-        loads[k].wait()
-        x = dot(n1_ref[...], wqkv_v[:, k * 512:(k + 1) * 512]) + qkvb_ref[:, k * 512:(k + 1) * 512]
-        for c in range(4):
-            block = x[:, c * PAIR:(c + 1) * PAIR]
-            if k < 4:
-                block = turn(block, cos_ref[...], sina_ref[...], sinb_ref[...])
-            qkv_ref[:, k * 512 + c * PAIR:k * 512 + (c + 1) * PAIR] = block.astype(jnp.bfloat16)
-
-    @pl.loop(0, WIDTH // PAIR)
-    def _(pair):
-        keys = split_heads(qkv_ref[:, lanes(WIDTH + pair * PAIR)])
-        values = split_heads(qkv_ref[:, lanes(2 * WIDTH + pair * PAIR)])
-        for i in range(SEQ // PAIR):
-            n = (i + 1) * 2 * PAIR
-            probs = probabilities(qkv_ref[i * PAIR:(i + 1) * PAIR, lanes(pair * PAIR)], keys[:n], i)
-            probs = jnp.concatenate([p.astype(jnp.bfloat16) for p in probs], axis=1)
-            ctx_ref[i * PAIR:(i + 1) * PAIR, lanes(pair * PAIR)] = dot(probs, values[:n]).astype(jnp.bfloat16)
-
-    loads[6].wait()
-    for k in range(2):
-        cols = slice(k * 512, (k + 1) * 512)
-        acc[:, cols] = h_ref[:, cols].astype(jnp.float32) + dot(ctx_ref[...], wout_v[:, cols]) + outb_ref[:, cols]
-    stores = []
-    for t in range(N_TILES):
-        cols = slice(t * TILE, (t + 1) * TILE)
-        loads[7 + 2 * t].wait()
-        pre = dot(n2_ref[...], wup_v[:, cols]) + upb_ref[:, cols]
-        pre_v[t] = pre
-        stores.append(pltpu.make_async_copy(pre_v.at[t], pre_hbm.at[t], pre_sems.at[t]))
-        stores[-1].start()
-        act_ref[:, cols] = (0.5 * pre * (1.0 + lax.erf(pre * INV_SQRT2))).astype(jnp.bfloat16)
-        loads[8 + 2 * t].wait()
-        acc[...] += dot(act_ref[:, cols], wdown_v[cols, :])
-    y_ref[...] = acc[...].astype(jnp.bfloat16)
-    for store in stores:
-        store.wait()
-
-
-def forward_layer(hidden, weights, vectors, tables):
-    up_weight, down_weight, qkv_weight, out_weight = weights
-    g1, b1, g2, b2, qkv_bias, out_bias, up_bias, down_bias = [v.reshape(1, -1) for v in vectors]
-    bf16 = jnp.bfloat16
-    shapes = [((SEQ, WIDTH), bf16)] * 3 + [((SEQ, 3 * WIDTH), bf16), ((SEQ, WIDTH), bf16), ((SEQ, HIDDEN), bf16),
-                                           ((N_TILES, SEQ, TILE), jnp.float32)]
-    return pl.pallas_call(
-        forward_kernel,
-        out_shape=[jax.ShapeDtypeStruct(s, d) for s, d in shapes],
-        in_specs=[IN_VMEM] * 11 + [ANY] * 4,
-        out_specs=[IN_VMEM] * 6 + [ANY],
-        scratch_shapes=[pltpu.VMEM((WIDTH, 3 * WIDTH), bf16), pltpu.VMEM((WIDTH, WIDTH), bf16), pltpu.VMEM((WIDTH, HIDDEN), bf16),
-                        pltpu.VMEM((HIDDEN, WIDTH), bf16), pltpu.VMEM((SEQ, WIDTH), jnp.float32),
-                        pltpu.VMEM((N_TILES, SEQ, TILE), jnp.float32), pltpu.SemaphoreType.DMA((23,)), pltpu.SemaphoreType.DMA((N_TILES,))],
-        compiler_params=pltpu.CompilerParams(vmem_limit_bytes=VMEM_LIMIT),
-        cost_estimate=pl.CostEstimate(flops=10 * 10**9, bytes_accessed=45 * 10**6, transcendentals=4 * 10**6),
-        name='forward_layer',
-    )(hidden, g1, b1, g2, b2, qkv_bias, out_bias + down_bias, up_bias, *tables, qkv_weight, out_weight, up_weight, down_weight)
 
 
 def backward_kernel(dout_ref, h_ref, g1_ref, g2_ref, cos_ref, sina_ref, sinb_ref, qkv_ref, pre_hbm, wqkv, wout, wup, wdown,
@@ -638,27 +732,38 @@
     return [jnp.tile(jnp.concatenate(table, axis=1), (1, 2)) for table in tables]
 
 
+def heads_last(tensor):
+    lead = tensor.shape[:-2]
+    return tensor.reshape(lead + (16, 3, 64)).swapaxes(-3, -2).reshape(lead + (3072,))
+
+
+def heads_first(tensor):
+    lead = tensor.shape[:-1]
+    return tensor.reshape(lead + (3, 16, 64)).swapaxes(-3, -2).reshape(lead + (16, 192))
+
+
+def vector_places():
+    shard, lane, start = [], [], 0
+    for k, (share, size) in enumerate(zip(SHARES, SIZES)):
+        place_of = np.arange(size)
+        if k == 4:
+            place_of = heads_last(place_of.reshape(16, 192))
+        shard.append(place_of // share)
+        lane.append(start + place_of % share)
+        start += share
+    return [jnp.asarray(np.concatenate(part)[None].astype(np.int32)) for part in (shard, lane)]
+
+
 def pack_vectors(vectors):
     packed = jnp.concatenate(vectors, axis=-1)
     return jnp.pad(packed, ((0, 0), (0, 128 - packed.shape[-1])))
-
-
-def heads_last(tensor):
-    lead = tensor.shape[:-2]
-    return jnp.swapaxes(tensor.reshape(lead + (16, 3, 64)), -3, -2).reshape(lead + (3072,))
-
-
-def heads_first(tensor):
-    lead = tensor.shape[:-1]
-    return jnp.swapaxes(tensor.reshape(lead + (3, 16, 64)), -3, -2).reshape(lead + (16, 192))
 
 
 def solution(mesh):
     shard_axes = ('node', 'local')
     act_spec = P(shard_axes)
     param_spec = P(None, shard_axes)
-    n_local = mesh.shape['local']
-    pairs = [(i, i + 1 - 2 * (i % 2)) for i in range(n_local)]
+    pairs = [(i, i + 1 - 2 * (i % 2)) for i in range(mesh.shape['local'])]
 
     def with_partner(tensor):
         return lax.ppermute(tensor, 'local', pairs)
@@ -669,47 +774,30 @@
         core = lax.rem(lax.axis_index('local'), 2)
         tables = rope_tables(x.shape[1], qkv_weight.shape[3] // 3)
 
-        def half_of(tensor):
+        def columns(tensor):
             width = tensor.shape[1] // 2
-            return (lax.dynamic_slice_in_dim(tensor, core * width, width, 1),
-                    lax.dynamic_slice_in_dim(tensor, (1 - core) * width, width, 1))
-
-        def columns(tensor):
-            mine, other = half_of(tensor)
-            return jnp.concatenate([mine, with_partner(other)], axis=0)
-
-        def rows(tensor):
-            return jnp.concatenate([tensor, with_partner(tensor)], axis=0)
+            mine = lax.dynamic_slice_in_dim(tensor, core * width, width, 1)
+            other = with_partner(lax.dynamic_slice_in_dim(tensor, (1 - core) * width, width, 1))
+            return jnp.concatenate([jnp.where(core == 0, mine, other), jnp.where(core == 0, other, mine)], axis=0)
 
         small = (ln1_gain, ln1_bias, ln2_gain, ln2_bias, qkv_bias, out_bias, up_bias, down_bias)
-        widths = [tensor.shape[1] for tensor in small]
         small_tile = jnp.pad(pack_vectors(small), ((0, 8 - num_layers), (0, 0)))
-        layers, small_full = gather_all(up_weight, down_weight, heads_last(qkv_weight), out_weight, small_tile)
-
-        def vectors_of(layer):
-            found, start = [], 0
-            for width in widths:
-                found.append(small_full[:, layer, start:start + width].reshape(-1).astype(jnp.float32))
-                start += width
-            found[4] = heads_last(found[4].reshape(16, 192))
-            return found
-
-        hidden = x[0]
-        inputs, states, vectors = [], [], []
-        for layer in range(num_layers):
-            inputs.append(hidden)
-            vectors.append(vectors_of(layer))
-            hidden, *state = forward_layer(hidden, layers[layer], vectors[layer], tables)
-            states.append(state)
-        y_out = hidden
+        weights, vectors, states = forward(x[0], (up_weight, down_weight, heads_last(qkv_weight), out_weight), small_tile,
+                                           tables, *vector_places())
+        inputs = [x[0]] + [state[0] for state in states]
         d_hidden = y_cot[0]
         sums = [None] * num_layers
         for layer in reversed(range(num_layers)):
-            normed_attn, normed_mlp, qkv, context, act, pre = states[layer]
+            _, normed_attn, normed_mlp, context, act, qkv, pre = states[layer]
             d_out = d_hidden
+            gains = [vectors[layer, OFFSETS[k]:OFFSETS[k] + SIZES[k]] for k in range(4)]
             d_hidden, d_pre, d_qkv, dg1, db1, dg2, db2, dqkvb, dupb, dsum = backward_layer(
-                d_out, inputs[layer], layers[layer], vectors[layer], tables, qkv, pre)
+                d_out, inputs[layer], weights[layer], gains, tables, qkv, pre)
             d_out_cols = columns(d_out)
+
+            def rows(tensor):
+                return tensor.reshape((-1, tensor.shape[-1]))
+
             down_grad = product('sd,se->de', rows(act), d_out_cols)
             out_grad = product('sd,se->de', rows(context), d_out_cols)
             up_grad = product('sd,se->de', rows(normed_mlp), columns(d_pre))
@@ -724,11 +812,11 @@
 
         small_sums = jnp.stack([lax.dynamic_index_in_dim(s[4], core, 0, False) for s in sums]).astype(jnp.bfloat16)
         small_grads, start = [], 0
-        for width in widths:
+        for width in SHARES:
             small_grads.append(small_sums[:, start:start + width])
             start += width
         g1, b1, g2, b2, qb, ob, ub, db = small_grads
-        return (y_out[None], d_hidden[None], g1, b1, heads_first(joined(2)), qb, joined(3), ob,
+        return (inputs[-1][None], d_hidden[None], g1, b1, heads_first(joined(2)), qb, joined(3), ob,
                 g2, b2, joined(0), ub, joined(1), db)
 
     return jax.shard_map(device_step, mesh=mesh,

time: 606 us -> 593 us (0.979)
  Pallas kernels: 473 us -> 451 us
  local copies, waits for them, and re-layouts: 50.8 us -> 65.3 us
  matrix products: 51.2 us -> 39.9 us
    dot_general x0 -> x8, local copies, waits for them, and re-layouts: none -> 32.9 us  [product(): jnp.einsum(einsum_form, first_op, second_op, preferred_element_type=jnp.f...]
    pallas_call x3 -> x1, Pallas kernels: 184 us -> 162 us  [forward(): pl.pallas_call(functools.partial(forward_kernel, n_layers), out_shape=[ja...]
    dot_general x8, matrix products: 51.2 us -> 39.9 us  [product(): jnp.einsum(einsum_form, first_op, second_op, preferred_element_type=jnp.f...]
    select_n x0 -> x6, other arithmetic: none -> 9.91 us  [columns(): jnp.where(core == 0, mine, other)]
    convert_element_type x10 -> x0, local copies, waits for them, and re-layouts: 6.89 us -> none  [vectors_of(): small_full[:, layer, start:start + width].reshape(-1).astype(jnp.float32)]
  transfers between devices with their start and end apart: 14 -> 6, of which waited for: 0 -> 0; matrix products, arithmetic and copies ran while one was open for 13% -> 18% of each run, Pallas kernels for 24% -> 24%
where the time goes in v3:
time: 593 us; the launch traced here: 585 us
  Pallas kernels  451 us (76%)
  local copies, waits for them, and re-layouts  65.3 us (11%)
  matrix products  39.9 us (7%)
  other arithmetic  24.3 us (4%)
    pallas_call x2, Pallas kernels, reduce_all(): pl.pallas_call(reduce_kernel, out_shape=shapes, in_specs=[ANY] * 5, out_s...  206 us
    pallas_call x1, Pallas kernels, forward(): pl.pallas_call(functools.partial(forward_kernel, n_layers), out_shape=[ja...  162 us
    pallas_call x2, Pallas kernels, backward_layer(): pl.pallas_call(backward_kernel, out_shape=[jax.ShapeDtypeStruct(s, d) for...  83.5 us
    dot_general x8, matrix products, product(): jnp.einsum(einsum_form, first_op, second_op, preferred_element_type=jnp.f...  39.9 us
    dot_general x8, local copies, waits for them, and re-layouts, product(): jnp.einsum(einsum_form, first_op, second_op, preferred_element_type=jnp.f...  32.9 us
  transfers between devices with their start and end apart: 6, of which 0 were waited for; matrix products, arithmetic and copies ran while one was open for 18% of the time, Pallas kernels for 24%

profile of v3, /device:TPU:1, one launch (start us, length us, event | category | flops | bytes accessed | tf_op | source)
XLA Modules:
  0.0 584.6 jit_solution(8294340781455747182)
XLA Ops:
  5.4 161.7 %forward_layers.1 = (bf16[4,4,4,2,8,4096]{5,4,3,2,1,0:T(8,128)(2,1)}, bf16[4,4,4,2,32,1024]{5,4,3,2,1,0:T(8,128)(2,1)}, bf16[4,4,4,2,8,3072]{5,4,3,2,1,0:T(8,128...) custom-call(bf16[384,1024]{1,0:T(8,128)(2,1)} %bitcast.183, ...), custom_call_target="tpu_custom_call" | custom-call | flops 20000000000 | bytes 100000000 | tf_op jit(solution)/shard_map/forward_layers/pallas_call | solution.py:394
  168.5 41.9 %backward_layer.2 = (bf16[384,1024]{1,0:T(8,128)(2,1)}, bf16[384,4096]{1,0:T(8,128)(2,1)}, bf16[384,3072]{1,0:T(8,128)(2,1)}, f32[1,1024]{1,0:T(1,128)}, f32[1,1...) custom-call(bf16[384,1024]{1,0:T(8,128)(2,1)} %bitcast.178, ...), custom_call_target="tpu_custom_call" | custom-call | flops 12999999488 | bytes 45000000 | tf_op jit(solution)/shard_map/backward_layer/pallas_call | solution.py:704
  210.4 1.8 constant_dynamic-slice_fusion.5
  212.4 41.6 %backward_layer.3 = (bf16[384,1024]{1,0:T(8,128)(2,1)}, bf16[384,4096]{1,0:T(8,128)(2,1)}, bf16[384,3072]{1,0:T(8,128)(2,1)}, f32[1,1024]{1,0:T(1,128)}, f32[1,1...) custom-call(bf16[384,1024]{1,0:T(8,128)(2,1)} %get-tuple-element.76., ...), custom_call_target="tpu_custom_call" | custom-call | flops 12999999488 | bytes 45000000 | tf_op jit(solution)/shard_map/backward_layer/pallas_call | solution.py:704
  254.0 2.4 constant_dynamic-slice_fusion.4
  256.7 2.9 constant_dynamic-slice_fusion.6
  259.8 2.4 constant_dynamic-slice_fusion.1
  270.6 1.7 concatenate.77
  273.8 2.6 copy.55
  276.4 2.6 copy.54
  279.0 8.6 %copy.53 = bf16[4096,768]{1,0:T(8,128)(2,1)} copy(bf16[4096,768]{0,1:T(8,128)(2,1)} %bitcast.154) | data formatting | bytes 12582912 | tf_op jit(solution)/shard_map/sd,se->de/dot_general | solution.py:721
  287.7 2.7 copy.52
  296.5 1.7 concatenate.81
  299.7 2.6 copy.59
  302.3 2.6 copy.57
  304.9 8.6 %copy.58 = bf16[4096,768]{1,0:T(8,128)(2,1)} copy(bf16[4096,768]{0,1:T(8,128)(2,1)} %bitcast.153) | data formatting | bytes 12582912 | tf_op jit(solution)/shard_map/sd,se->de/dot_general | solution.py:721
  313.5 2.6 copy.60
  317.5 1.4 broadcast_select_fusion.9
  319.0 8.9 %fusion.15.refs_1_ = f32[4,4,4,64,512]{4,3,2,1,0:T(8,128)} fusion(bf16[4,4,4,64,768]{4,3,2,1,0:T(8,128)(2,1)} %bitcast.155, bf16[384,512]{1,0:T(8,128)(2,1)S(1)} %get-tuple-element.129, bf16[384,512]{1,0:T(8,128)(2,1)S(1)} %get-tuple-element.128), kind=kOutput, calls=%fused_computation.29 | convolution fusion | flops 3222798336 | bytes 15466496 | tf_op jit(solution)/shard_map/sd,se->de/dot_general | solution.py:721
  327.8 2.3 fusion.14.refs_3_
  330.4 5.6 fusion.13.refs_1_
  336.1 2.3 fusion.12.refs_3_
  338.4 1.8 broadcast_select_fusion.7
  340.2 4.7 fusion.6.refs_2_
  344.9 1.8 broadcast_select_fusion.5
  346.7 4.6 fusion.9.refs_2_
  351.4 2.3 broadcast_select_fusion.3
  353.7 5.6 fusion.refs_0_
  359.3 101.3 %reduce_gradients.2 = (f32[2,8,2048]{2,1,0:T(8,128)}, f32[2,32,512]{2,1,0:T(8,128)}, f32[2,8,1536]{2,1,0:T(8,128)}, f32[2,8,512]{2,1,0:T(8,128)}, f32[8,128]{1,0:T(8,128)}) custom-call(f32[4,4,4,16,2048]{4,3,2,1,0:T(8,128)} %fusion.refs_0_, f32[4,4,4,64,512]{4,3,2,1,0:T(8,128)} %fusion.15.refs_1_, f32[4,4,4,16,1536]{4,3,2,1,0:T(8,128)} %fusion.6.refs_2_, ...), custom_call_target="tpu_custom_call" | custom-call | tf_op jit(solution)/shard_map/reduce_gradients/pallas_call | solution.py:558
  461.4 2.3 broadcast_select_fusion.1
  463.7 5.8 fusion.3.refs_0_
  469.6 104.9 %reduce_gradients.3 = (f32[2,8,2048]{2,1,0:T(8,128)}, f32[2,32,512]{2,1,0:T(8,128)}, f32[2,8,1536]{2,1,0:T(8,128)}, f32[2,8,512]{2,1,0:T(8,128)}, f32[8,128]{1,0:T(8,128)}) custom-call(f32[4,4,4,16,2048]{4,3,2,1,0:T(8,128)} %fusion.3.refs_0_, f32[4,4,4,64,512]{4,3,2,1,0:T(8,128)} %fusion.13.refs_1_, f32[4,4,4,16,1536]{4,3,2,1,0:T(8,128)} %fusion.9.refs_2_, ...), custom_call_target="tpu_custom_call" | custom-call | tf_op jit(solution)/shard_map/reduce_gradients/pallas_call | solution.py:558
  (197 shorter events, 36.0 us)
Async XLA Ops:
  1.1 3.6 copy-start.32
  1.1 3.5 copy-start.33
  1.1 3.5 copy-start.34
  212.2 104.9 %collective-permute-start.1 = (bf16[384,512]{1,0:T(8,128)(2,1)}, bf16[384,512]{1,0:T(8,128)(2,1)}, u32[]{:S(2)}, u32[]{:S(2)}) collective-permute-start(bf16[384,512]{1,0:T(8,128)(2,1)} %constant_dynamic-slice_fusion.5), channel_id=1, source_target_pairs={{0,1},{1,0},{2,3},{3,2},{4,5},{5,4},{6,7},{7,6},{8,9},{9,8},{10,11... | collective-permute-start | bytes 1179656 | tf_op jit(solution)/shard_map/ppermute | solution.py:769
  256.4 82.0 %collective-permute-start.2 = (bf16[384,1536]{1,0:T(8,128)(2,1)}, bf16[384,1536]{1,0:T(8,128)(2,1)}, u32[]{:S(2)}, u32[]{:S(2)}) collective-permute-start(bf16[384,1536]{1,0:T(8,128)(2,1)} %constant_dynamic-slice_fusion.4), channel_id=1, source_target_pairs={{0,1},{1,0},{2,3},{3,2},{4,5},{5,4},{6,7},{7,6},{8,9},{9,8},{10,11... | collective-permute-start | bytes 3538952 | tf_op jit(solution)/shard_map/ppermute | solution.py:769
  256.7 5.8 copy-start
  259.6 91.8 %collective-permute-start = (bf16[384,2048]{1,0:T(8,128)(2,1)}, bf16[384,2048]{1,0:T(8,128)(2,1)}, u32[]{:S(2)}, u32[]{:S(2)}) collective-permute-start(bf16[384,2048]{1,0:T(8,128)(2,1)} %constant_dynamic-slice_fusion.6), channel_id=1, source_target_pairs={{0,1},{1,0},{2,3},{3,2},{4,5},{5,4},{6,7},{7,6},{8,9},{9,8},{10,11... | collective-permute-start | bytes 4718600 | tf_op jit(solution)/shard_map/ppermute | solution.py:769
  262.2 82.7 %collective-permute-start.5 = (bf16[384,1536]{1,0:T(8,128)(2,1)}, bf16[384,1536]{1,0:T(8,128)(2,1)}, u32[]{:S(2)}, u32[]{:S(2)}) collective-permute-start(bf16[384,1536]{1,0:T(8,128)(2,1)} %constant_dynamic-slice_fusion.1), channel_id=1, source_target_pairs={{0,1},{1,0},{2,3},{3,2},{4,5},{5,4},{6,7},{7,6},{8,9},{9,8},{10,11... | collective-permute-start | bytes 3538952 | tf_op jit(solution)/shard_map/ppermute | solution.py:769
  262.5 3.7 copy-start.31
  262.5 4.4 copy-start.30
  262.5 5.2 copy-start.29
  262.5 6.0 %copy-start.28 = (f32[1,1024]{1,0:T(1,128)S(1)}, f32[1,1024]{1,0:T(1,128)}, u32[]{:S(2)}) copy-start(f32[1,1024]{1,0:T(1,128)} %get-tuple-element.93) | copy-start | bytes 12292
  262.5 7.3 %copy-start.27 = (f32[1,1024]{1,0:T(1,128)S(1)}, f32[1,1024]{1,0:T(1,128)}, u32[]{:S(2)}) copy-start(f32[1,1024]{1,0:T(1,128)} %get-tuple-element.95) | copy-start | bytes 12292
  263.8 197.6 %collective-permute-start.3 = (bf16[384,2048]{1,0:T(8,128)(2,1)}, bf16[384,2048]{1,0:T(8,128)(2,1)}, u32[]{:S(2)}, u32[]{:S(2)}) collective-permute-start(bf16[384,2048]{1,0:T(8,128)(2,1)} %constant_dynamic-slice_fusion.2), channel_id=1, source_target_pairs={{0,1},{1,0},{2,3},{3,2},{4,5},{5,4},{6,7},{7,6},{8,9},{9,8},{10,11... | collective-permute-start | bytes 4718600 | tf_op jit(solution)/shard_map/ppermute | solution.py:769
  287.7 3.6 copy-start.18
  287.7 4.4 copy-start.26
  287.7 5.1 copy-start.25
  287.7 5.9 %copy-start.24 = (f32[1,1024]{1,0:T(1,128)S(1)}, f32[1,1024]{1,0:T(1,128)}, u32[]{:S(2)}) copy-start(f32[1,1024]{1,0:T(1,128)} %get-tuple-element.106) | copy-start | bytes 12292
  287.7 6.7 %copy-start.23 = (f32[1,1024]{1,0:T(1,128)S(1)}, f32[1,1024]{1,0:T(1,128)}, u32[]{:S(2)}) copy-start(f32[1,1024]{1,0:T(1,128)} %get-tuple-element.107) | copy-start | bytes 12292
  287.7 8.0 %copy-start.22 = (f32[1,1024]{1,0:T(1,128)S(1)}, f32[1,1024]{1,0:T(1,128)}, u32[]{:S(2)}) copy-start(f32[1,1024]{1,0:T(1,128)} %get-tuple-element.109) | copy-start | bytes 12292
  317.1 13.0 %collective-permute-start.4 = (bf16[384,512]{1,0:T(8,128)(2,1)S(1)}, bf16[384,512]{1,0:T(8,128)(2,1)S(1)}, u32[]{:S(2)}, u32[]{:S(2)}) collective-permute-start(bf16[384,512]{1,0:T(8,128)(2,1)S(1)} %dynamic-slice_bitcast_fusion), channel_id=1, source_target_pairs={{0,1},{1,0},{2,3},{3,2},{4,5},{5,4},{6,7},{7,6},{8,9},{9,8},{10,11... | collective-permute-start | bytes 1179656 | tf_op jit(solution)/shard_map/ppermute | solution.py:769
  317.5 12.8 %slice-start = ((s8[6291456]{0:T(1024)(128)(4,1)}), s8[4194304]{0:T(1024)(128)(4,1)S(1)}, s32[]{:S(2)}) async-start(s8[6291456]{0:T(1024)(128)(4,1)} %bitcast.156), calls=%async_computation | async-start | bytes 8388608
  318.9 8.9 %copy-start.7 = (bf16[1024,768]{1,0:T(8,128)(2,1)S(1)}, bf16[1024,768]{1,0:T(8,128)(2,1)}, u32[]{:S(2)}) copy-start(bf16[1024,768]{1,0:T(8,128)(2,1)} %copy.55) | copy-start | bytes 4718596
  319.0 11.4 %slice-start.1 = ((s8[6291456]{0:T(1024)(128)(4,1)}), s8[2097152]{0:T(1024)(128)(4,1)S(1)}, s32[]{:S(2)}) async-start(s8[6291456]{0:T(1024)(128)(4,1)} %bitcast.156), calls=%async_computation.1 | async-start | bytes 4194304
  330.4 5.7 copy-start.9
  340.2 4.7 copy-start.2
  346.7 4.6 copy-start.1
  469.5 107.4 %copy-start.14 = (f32[2,32,512]{2,1,0:T(8,128)S(1)}, f32[2,32,512]{2,1,0:T(8,128)}, u32[]{:S(2)}) copy-start(f32[2,32,512]{2,1,0:T(8,128)} %get-tuple-element.118) | copy-start | bytes 393220
  469.5 108.3 %copy-start.13 = (f32[2,8,2048]{2,1,0:T(8,128)S(1)}, f32[2,8,2048]{2,1,0:T(8,128)}, u32[]{:S(2)}) copy-start(f32[2,8,2048]{2,1,0:T(8,128)} %get-tuple-element.116) | copy-start | bytes 393220
  469.5 109.3 %copy-start.17 = (f32[2,8,512]{2,1,0:T(8,128)S(1)}, f32[2,8,512]{2,1,0:T(8,128)}, u32[]{:S(2)}) copy-start(f32[2,8,512]{2,1,0:T(8,128)} %get-tuple-element.114) | copy-start | bytes 98308
  469.6 110.1 %copy-start.15 = (f32[2,8,1536]{2,1,0:T(8,128)S(1)}, f32[2,8,1536]{2,1,0:T(8,128)}, u32[]{:S(2)}) copy-start(f32[2,8,1536]{2,1,0:T(8,128)} %get-tuple-element.112) | copy-start | bytes 294916
  574.4 5.5 copy-start.16
  (16 other events, 44.7 us)

commit v4 on v3

v4 whole, which is shorter than its diff:
```python
import functools
import jax
import jax.numpy as jnp
import numpy as np
from jax import lax
from jax.experimental import pallas as pl
from jax.experimental.pallas import tpu as pltpu
from jax.sharding import PartitionSpec as P

EPSILON = 1e-5
MESH = pl.DeviceIdType.MESH
ANY = pl.BlockSpec(memory_space=pl.ANY)
IN_VMEM = pl.BlockSpec(memory_space=pltpu.VMEM)
ORDERS = ((2, 1, 0), (1, 0, 2), (0, 2, 1))
VMEM_LIMIT = 67 * 10**6


class Chip:
    def __init__(self, where):
        self.where = where
        self.near = [(v, v + 1 - 2 * lax.rem(v, 2), lax.rem(v + 2, 4), 3 - v) for v in where]
        base = (where[0] * 4 + where[1], where[2] * 2)
        steps = ((4, 0), (1, 0), (0, 2))
        self.beside = [[tuple(b + (near[mask] - near[0]) * s if s and mask else b for b, s in zip(base, step))
                        for mask in range(4)] for near, step in zip(self.near, steps)]

    def device(self, axis, mask, core):
        node, local = self.beside[axis][mask]
        return (node, local + core)


def place():
    node = lax.axis_index('node')
    local = lax.axis_index('local')
    return Chip((lax.div(node, 4), lax.rem(node, 4), lax.div(local, 2))), lax.rem(local, 2)


def colour_plan(colour):
    return ORDERS[colour // 2], ((1, 3) if colour % 2 == 0 else (3, 1))


def signal_partners(semaphore, chip, core):
    for axis in range(3):
        for mask in (1, 3):
            pl.semaphore_signal(semaphore, inc=1, device_id=chip.device(axis, mask, core), device_id_type=MESH)
    pl.semaphore_signal(semaphore, inc=1, device_id=chip.device(0, 0, 1 - core), device_id_type=MESH)


def entry_barrier(chip, core):
    barrier = pltpu.get_barrier_semaphore()
    signal_partners(barrier, chip, core)
    pl.semaphore_wait(barrier, 7)


SHARES = (8, 8, 8, 8, 24, 8, 32, 8)
SIZES = tuple(128 * share for share in SHARES)
OFFSETS = tuple(sum(SIZES[:k]) for k in range(len(SIZES)))
N_VEC = sum(SIZES)


SEQ, WIDTH, HIDDEN, TILE = 384, 1024, 4096, 512
N_TILES = HIDDEN // TILE
PAIR = 128
INV_SQRT2 = 0.7071067811865476
INV_SQRT2PI = 0.3989422804014327
SCALE = 0.125


def dot(a, b):
    return lax.dot_general(a, b, (((1,), (0,)), ((), ())), preferred_element_type=jnp.float32)


def dot_t(a, b):
    return lax.dot_general(a, b, (((1,), (1,)), ((), ())), preferred_element_type=jnp.float32)


def lanes(start, width=PAIR):
    return pl.ds(pl.multiple_of(start, PAIR), width)


def turn(x, cos, sin_a, sin_b):
    return x * cos + pltpu.roll(x, PAIR - 8, 1) * sin_a + pltpu.roll(x, 8, 1) * sin_b


def turn_back(d, cos, sin_a, sin_b):
    return d * cos + pltpu.roll(d * sin_a, 8, 1) + pltpu.roll(d * sin_b, PAIR - 8, 1)


def split_heads(x):
    first = lax.broadcasted_iota(jnp.int32, (PAIR, PAIR), 1) < PAIR // 2
    rows = []
    for j in range(SEQ // PAIR):
        block = x[j * PAIR:(j + 1) * PAIR]
        rows += [jnp.where(first, block, jnp.zeros_like(block)), jnp.where(first, jnp.zeros_like(block), block)]
    return jnp.concatenate(rows, axis=0)


def probabilities(q_block, keys, i):
    scores = dot_t(q_block, keys)
    causal = (lax.broadcasted_iota(jnp.int32, (PAIR, PAIR), 0) >= lax.broadcasted_iota(jnp.int32, (PAIR, PAIR), 1))
    probs = [None] * (2 * i + 2)
    for head in range(2):
        chunks = [scores[:, (2 * j + head) * PAIR:(2 * j + head + 1) * PAIR] * SCALE for j in range(i + 1)]
        chunks[i] = jnp.where(causal, chunks[i], -1e30)
        top = chunks[0]
        for chunk in chunks[1:]:
            top = jnp.maximum(top, chunk)
        top = jnp.max(top, axis=1, keepdims=True)
        chunks = [jnp.exp(chunk - top) for chunk in chunks]
        total = chunks[0]
        for chunk in chunks[1:]:
            total = total + chunk
        inverse = 1.0 / jnp.sum(total, axis=1, keepdims=True)
        for j in range(i + 1):
            probs[2 * j + head] = chunks[j] * inverse
    return probs


def normalised(h):
    center = h - jnp.mean(h, axis=1, keepdims=True)
    inverse = lax.rsqrt(jnp.mean(center * center, axis=1, keepdims=True) + EPSILON)
    return center * inverse, inverse


LN_ROWS = 64


GATHER_PARTS = ((0, 0, 2048, 0), (0, 2048, 2048, 1), (1, 0, 512, 2), (1, 512, 512, 3),
                (2, 0, 2048, 4), (2, 2048, 1024, 5), (3, 0, 1024, 5))


class Gather:
    def __init__(self, chip, core, parts, sems):
        self.chip, self.core, self.parts = chip, core, parts
        self.send_sem, self.recv_sem, self.pass_send, self.pass_recv = sems
        self.copies, self.passed, self.first, self.second = [], {}, {}, {}

    def copy(self, sems, n, slot, where, own, device):
        full, shard, cols, _ = self.parts[n]
        box = full.at[where[0], where[1], where[2], self.core, :, cols]
        copy = pltpu.make_async_remote_copy(
            src_ref=shard if own else box, dst_ref=box, send_sem=sems[0].at[n, slot], recv_sem=sems[1].at[n, slot],
            device_id=device, device_id_type=MESH)
        copy.start()
        self.copies.append(copy)
        return copy

    def reach(self, n, slot, where, own, axis, mask):
        return self.copy((self.send_sem, self.recv_sem), n, slot, where, own, self.chip.device(axis, mask, self.core))

    def pass_on(self, n, slot, where, own=False):
        copy = self.copy((self.pass_send, self.pass_recv), n, slot, where, own, self.chip.device(0, 0, 1 - self.core))
        self.passed.setdefault(n, []).append(copy)

    def span(self, n, stage, mask):
        order, masks = colour_plan(self.parts[n][3])
        where = list(self.chip.where)
        for axis in order[:stage]:
            where[axis] = pl.ds(0, 4)
        where[order[stage]] = self.chip.near[order[stage]][mask]
        return where, order[stage], masks

    def start(self, ns, stage):
        for turn in range(2):
            for n in ns:
                where, axis, masks = self.span(n, stage, 0)
                self.first[n, turn] = self.reach(n, 3 * stage + turn, where, stage == 0, axis, masks[turn])

    def pass_own(self, ns):
        for n in ns:
            self.pass_on(n, 9, self.chip.where, True)

    def middle(self, ns, stage):
        for n in ns:
            order, masks = colour_plan(self.parts[n][3])
            self.first[n, 0].wait_recv()
            where, axis, masks = self.span(n, stage, masks[0])
            self.second[n] = self.reach(n, 3 * stage + 2, where, False, axis, masks[1])
            self.pass_on(n, 3 * stage, where)

    def late(self, ns, stage):
        for n in ns:
            _, masks = colour_plan(self.parts[n][3])
            self.first[n, 1].wait_recv()
            self.pass_on(n, 3 * stage + 1, self.span(n, stage, masks[1])[0])

    def end(self, ns, stage):
        for n in ns:
            self.second[n].wait_recv()
            self.pass_on(n, 3 * stage + 2, self.span(n, stage, 2)[0])

    def arrived(self, ns):
        for n in ns:
            for copy in self.passed.pop(n):
                copy.wait_recv()


def unpack_vectors(small_v, layer, sel_shard, sel_lane, vec_ref):
    tiles = small_v[...].astype(jnp.float32).reshape((PAIR,) + small_v.shape[-2:])
    held = jnp.where(lax.broadcasted_iota(jnp.int32, tiles.shape, 1) == layer, tiles, 0.0)
    held = jnp.sum(held, axis=1).astype(jnp.bfloat16)
    for k in range(N_VEC // WIDTH):
        cols = slice(k * WIDTH, (k + 1) * WIDTH)
        number = lax.broadcasted_iota(jnp.int32, (PAIR, WIDTH), 0)
        pick = (number == sel_lane[:, cols]).astype(jnp.float32).astype(jnp.bfloat16)
        spread = jnp.where(number == sel_shard[:, cols], dot(held, pick), 0.0)
        vec_ref[layer:layer + 1, cols] = jnp.sum(spread, axis=0, keepdims=True)


def forward_kernel(n_layers, *refs):
    x_ref, cos_ref, sina_ref, sinb_ref, sel_shard, sel_lane = refs[:6]
    shards, refs = refs[6:11], refs[11:]
    fulls, refs = refs[:4 * n_layers + 1], refs[4 * n_layers + 1:]
    vec_ref, refs = refs[0], refs[1:]
    saved, refs = refs[:7 * n_layers], refs[7 * n_layers:]
    (wup_v, wdown_v, wqkv_v, wout_v, small_v, acc, pre_v, n1_v, n2_v, qkv_v, ctx_v, act_v, y_v,
     send_sem, recv_sem, pass_send, pass_recv, own_sem, load_sem, save_sem, share_send, share_recv) = refs
    chip, core = place()
    entry_barrier(chip, core)

    parts = []
    for layer in range(n_layers):
        for arr, col, width, colour in GATHER_PARTS:
            cols = pl.ds(col, width)
            parts.append((fulls[4 * layer + arr], shards[arr].at[layer, :, cols], cols, colour))
    parts.append((fulls[-1], shards[4], pl.ds(0, PAIR), 4))
    gather = Gather(chip, core, parts, (send_sem, recv_sem, pass_send, pass_recv))
    per = len(GATHER_PARTS)
    now = list(range(per)) + [len(parts) - 1]
    nxt = list(range(per, 2 * per))

    own = []
    for layer in range(n_layers):
        for arr in range(4):
            own.append((shards[arr].at[layer], fulls[4 * layer + arr]))
    own.append((shards[4], fulls[-1]))
    own = [pltpu.make_async_copy(src, dst.at[*chip.where, core], own_sem.at[k]) for k, (src, dst) in enumerate(own)]
    gather.start(now, 0)
    for copy in own:
        copy.start()
    gather.start(nxt, 0)
    gather.pass_own(now + nxt)
    for copy in own:
        copy.wait()
    for stage in range(3):
        gather.middle(now, stage)
        if stage:
            gather.start(nxt, stage)
        gather.late(now, stage)
        gather.end(now, stage)
        if stage < 2:
            gather.start(now, stage + 1)
            gather.middle(nxt, stage)
            gather.late(nxt, stage)
            gather.end(nxt, stage)

    saves, shares = [], []

    def save(src, dst):
        copy = pltpu.make_async_copy(src, dst, save_sem.at[len(saves)])
        copy.start()
        saves.append(copy)

    def share(src, dst):
        save(src, dst.at[core])
        copy = pltpu.make_async_remote_copy(
            src_ref=src, dst_ref=dst.at[core], send_sem=share_send.at[len(shares)], recv_sem=share_recv.at[len(shares)],
            device_id=chip.device(0, 0, 1 - core), device_id_type=MESH)
        copy.start()
        shares.append(copy)

    def load(layer, arr, k, width=None):
        full, held = fulls[4 * layer + arr].at[:, :, :, :, :, :], (wup_v, wdown_v, wqkv_v, wout_v)[arr]
        if width:
            cols = pl.ds(k * width, width)
            full, held = full.at[:, :, :, :, :, cols], held.at[:, :, :, :, :, cols]
        copy = pltpu.make_async_copy(full, held, load_sem.at[arr, k])
        copy.start()
        return copy

    def matrix(held, cols=slice(None)):
        return held[:, :, :, :, :, cols].reshape((-1, held.shape[-1] if cols == slice(None) else cols.stop - cols.start))

    def have(layer, arrs):
        gather.arrived([n for n in (now if layer == 0 else nxt) if n in gather.passed
                        and (parts[n][0] is fulls[-1] or any(parts[n][0] is fulls[4 * layer + arr] for arr in arrs))])

    for layer in range(n_layers):
        h_ref = y_v if layer else x_ref
        y_hbm, n1_hbm, n2_hbm, ctx_hbm, act_hbm, qkv_hbm, pre_hbm = saved[7 * layer:7 * layer + 7]
        have(layer, [2])
        loads = [load(layer, 2, k, TILE) for k in range(6)]
        if layer == 0:
            fetch = pltpu.make_async_copy(fulls[-1], small_v, load_sem.at[3, 1])
            fetch.start()
            fetch.wait()
            for k in range(n_layers):
                unpack_vectors(small_v, k, sel_shard, sel_lane, vec_ref)
        else:
            for copy in saves:
                copy.wait()
            for copy in shares:
                copy.wait_send()
            saves.clear()

        def vector(k, cols=slice(None)):
            at = OFFSETS[k]
            return vec_ref[layer:layer + 1, at:at + SIZES[k]] if cols == slice(None) else vec_ref[layer:layer + 1, at + cols.start:at + cols.stop]

        for r in range(SEQ // LN_ROWS):
            rows = slice(r * LN_ROWS, (r + 1) * LN_ROWS)
            scaled, _ = normalised(h_ref[rows, :].astype(jnp.float32))
            n1_v[rows, :] = (scaled * vector(0) + vector(1)).astype(jnp.bfloat16)
            n2_v[rows, :] = (scaled * vector(2) + vector(3)).astype(jnp.bfloat16)
        share(n1_v, n1_hbm)
        share(n2_v, n2_hbm)
        for k in range(6):
            cols = slice(k * TILE, (k + 1) * TILE)
            loads[k].wait()
            x = dot(n1_v[...], matrix(wqkv_v, cols)) + vector(4, cols)
            for c in range(TILE // PAIR):
                block = x[:, c * PAIR:(c + 1) * PAIR]
                if k < 4:
                    block = turn(block, cos_ref[...], sina_ref[...], sinb_ref[...])
                at = k * TILE + c * PAIR
                qkv_v[:, at:at + PAIR] = block.astype(jnp.bfloat16)
        save(qkv_v, qkv_hbm)
        have(layer, [0, 1, 3])
        out_load = load(layer, 3, 0)
        up_loads = [load(layer, 0, t, TILE) for t in range(N_TILES)]
        down_load = load(layer, 1, 0)

        @pl.loop(0, WIDTH // PAIR)
        def _(pair):
            keys = split_heads(qkv_v[:, lanes(WIDTH + pair * PAIR)])
            values = split_heads(qkv_v[:, lanes(2 * WIDTH + pair * PAIR)])
            for i in range(SEQ // PAIR):
                n = (i + 1) * 2 * PAIR
                rows = slice(i * PAIR, (i + 1) * PAIR)
                probs = probabilities(qkv_v[rows, lanes(pair * PAIR)], keys[:n], i)
                probs = jnp.concatenate([p.astype(jnp.bfloat16) for p in probs], axis=1)
                ctx_v[rows, lanes(pair * PAIR)] = dot(probs, values[:n]).astype(jnp.bfloat16)

        share(ctx_v, ctx_hbm)
        if layer == 0:
            gather.middle(nxt, 2)
        out_load.wait()
        for cols in (slice(0, TILE), slice(TILE, WIDTH)):
            acc[:, cols] = (h_ref[:, cols].astype(jnp.float32) + dot(ctx_v[...], matrix(wout_v, cols))
                            + (vector(5, cols) + vector(7, cols)))
        down_load.wait()
        for t in range(N_TILES):
            cols = slice(t * TILE, (t + 1) * TILE)
            up_loads[t].wait()
            pre = dot(n2_v[...], matrix(wup_v, cols)) + vector(6, cols)
            pre_v[t] = pre
            act_v[:, cols] = (0.5 * pre * (1.0 + lax.erf(pre * INV_SQRT2))).astype(jnp.bfloat16)
            acc[...] += dot(act_v[:, cols], wdown_v[t // 2, t % 2 * 2:t % 2 * 2 + 2].reshape((TILE, WIDTH)))
            if layer == 0 and t == N_TILES // 2:
                gather.late(nxt, 2)
        save(pre_v, pre_hbm)
        share(act_v, act_hbm)
        y_v[...] = acc[...].astype(jnp.bfloat16)
        save(y_v, y_hbm)
        if layer == 0:
            gather.end(nxt, 2)
    for copy in saves:
        copy.wait()
    per = len(shares) // n_layers
    for copy in shares:
        copy.wait_recv()
    for copy in shares[-per:]:
        copy.wait_send()
    for copy in gather.copies:
        copy.wait_send()


def forward(x, shards, small_tile, tables, sel_shard, sel_lane):
    n_layers = shards[0].shape[0]
    bf16, f32 = jnp.bfloat16, jnp.float32
    chips = (4, 4, 4, 2)
    full = [(chips + tensor.shape[1:], bf16) for tensor in shards]
    shapes = full * n_layers + [(chips + small_tile.shape, bf16), ((n_layers, N_VEC), f32)]
    kept = [((SEQ, WIDTH), bf16)] + [((2, SEQ, width), bf16) for width in (WIDTH, WIDTH, WIDTH, HIDDEN)]
    kept += [((SEQ, 3 * WIDTH), bf16), ((N_TILES, SEQ, TILE), f32)]
    shapes += kept * n_layers
    n_parts = len(GATHER_PARTS) * n_layers + 1
    dma = pltpu.SemaphoreType.DMA
    scratch = [pltpu.VMEM(*s) for s in full]
    scratch += [pltpu.VMEM(chips + small_tile.shape, bf16), pltpu.VMEM((SEQ, WIDTH), f32), pltpu.VMEM((N_TILES, SEQ, TILE), f32)]
    scratch += [pltpu.VMEM((SEQ, width), bf16) for width in (WIDTH, WIDTH, 3 * WIDTH, WIDTH, HIDDEN, WIDTH)]
    scratch += [dma((n_parts, 9)), dma((n_parts, 9)), dma((n_parts, 10)), dma((n_parts, 10)), dma((4 * n_layers + 1,)),
                dma((4, N_TILES)), dma((7,)), dma((4 * n_layers,)), dma((4 * n_layers,))]
    out_specs = [ANY] * len(shapes)
    out_specs[4 * n_layers + 1] = IN_VMEM
    outs = pl.pallas_call(
        functools.partial(forward_kernel, n_layers),
        out_shape=[jax.ShapeDtypeStruct(s, d) for s, d in shapes],
        in_specs=[IN_VMEM] * 11,
        out_specs=out_specs,
        scratch_shapes=scratch,
        compiler_params=pltpu.CompilerParams(collective_id=0, has_side_effects=True, vmem_limit_bytes=VMEM_LIMIT),
        cost_estimate=pl.CostEstimate(flops=20 * 10**9, bytes_accessed=10**8, transcendentals=10**7),
        name='forward_layers',
    )(x, *tables, sel_shard, sel_lane, *shards, small_tile)
    weights = [[t.reshape((-1, t.shape[-1])) for t in outs[4 * k:4 * k + 4]] for k in range(n_layers)]
    outs = outs[4 * n_layers + 1:]
    return weights, outs[0], [outs[1 + 7 * k:8 + 7 * k] for k in range(n_layers)]


WAVES = ((384, 384, 384, 384, 512, 512), (384, 384, 384, 384, 256, 256), (256,) * 6)
COLOURS = range(6)
US_PER_COLUMN, US_PER_STEP = 0.0165, 2.5
WIRE_PARTS = (0.25, 0.5, 0.75, 0.81, 0.88, 0.94, 0.95, 0.97, 0.98, 1)
UP, DOWN, QKV, OUT = range(4)


def pieces(wave, colour):
    if wave == 2:
        return [(QKV, 0, 256 * colour, 0, 256)]
    if colour < 4:
        return [(UP if wave else DOWN, 0 if wave else colour, 384 * colour if wave else 0, 0, 384)]
    if wave:
        return [(UP, 0, 256 * colour + 512, 0, 256)]
    group = 2 * colour - 8
    return [(DOWN, group, 384, 0, 128), (DOWN, group + 1, 384, 128, 128), (OUT, 0, 128 * group, 256, 256)]


def add_into(dst, src, n_axes):
    if n_axes < 2:
        dst[...] += src[...]
        return

    @pl.loop(0, 4)
    def _(k):
        dst[k] += src[k]


def at_axis(ref, axis, value, n_axes):
    every = [pl.ds(0, 4)] * n_axes
    every[axis] = value
    return ref.at[tuple(every)]


class Reduce:
    def __init__(self, chip, core, grads, came, fin, sems, spare, write):
        self.chip, self.core, self.grads, self.came, self.fin = chip, core, grads, came, fin
        self.send_sem, self.recv_sem, (self.spare, self.spare_sem) = sems[0], sems[1], spare
        self.write = write

    def plan(self, k):
        order, (one, two) = colour_plan(k)
        return order, one, two

    def box(self, k, stage):
        order, *_ = colour_plan(k)
        ref = self.came[k][0].at[0]
        axes = [axis for axis in range(3) if axis != order[0]]
        spot = axes.index(order[1])
        if stage == 1:
            return ref, spot, 2
        return at_axis(ref, spot, self.chip.where[order[1]], 2), 0, 1

    def copy(self, k, slot):
        order, one, two = self.plan(k)
        stage, turn = slot // 3, slot % 3
        if slot == 9:
            src, dst = self.final(k).at[1 - self.core], self.fin[k]
            device = self.chip.device(0, 0, 1 - self.core)
        else:
            axis = order[stage]
            device = self.chip.device(axis, two if turn == 2 else one, self.core)
            dst = self.came[k][2 * stage + turn // 2]
            dst = dst if turn == 2 else dst.at[turn]
            value = self.chip.near[axis][(one, 2, two)[turn]]
            if stage:
                ref, spot, n_axes = self.box(k, stage)
                src = at_axis(ref, spot, value, n_axes)
            else:
                src = self.came[k][0].at[1] if turn == 2 else at_axis(self.grads[k], axis, value, 3)
        return pltpu.make_async_remote_copy(src_ref=src, dst_ref=dst, send_sem=self.send_sem.at[k, slot],
                                            recv_sem=self.recv_sem.at[k, slot], device_id=device, device_id_type=MESH)

    def send(self, k, slot):
        self.copy(k, slot).start()

    def start(self):
        for slot in (1, 0):
            for k in COLOURS:
                self.send(k, slot)

    def local(self, k, slot):
        order, _, two = self.plan(k)
        width = self.grads[k].shape[-1]
        return pltpu.make_async_copy(at_axis(self.grads[k], order[0], self.chip.near[order[0]][two if slot else 0], 3),
                                     self.spare.at[k % 2, :, :, :, :, pl.ds(0, width)], self.spare_sem.at[k % 2])

    def first(self, slot):
        self.local(0, slot).start()
        for k in COLOURS:
            if k < 5:
                self.local(k + 1, slot).start()
            self.local(k, slot).wait()
            self.copy(k, slot).wait_recv()
            width = self.grads[k].shape[-1]
            add_into(self.came[k][0].at[slot], self.spare.at[k % 2, :, :, :, :, pl.ds(0, width)], 2)
            if slot:
                self.send(k, 2)

    def halve(self, stage):
        for k in COLOURS:
            order, one, two = self.plan(k)
            ref, spot, n_axes = self.box(k, stage)
            near = self.chip.near[order[stage]]
            self.copy(k, 3 * stage - 1).wait_recv()
            arrived = self.came[k][2 * stage - 1]
            for slot, value in ((1, near[2]), (0, near[one]), (2, near[two]), (2, near[0])):
                add_into(at_axis(ref, spot, value, n_axes), at_axis(arrived, spot, value, n_axes), n_axes - 1)
                if slot < 2:
                    self.send(k, 3 * stage + slot)

    def settle(self, stage, slot):
        for k in COLOURS:
            order, one, two = self.plan(k)
            ref, spot, n_axes = self.box(k, stage)
            value = self.chip.near[order[stage]][two if slot else 0]
            self.copy(k, 3 * stage + slot).wait_recv()
            add_into(at_axis(ref, spot, value, n_axes), self.came[k][2 * stage].at[slot], n_axes - 1)
            if slot:
                self.send(k, 3 * stage + 2)

    def final(self, k):
        order, *_ = colour_plan(k)
        return self.box(k, 2)[0].at[self.chip.where[order[2]]]

    def cross(self):
        for k in COLOURS:
            self.copy(k, 8).wait_recv()
            add_into(self.final(k), self.came[k][5], 0)
            self.send(k, 9)

    def finish(self):
        for k in COLOURS:
            self.write(k, self.core, self.final(k)[self.core])
        for k in COLOURS:
            self.copy(k, 9).wait_recv()
            self.write(k, 1 - self.core, self.fin[k][...])
        for k in COLOURS:
            for slot in range(10):
                self.copy(k, slot).wait_send()

    def steps(self, now):
        todo = [lambda: self.first(1), lambda: self.first(0), lambda: self.halve(1), lambda: self.settle(1, 1),
                lambda: self.settle(1, 0), lambda: self.halve(2), lambda: self.settle(2, 1), lambda: self.settle(2, 0),
                self.cross, self.finish]
        wire = sum(grad.shape[-1] for grad in self.grads) * US_PER_COLUMN
        return [(now + wire * part + US_PER_STEP * (k + 1), k, step) for k, (part, step) in enumerate(zip(WIRE_PARTS, todo))]


class VectorSum:
    def __init__(self, chip, core, total, came, send_sem, recv_sem):
        self.total, self.came, self.send_sem, self.recv_sem = total, came, send_sem, recv_sem
        self.devices = [chip.device(axis, mask, core) for axis in range(3) for mask in (1, 3)]
        self.devices.append(chip.device(0, 0, 1 - core))

    def copy(self, k):
        return pltpu.make_async_remote_copy(src_ref=self.total, dst_ref=self.came.at[k], send_sem=self.send_sem.at[k],
                                            recv_sem=self.recv_sem.at[k], device_id=self.devices[k], device_id_type=MESH)

    def step(self, k):
        if k:
            self.copy(k - 1).wait()
            self.total[...] += self.came[k - 1]
        if k < 7:
            self.copy(k).start()


def backward_kernel(*refs):
    dout_ref, cos_ref, sina_ref, sinb_ref, vec_ref, sel_shard, sel_lane = refs[:7]
    refs = refs[7:]
    (wup, wdown, wqkv, wout), refs = refs[:4], refs[4:]
    (h_hbm, n1_hbm, n2_hbm, ctx_hbm, act_hbm, qkv_hbm, pre_hbm), refs = refs[:7], refs[7:]
    dx_hbm, small_ref, sums, refs = refs[0], refs[1], refs[2:6], refs[6:]
    grads, (dout_cols, dpre_cols, dqkv_cols), refs = refs[:18], refs[18:21], refs[21:]
    came, fins, refs = refs[:108], refs[108:126], refs[126:]
    (spare, tile_v, big_v, rhs_v, wup_v, wdown_v, pre_v, dn1, dn2, dctx, dk_acc, dv_acc, qkv_v, dpre_v, dqkv_v, dh_v, h_v, total,
     came_vec, send_sem, recv_sem, spare_sem, tile_sem, big_sem, rhs_sem, mlp_sem, io_sem, share_sem, share_send, share_recv,
     vec_send, vec_recv) = refs
    chip, core = place()
    entry_barrier(chip, core)
    partner = chip.device(0, 0, 1 - core)
    clock, queue = 0.0, []

    def due(now):
        ready = sorted(item[:2] + (n,) for n, item in enumerate(queue) if item[0] <= now)
        found = [queue[n][2] for *_, n in ready]
        queue[:] = [item for item in queue if item[0] > now]
        return found

    def run(steps):
        for step in steps:
            step()

    def start(copies):
        for copy in copies:
            copy.start()
        return copies

    def wait(copies):
        for copy in copies:
            copy.wait()

    def hooks(count, each):
        return [(n, due(clock + each * (n + 1))) for n in range(count)]

    def at_hooks(n, planned):
        for when, steps in planned:
            if steps:
                @pl.when(n == when)
                def _():
                    run(steps)

    def share(k, src, width, dst):
        def half(which):
            return src.at[:, pl.ds(pl.multiple_of(which * width, PAIR), width)]
        mine = pltpu.make_async_copy(half(core), dst.at[core], share_sem.at[k])
        other = pltpu.make_async_remote_copy(
            src_ref=half(1 - core), dst_ref=dst.at[core], send_sem=share_send.at[k],
            recv_sem=share_recv.at[k], device_id=partner, device_id_type=MESH)
        return start([mine, other])

    def tokens_load(src, first, slot):
        return start([pltpu.make_async_copy(src.at[k, :, pl.ds(first, WIDTH)], big_v.at[slot, pl.ds(k * SEQ, SEQ)],
                                            big_sem.at[slot, k]) for k in range(2)])

    def whole_load(src, slot):
        return pltpu.make_async_copy(src, big_v.at[slot], big_sem.at[slot, 2])

    def rhs_load(src, first, width, slot):
        return start([pltpu.make_async_copy(src.at[k, :, pl.ds(first, width)],
                                            rhs_v.at[slot, pl.ds(k * SEQ, SEQ), pl.ds(0, width)], rhs_sem.at[slot, k])
                      for k in range(2)])

    def product(lhs_slot, rhs_slot, width, out_slot):
        value = lax.dot_general(big_v[lhs_slot, 0:2 * SEQ, :], rhs_v[rhs_slot, :, 0:width], (((0,), (0,)), ((), ())),
                                preferred_element_type=jnp.float32)
        tile_v[out_slot, :, :, :, :, :, 0:width] = value.reshape(tile_v.shape[1:-1] + (width,))

    def columns_of(wave, colour, first, width):
        return grads[6 * wave + colour].at[:, :, :, :, :, pl.ds(first, width)]

    def launch(wave):
        def write(k, half, block):
            for arr, group, col, first, width in pieces(wave, k):
                size = sums[arr].shape[-1] // 2
                at = pl.ds(pl.multiple_of(half * size + col, PAIR), width)
                sums[arr][group, :, at] = block[:, first:first + width].astype(jnp.bfloat16)
        current = Reduce(chip, core, grads[6 * wave:6 * wave + 6], [came[36 * wave + 6 * k:36 * wave + 6 * k + 6] for k in COLOURS],
                         fins[6 * wave:6 * wave + 6], (send_sem.at[wave], recv_sem.at[wave]), (spare, spare_sem), write)
        current.start()
        queue.extend(current.steps(clock))

    def tile_loads(t, slot):
        at = pl.multiple_of(t * TILE, TILE)
        return [pltpu.make_async_copy(wdown.at[pl.ds(at, TILE)], wdown_v.at[slot], mlp_sem.at[slot, 0]),
                pltpu.make_async_copy(pre_hbm.at[t], pre_v.at[slot], mlp_sem.at[slot, 1]),
                pltpu.make_async_copy(wup.at[:, pl.ds(at, TILE)], wup_v.at[slot], mlp_sem.at[slot, 2])]

    def vector_at(k, first=0, width=None):
        return pl.ds(pl.multiple_of(OFFSETS[k] + first, PAIR), width or SIZES[k])

    out_share = share(0, dout_ref, TILE, dout_cols)
    loads = tokens_load(act_hbm, 0, 0)
    input_loads = start([pltpu.make_async_copy(qkv_hbm, qkv_v, io_sem.at[0]), pltpu.make_async_copy(h_hbm, h_v, io_sem.at[1])])
    for t in range(2):
        start(tile_loads(t, t))
    d_sum = jnp.sum(dout_ref[...].astype(jnp.float32), axis=0, keepdims=True)
    total[:, vector_at(5)] = d_sum
    total[:, vector_at(7)] = d_sum
    wait(out_share)
    wait(rhs_load(dout_cols, 0, TILE, 0))
    outs = [[], []]
    for z in range(5):
        slot = z % 2
        wait(loads)
        if z < 4:
            loads = tokens_load(act_hbm if z < 3 else ctx_hbm, (z + 1) % 4 * WIDTH, 1 - slot)
        wait(outs[slot])
        product(slot, 0, TILE, slot)
        found = []
        if z < 4:
            for k in range(4):
                for colour, col, first, width in ((k, 0, 0, 384), (4 + k // 2, 384, k % 2 * PAIR, PAIR)):
                    for c in range(2):
                        found.append((tile_v.at[slot, :, :, 2 * c + k // 2, k % 2, :, pl.ds(col, width)],
                                      columns_of(0, colour, first, width).at[z, :, :, c]))
        else:
            for k in range(2):
                found.append((tile_v.at[slot, :, :, :, :, :, pl.ds(256 * k, 256)], columns_of(0, 4 + k, 256, 256)))
        outs[slot] = start([pltpu.make_async_copy(*one, tile_sem.at[slot, n]) for n, one in enumerate(found)])
    wait(outs[0] + outs[1])
    clock += 8
    launch(0)

    n2_loads = tokens_load(n2_hbm, 0, 0)
    out_load = whole_load(wout, 1)
    out_load.start()
    dn2[...] = jnp.zeros_like(dn2)

    def pre_copy(t, slot, to_partner):
        dst = dpre_cols.at[core, :, pl.ds(pl.multiple_of(lax.rem(t, 4) * TILE, TILE), TILE)]
        if to_partner:
            return pltpu.make_async_remote_copy(
                src_ref=dpre_v.at[slot], dst_ref=dst, send_sem=share_send.at[2 + t],
                recv_sem=share_recv.at[2 + t], device_id=partner, device_id_type=MESH)
        return pltpu.make_async_copy(dpre_v.at[slot], dst, share_sem.at[2 + slot])

    def pre_act(t, begin):
        for to_partner in (False, True):
            @pl.when(lax.div(t, 4) == (1 - core if to_partner else core))
            def _():
                copy = pre_copy(t, lax.rem(t, 2), to_partner)
                if begin:
                    copy.start()
                elif to_partner:
                    copy.wait_send()
                else:
                    copy.wait()

    planned = hooks(N_TILES, 2.1)

    @pl.loop(0, N_TILES)
    def _(t):
        slot = lax.rem(t, 2)
        wait(tile_loads(t, slot))
        d_act = dot_t(dout_ref[...], wdown_v[slot]).astype(jnp.bfloat16).astype(jnp.float32)
        pre = pre_v[slot]
        slope = 0.5 * (1.0 + lax.erf(pre * INV_SQRT2)) + pre * (INV_SQRT2PI * jnp.exp(-0.5 * pre * pre))
        d_pre = d_act * slope
        total[:, vector_at(6, t * TILE, TILE)] = jnp.sum(d_pre, axis=0, keepdims=True)

        @pl.when(t > 1)
        def _():
            pre_act(t - 2, False)

        dpre_v[slot] = d_pre.astype(jnp.bfloat16)
        pre_act(t, True)
        dn2[...] += dot_t(dpre_v[slot], wup_v[slot])

        @pl.when(t + 2 < N_TILES)
        def _():
            start(tile_loads(t + 2, slot))

        at_hooks(t, planned)

    clock += 2.1 * N_TILES
    for t in range(N_TILES - 2, N_TILES):
        pre_act(t, False)
    for t in range(4):
        pre_copy(4 * core + t, 0, True).wait_recv()

    def gradient_wave(wave, source, lhs_slot):
        widths = WAVES[wave]
        loads = rhs_load(source, 0, widths[0], 0)
        outs = [[], []]
        for k in COLOURS:
            slot, width = k % 2, widths[k]
            wait(loads)
            if k < 5:
                loads = rhs_load(source, sum(widths[:k + 1]), widths[k + 1], 1 - slot)
            wait(outs[slot])
            product(lhs_slot, slot, width, slot)
            outs[slot] = start([pltpu.make_async_copy(tile_v.at[slot, :, :, :, :, :, pl.ds(0, width)],
                                                      columns_of(wave, k, 0, width), tile_sem.at[slot, 0])])
        wait(outs[0] + outs[1])
        launch(wave)

    wait(n2_loads)
    clock += 5
    gradient_wave(1, dpre_cols, 0)

    out_load.wait()
    for k in range(2):
        rows = slice(k * TILE, (k + 1) * TILE)
        dctx[:, rows] = dot_t(dout_ref[...], big_v[1, rows, :]).astype(jnp.bfloat16)
    qkv_loads = [whole_load(wqkv.at[:, pl.ds(k * WIDTH, WIDTH)], k % 2) for k in range(3)]
    start(qkv_loads[:2])
    wait(input_loads)
    clock += 2
    run(due(clock))
    planned = hooks(N_TILES, 2.0)

    @pl.loop(0, WIDTH // PAIR)
    def _(pair):
        at = lanes(pair * PAIR)
        keys = split_heads(qkv_v[:, lanes(WIDTH + pair * PAIR)])
        values = split_heads(qkv_v[:, lanes(2 * WIDTH + pair * PAIR)])
        q_t = qkv_v[:, at].T
        dc_t = dctx[:, at].T
        bias_sums = [jnp.zeros((1, PAIR), jnp.float32)] * 3
        for i in range(SEQ // PAIR):
            n = (i + 1) * 2 * PAIR
            rows = slice(i * PAIR, (i + 1) * PAIR)
            probs = probabilities(qkv_v[rows, at], keys[:n], i)
            d_all = dot_t(dctx[rows, at], values[:n]).astype(jnp.bfloat16).astype(jnp.float32)
            d_probs = [d_all[:, j * PAIR:(j + 1) * PAIR] for j in range(2 * i + 2)]
            d_scores = [None] * (2 * i + 2)
            for head in range(2):
                mean = probs[head] * d_probs[head]
                for j in range(1, i + 1):
                    mean = mean + probs[2 * j + head] * d_probs[2 * j + head]
                mean = jnp.sum(mean, axis=1, keepdims=True)
                for j in range(head, 2 * i + 2, 2):
                    d_scores[j] = (probs[j] * (d_probs[j] - mean) * SCALE).astype(jnp.bfloat16)
            d_scores = jnp.concatenate(d_scores, axis=1)
            probs = jnp.concatenate([p.astype(jnp.bfloat16) for p in probs], axis=1)
            d_query = dot(d_scores, keys[:n]).astype(jnp.bfloat16).astype(jnp.float32)
            d_query = turn_back(d_query, cos_ref[rows, :], sina_ref[rows, :], sinb_ref[rows, :])
            bias_sums[0] = bias_sums[0] + jnp.sum(d_query, axis=0, keepdims=True)
            dqkv_v[rows, at] = d_query.astype(jnp.bfloat16)
            d_keys = dot(q_t[:, rows], d_scores)
            d_values = dot(dc_t[:, rows], probs)
            old = 2 * i * PAIR
            if i:
                dk_acc[:, :old] += d_keys[:, :old]
                dv_acc[:, :old] += d_values[:, :old]
            dk_acc[:, old:n] = d_keys[:, old:]
            dv_acc[:, old:n] = d_values[:, old:]
        first = lax.broadcasted_iota(jnp.int32, (PAIR, PAIR), 0) < PAIR // 2
        for j in range(SEQ // PAIR):
            rows = slice(j * PAIR, (j + 1) * PAIR)
            left, right = slice(2 * j * PAIR, (2 * j + 1) * PAIR), slice((2 * j + 1) * PAIR, (2 * j + 2) * PAIR)
            d_key = jnp.where(first, dk_acc[:, left], dk_acc[:, right]).T.astype(jnp.bfloat16).astype(jnp.float32)
            d_key = turn_back(d_key, cos_ref[rows, :], sina_ref[rows, :], sinb_ref[rows, :])
            bias_sums[1] = bias_sums[1] + jnp.sum(d_key, axis=0, keepdims=True)
            dqkv_v[rows, lanes(WIDTH + pair * PAIR)] = d_key.astype(jnp.bfloat16)
            d_value = jnp.where(first, dv_acc[:, left], dv_acc[:, right]).T.astype(jnp.bfloat16)
            bias_sums[2] = bias_sums[2] + jnp.sum(d_value.astype(jnp.float32), axis=0, keepdims=True)
            dqkv_v[rows, lanes(2 * WIDTH + pair * PAIR)] = d_value
        for k, bias_sum in enumerate(bias_sums):
            total[:, vector_at(4, k * WIDTH + pair * PAIR, PAIR)] = bias_sum
        at_hooks(pair, planned)

    clock += 2.0 * N_TILES
    qkv_share = share(1, dqkv_v, 3 * TILE, dqkv_cols)
    for k in range(3):
        qkv_loads[k].wait()
        part = dot_t(dqkv_v[:, k * WIDTH:(k + 1) * WIDTH], big_v[k % 2])
        if k == 0:
            dn1[...] = part
            qkv_loads[2].start()
        else:
            dn1[...] += part
    n1_loads = tokens_load(n1_hbm, 0, 1)
    for k in range(4):
        total[:, vector_at(k)] = jnp.zeros((1, WIDTH), jnp.float32)

    @pl.loop(0, SEQ // LN_ROWS)
    def _(r):
        rows = pl.ds(pl.multiple_of(r * LN_ROWS, LN_ROWS), LN_ROWS)
        scaled, inverse = normalised(h_v[rows, :].astype(jnp.float32))
        d1 = dn1[rows, :].astype(jnp.bfloat16).astype(jnp.float32)
        d2 = dn2[rows, :].astype(jnp.bfloat16).astype(jnp.float32)
        for k, value in enumerate((d1 * scaled, d1, d2 * scaled, d2)):
            total[:, vector_at(k)] += jnp.sum(value, axis=0, keepdims=True)
        g1, g2 = [vec_ref[:, OFFSETS[k]:OFFSETS[k] + WIDTH] for k in (0, 2)]
        d_scaled = d1 * g1 + d2 * g2
        d_h = inverse * (d_scaled - jnp.mean(d_scaled, axis=1, keepdims=True)
                         - scaled * jnp.mean(d_scaled * scaled, axis=1, keepdims=True))
        dh_v[rows, :] = (dout_ref[rows, :].astype(jnp.float32) + d_h).astype(jnp.bfloat16)

    clock += 6
    run(due(clock))
    wait(n1_loads + qkv_share)
    clock += 4
    gradient_wave(2, dqkv_cols, 1)
    run(due(clock))

    dx_copy = pltpu.make_async_copy(dh_v, dx_hbm, io_sem.at[2])
    dx_copy.start()
    rest = due(10 ** 9)
    vectors = VectorSum(chip, core, total, came_vec, vec_send, vec_recv)
    for k in range(8):
        vectors.step(k)
        run(rest[:2])
        rest = rest[2:]
    run(rest)
    node, local = chip.device(0, 0, core)
    me = node * 8 + local
    row = jnp.zeros((8, PAIR), jnp.float32)
    for k in range(N_VEC // WIDTH):
        cols = slice(k * WIDTH, (k + 1) * WIDTH)
        mine = (sel_shard[:, cols] == me).astype(jnp.float32)
        left = jnp.zeros((8, WIDTH), jnp.float32) + total[:, cols] * mine
        pick = (lax.broadcasted_iota(jnp.int32, (PAIR, WIDTH), 0) == sel_lane[:, cols]).astype(jnp.float32).astype(jnp.bfloat16)
        for _ in range(3):
            high = left.astype(jnp.bfloat16)
            row = row + dot_t(high, pick)
            left = left - high.astype(jnp.float32)
    small_ref[...] = row.astype(jnp.bfloat16)
    dx_copy.wait()


def backward(number, d_out, tables, vectors, sel_shard, sel_lane, weights, saved):
    bf16, f32 = jnp.bfloat16, jnp.float32
    dma = pltpu.SemaphoreType.DMA
    shapes = [((SEQ, WIDTH), bf16), ((8, PAIR), bf16)]
    shapes += [((groups, 8, width), bf16) for groups, width in ((1, HIDDEN), (4, WIDTH), (1, 3 * WIDTH), (1, WIDTH))]
    blocks = [(2, 8, width) for wave in WAVES for width in wave]
    shapes += [((4, 4, 4) + block, f32) for block in blocks]
    shapes += [((2, SEQ, width), bf16) for width in (TILE, 4 * TILE, 3 * TILE)]
    leads = ((2, 4, 4), (4, 4), (2, 4), (4,), (2,), ())
    scratch = [pltpu.VMEM(lead + block, f32) for block in blocks for lead in leads]
    scratch += [pltpu.VMEM(block[1:], f32) for block in blocks]
    wide, row = (SEQ, WIDTH), (1, N_VEC)
    scratch += [pltpu.VMEM(*s) for s in (
        ((2, 4, 4, 2, 8, TILE), f32), ((2, 4, 4, 4, 2, 8, TILE), f32), ((2, WIDTH, WIDTH), bf16), ((2, 2 * SEQ, TILE), bf16),
        ((2, WIDTH, TILE), bf16), ((2, TILE, WIDTH), bf16), ((2, SEQ, TILE), f32), (wide, f32), (wide, f32), (wide, bf16),
        ((PAIR, 2 * SEQ), f32), ((PAIR, 2 * SEQ), f32), ((SEQ, 3 * WIDTH), bf16), ((2, SEQ, TILE), bf16), ((SEQ, 3 * WIDTH), bf16),
        (wide, bf16), (wide, bf16), (row, f32), ((7,) + row, f32))]
    scratch += [dma(s) for s in ((3, 6, 10), (3, 6, 10), (2,), (2, 16), (2, 3), (2, 2), (2, 3), (3,), (4,),
                                 (10,), (10,), (7,), (7,))]
    out_specs = [ANY] + [IN_VMEM] * 5 + [ANY] * (len(shapes) - 6)
    outs = pl.pallas_call(
        backward_kernel,
        out_shape=[jax.ShapeDtypeStruct(s, d) for s, d in shapes],
        in_specs=[IN_VMEM] * 7 + [ANY] * 11,
        out_specs=out_specs,
        scratch_shapes=scratch,
        compiler_params=pltpu.CompilerParams(collective_id=number, has_side_effects=True, vmem_limit_bytes=VMEM_LIMIT),
        cost_estimate=pl.CostEstimate(flops=20 * 10**9, bytes_accessed=10**8, transcendentals=10**7),
        name='backward_layer',
    )(d_out, *tables, vectors, sel_shard, sel_lane, *weights, *saved)
    return outs[0], outs[1][0], [s.reshape((-1, s.shape[-1])) for s in outs[2:6]]


def rope_tables(seq_len, head_dim):
    rot_dim = head_dim // 4
    inv_freq = 1.0 / (10000.0 ** (jnp.arange(0, rot_dim, 2, dtype=jnp.float32) / rot_dim))
    angles = jnp.arange(seq_len, dtype=jnp.float32)[:, None] * inv_freq[None, :]
    cos, sin = jnp.cos(angles), jnp.sin(angles)
    zero = jnp.zeros_like(sin)
    rest = jnp.zeros((seq_len, head_dim - rot_dim), jnp.float32)
    tables = ([cos, cos, rest + 1.0], [-sin, zero, rest], [zero, sin, rest])
    return [jnp.tile(jnp.concatenate(table, axis=1), (1, 2)) for table in tables]


def heads_last(tensor):
    lead = tensor.shape[:-2]
    return tensor.reshape(lead + (16, 3, 64)).swapaxes(-3, -2).reshape(lead + (3072,))


def heads_first(tensor):
    lead = tensor.shape[:-1]
    return tensor.reshape(lead + (3, 16, 64)).swapaxes(-3, -2).reshape(lead + (16, 192))


def vector_places():
    shard, lane, start = [], [], 0
    for k, (share, size) in enumerate(zip(SHARES, SIZES)):
        place_of = np.arange(size)
        if k == 4:
            place_of = heads_last(place_of.reshape(16, 192))
        shard.append(place_of // share)
        lane.append(start + place_of % share)
        start += share
    return [jnp.asarray(np.concatenate(part)[None].astype(np.int32)) for part in (shard, lane)]


def pack_vectors(vectors):
    packed = jnp.concatenate(vectors, axis=-1)
    return jnp.pad(packed, ((0, 0), (0, 128 - packed.shape[-1])))


def solution(mesh):
    shard_axes = ('node', 'local')
    act_spec = P(shard_axes)
    param_spec = P(None, shard_axes)
    def device_step(x, y_cot, ln1_gain, ln1_bias, qkv_weight, qkv_bias, out_weight, out_bias,
                    ln2_gain, ln2_bias, up_weight, up_bias, down_weight, down_bias):
        num_layers = ln1_gain.shape[0]
        tables = rope_tables(x.shape[1], qkv_weight.shape[3] // 3)

        small = (ln1_gain, ln1_bias, ln2_gain, ln2_bias, qkv_bias, out_bias, up_bias, down_bias)
        small_tile = jnp.pad(pack_vectors(small), ((0, 8 - num_layers), (0, 0)))
        places = vector_places()
        weights, vectors, saved = forward(x[0], (up_weight, down_weight, heads_last(qkv_weight), out_weight), small_tile,
                                          tables, *places)
        hidden = [x[0]] + [layer[0] for layer in saved]
        saved = [[hidden[k]] + list(saved[k][1:]) for k in range(num_layers)]
        d_hidden, results = y_cot[0], []
        for k in reversed(range(num_layers)):
            d_hidden, *result = backward(k + 1, d_hidden, tables, vectors[k:k + 1], *places, weights[k], saved[k])
            results.insert(0, result)
        small_sums = jnp.stack([result[0] for result in results])
        up, down, qkv, out = [jnp.stack([result[1][arr] for result in results]) for arr in range(4)]
        small_grads, start = [], 0
        for width in SHARES:
            small_grads.append(small_sums[:, start:start + width])
            start += width
        g1, b1, g2, b2, qb, ob, ub, db = small_grads
        return (hidden[-1][None], d_hidden[None], g1, b1, heads_first(qkv), qb, out, ob, g2, b2, up, ub, down, db)

    return jax.shard_map(device_step, mesh=mesh,
                         in_specs=(act_spec, act_spec) + (param_spec,) * 12,
                         out_specs=(act_spec, act_spec) + (param_spec,) * 12,
                         check_vma=False)
```

time: 593 us -> 498 us (0.84)
  local copies, waits for them, and re-layouts: 65.3 us -> 12.9 us
  matrix products: 39.9 us -> 0 us
  other arithmetic: 24.3 us -> 5.48 us
  Pallas kernels: 451 us -> 469 us
    dot_general x8 -> x0, matrix products: 39.9 us -> none  [product(): jnp.einsum(einsum_form, first_op, second_op, preferred_element_type=jnp.f...]
    dot_general x8 -> x0, local copies, waits for them, and re-layouts: 32.9 us -> none  [product(): jnp.einsum(einsum_form, first_op, second_op, preferred_element_type=jnp.f...]
    pallas_call x4 -> x2, Pallas kernels: 290 us -> 307 us  [backward(): pl.pallas_call(backward_kernel, out_shape=[jax.ShapeDtypeStruct(s, d) for...]
    dynamic_slice x6 -> x0, local copies, waits for them, and re-layouts: 11.7 us -> none  [columns(): lax.dynamic_slice_in_dim(tensor, (1 - core) * width, width, 1)]
    select_n x6 -> x0, other arithmetic: 9.91 us -> none  [columns(): jnp.where(core == 0, mine, other)]
    pallas_call x14 -> x0, other arithmetic: 9.35 us -> none  [backward_layer(): pl.pallas_call(backward_kernel, out_shape=[jax.ShapeDtypeStruct(s, d) for...]
  transfers between devices with their start and end apart: 6 -> 0, of which waited for: 0 -> 0; matrix products, arithmetic and copies ran while one was open for 18% -> 0% of each run, Pallas kernels for 24% -> 0%
where the time goes in v4:
time: 498 us; the launch traced here: 488 us
  Pallas kernels  469 us (94%)
  local copies, waits for them, and re-layouts  12.9 us (3%)
  other arithmetic  5.48 us (1%)
    pallas_call x2, Pallas kernels, backward(): pl.pallas_call(backward_kernel, out_shape=[jax.ShapeDtypeStruct(s, d) for...  307 us
    pallas_call x1, Pallas kernels, forward(): pl.pallas_call(functools.partial(forward_kernel, n_layers), out_shape=[ja...  162 us

profile of v4, /device:TPU:1, one launch (start us, length us, event | category | flops | bytes accessed | tf_op | source)
XLA Modules:
  0.0 488.4 jit_solution(13755015814789184793)
XLA Ops:
  0.6 0.0 copy-start.2
  0.7 0.9 concatenate.15
  1.6 0.1 pad.28.clone
  1.6 0.1 pad.25.clone
  1.7 0.6 pad.29.refs_10_
  2.3 0.1 fusion
  2.5 0.1 maximum_maximum_fusion.2
  2.6 0.8 copy.35.refs_3_
  3.4 0.8 copy.34.refs_2_
  4.2 0.8 copy.33.refs_1_
  5.0 0.0 copy-done.2
  5.0 0.1 reshape.82
  5.2 0.8 reshape.83.refs_8_
  6.0 161.6 %forward_layers.1 = (bf16[4,4,4,2,8,4096]{5,4,3,2,1,0:T(8,128)(2,1)}, bf16[4,4,4,2,32,1024]{5,4,3,2,1,0:T(8,128)(2,1)}, bf16[4,4,4,2,8,3072]{5,4,3,2,1,0:T(8,128...) custom-call(bf16[384,1024]{1,0:T(8,128)(2,1)} %bitcast.35, ...), custom_call_target="tpu_custom_call" | custom-call | flops 20000000000 | bytes 100000000 | tf_op jit(solution)/shard_map/forward_layers/pallas_call | solution.py:396
  167.7 1.7 fusion.3
  169.4 153.8 %backward_layer.2 = (bf16[384,1024]{1,0:T(8,128)(2,1)}, bf16[8,128]{1,0:T(8,128)(2,1)}, bf16[1,8,4096]{2,1,0:T(8,128)(2,1)}, bf16[4,8,1024]{2,1,0:T(8,128)(2,1)}...) custom-call(bf16[384,1024]{1,0:T(8,128)(2,1)} %bitcast.34, ...), custom_call_target="tpu_custom_call" | custom-call | flops 20000000000 | bytes 100000000 | tf_op jit(solution)/shard_map/backward_layer/pallas_call | solution.py:924
  323.1 0.0 copy-start.3
  323.1 153.6 %backward_layer.3 = (bf16[384,1024]{1,0:T(8,128)(2,1)}, bf16[8,128]{1,0:T(8,128)(2,1)}, bf16[1,8,4096]{2,1,0:T(8,128)(2,1)}, bf16[4,8,1024]{2,1,0:T(8,128)(2,1)}...) custom-call(bf16[384,1024]{1,0:T(8,128)(2,1)} %get-tuple-element.62., ...), custom_call_target="tpu_custom_call" | custom-call | flops 20000000000 | bytes 100000000 | tf_op jit(solution)/shard_map/backward_layer/pallas_call | solution.py:924
  476.8 0.8 slice.38
  477.6 0.7 slice.39
  478.3 0.6 slice.42
  478.8 0.6 slice.46
  479.4 0.6 fusion.4
  480.0 1.3 pad_maximum_fusion.3
  481.4 0.8 pad_maximum_fusion.2
  482.2 1.5 pad_maximum_fusion
  483.7 1.5 pad_maximum_fusion.1
  485.3 0.2 reshape.92
  485.5 0.1 copy.44
  485.6 0.9 reshape.93
  486.4 0.9 copy.47
  487.3 0.9 copy.48
  (14 shorter events, 0.1 us)
Async XLA Ops:
  0.6 4.4 copy-start.2
  323.1 156.9 %copy-start.3 = (bf16[1,8,1024]{2,1,0:T(8,128)(2,1)S(1)}, bf16[1,8,1024]{2,1,0:T(8,128)(2,1)}, u32[]{:S(2)}) copy-start(bf16[1,8,1024]{2,1,0:T(8,128)(2,1)} %get-tuple-element.79) | copy-start | bytes 49156
  476.8 9.7 %copy-start = (bf16[384,1024]{1,0:T(8,128)(2,1)S(1)}, bf16[384,1024]{1,0:T(8,128)(2,1)}, u32[]{:S(2)}) copy-start(bf16[384,1024]{1,0:T(8,128)(2,1)} %get-tuple-element.49) | copy-start | bytes 2359300
  476.8 10.6 %copy-start.1 = (bf16[384,1024]{1,0:T(8,128)(2,1)S(1)}, bf16[384,1024]{1,0:T(8,128)(2,1)}, u32[]{:S(2)}) copy-start(bf16[384,1024]{1,0:T(8,128)(2,1)} %get-tuple-element.73) | copy-start | bytes 2359300
